TPU v7x, 256 devices: a whole 4x4x8 slice. The times are simulated.
256 devices in a mesh: gx: 32 (over z_hi, y, core), gy: 8 (over x, z_lo).
Axes of the slice: x: 4, y: 4, z: 8 (z_hi: 4, z_lo: 2; z = z_hi * 2 + z_lo), core: 2. Of those that a mesh axis runs over, the one named last changes fastest.
Arguments:
- state: float32 [12, 256, 16, 2048], P(None, 'gx', None, 'gy'), may hold values from -0.9 to 1, as said below
- tissue_mask: int32 [256, 16, 16], P('gx', None, 'gy'), may hold values 0 or 1
- layer_index: int32 [16], replicated, may hold values from 0 to 7
- fibre: float32 [2, 8], replicated, may hold values from -1.2 to 1.2
Outputs:
- new_state: float32 [12, 256, 16, 2048], P(None, 'gx', None, 'gy')
Inputs may be any that keep to these rules, and one draw needn't show every extreme that they name: `state`: component 0 lies within -0.9 to 0.3, components 1 to 10 within 0 to 1, component 11 within 0.05 to 1.
All inputs are finite; a program needn't handle non-finite values.
Results may differ from a plain program's by a relative error of at most 0.00002.
Values sent between devices are 32-bit elements.
No kernel may reach another device: no remote copies, remote signals or barrier semaphores. Data moves between devices by JAX's collectives and lax.ppermute only.
A program may use at most 64 MiB of HBM per device.

v0:
```python
import math

import jax
import jax.numpy as jnp
from jax import lax
from jax.sharding import PartitionSpec as P

STEPS = 8
MASK_BLOCK = 128


time_step = 0.02
thermal_volt = 8314.472 * 310.0 / 96485.3415
potassium_out = 5.4
sodium_out = 140.0
calcium_out = 2.0
potassium_in = 138.3
sodium_in = 7.67
transverse = 0.04
longitudinal = 0.12


def padded(x, sides, width):
    for axis, dim in sides:
        size, length = (lax.axis_size(axis), x.shape[dim])
        up = [(i, (i + 1) % size) for i in range(size - 1)]
        down = [(j, i) for i, j in up]
        last = lax.slice_in_dim(x, length - width, length, axis=dim)
        leading = lax.slice_in_dim(x, 0, width, axis=dim)
        before = lax.ppermute(last, axis, up)
        after = lax.ppermute(leading, axis, down)
        x = jnp.concatenate([before, x, after], axis=dim)
    return x


def settle(gate, steady, tau):
    return steady + (gate - steady) * jnp.exp(-time_step / tau)


def settle_rate(gate, steady, rate):
    return steady + (gate - steady) * jnp.exp(-time_step * rate)


def membrane(state):
    sig = jax.nn.sigmoid
    voltage = 100.0 * state[0]
    sodium_act = state[1]
    sodium_inact = state[2]
    sodium_slow = state[3]
    calcium_act = state[4]
    calcium_inact = state[5]
    transient_act = state[6]
    transient_inact = state[7]
    rapid_act = state[8]
    rapid_inact = state[9]
    slow_act = state[10]
    calcium = state[11]
    calcium_mm = jnp.maximum(calcium, 0.02) * 0.001
    rev_potassium = thermal_volt * math.log(potassium_out / potassium_in)
    rev_sodium = thermal_volt * math.log(sodium_out / sodium_in)
    rev_slow = thermal_volt * math.log(
        (potassium_out + 0.03 * sodium_out) / (potassium_in + 0.03 * sodium_in)
    )
    rev_calcium = 0.5 * thermal_volt * jnp.log(calcium_out / calcium_mm)
    sodium_current = 14.838 * sodium_act**3 * sodium_inact * sodium_slow * (voltage - rev_sodium)
    calcium_current = 0.08 * calcium_act * calcium_inact * (voltage - rev_calcium)
    transient_current = 0.294 * transient_act * transient_inact * (voltage - rev_potassium)
    rapid_current = 0.153 * rapid_act * rapid_inact * (voltage - rev_potassium)
    slow_current = 0.392 * slow_act**2 * (voltage - rev_slow)
    above = voltage - rev_potassium
    alpha_inward = 0.1 * sig(-0.06 * (above - 200.0))
    beta_inward = (3.0 * jnp.exp(0.0002 * (above + 100.0)) + jnp.exp(0.1 * (above - 10.0))) * sig(
        0.5 * above
    )
    inward_current = 5.405 * alpha_inward / (alpha_inward + beta_inward) * above
    plateau_current = 0.0146 * sig((voltage - 25.0) / 5.98) * above
    scaled = voltage / thermal_volt
    pump_current = (
        2.724
        * potassium_out
        / (potassium_out + 1.0)
        * sodium_in
        / (sodium_in + 40.0)
        / (1.0 + 0.1245 * jnp.exp(-0.1 * scaled) + 0.0353 * jnp.exp(-scaled))
    )
    exchange_current = (
        1000.0
        * (
            jnp.exp(0.35 * scaled) * sodium_in**3 * calcium_out
            - 2.5 * jnp.exp(-0.65 * scaled) * sodium_out**3 * calcium_mm
        )
        / ((87.5**3 + sodium_out**3) * (1.38 + calcium_out) * (1.0 + 0.1 * jnp.exp(-0.65 * scaled)))
    )
    pump_calcium = 0.1238 * calcium_mm / (calcium_mm + 0.0005)
    back_sodium = 0.00029 * (voltage - rev_sodium)
    back_calcium = 0.000592 * (voltage - rev_calcium)
    ionic_total = (
        sodium_current
        + calcium_current
        + transient_current
        + rapid_current
        + slow_current
        + inward_current
        + plateau_current
        + pump_current
        + exchange_current
        + pump_calcium
        + back_sodium
        + back_calcium
    )
    new_voltage = voltage - time_step * ionic_total
    new_calcium = calcium - time_step * 0.05 * (
        calcium_current + back_calcium + pump_calcium - 2.0 * exchange_current
    )
    upper = sig((voltage + 40.0) / 2.0)
    lower = sig(-(voltage + 40.0) / 2.0)
    tau_act = sig((voltage + 60.0) / 5.0) * (
        0.1 * sig(-(voltage + 35.0) / 5.0) + 0.1 * sig(-(voltage - 50.0) / 200.0)
    )
    new_act = settle(sodium_act, sig((voltage + 56.86) / 9.03) ** 2, tau_act)
    inact_steady = sig(-(voltage + 71.55) / 7.43) ** 2
    rate_inact = (
        lower * 0.057 * jnp.exp(-(voltage + 80.0) / 6.8)
        + upper * (0.77 / 0.13) * sig((voltage + 10.66) / 11.1)
        + lower * (2.7 * jnp.exp(0.079 * voltage) + 310000.0 * jnp.exp(0.3485 * voltage))
    )
    new_inact = settle_rate(sodium_inact, inact_steady, rate_inact)
    rate_slow = (
        lower
        * (-25428.0 * jnp.exp(0.2444 * voltage) - 6.948e-06 * jnp.exp(-0.04391 * voltage))
        * (voltage + 37.78)
        * sig(-0.311 * (voltage + 79.23))
        + lower * 0.02424 * jnp.exp(-0.01052 * voltage) * sig(0.1378 * (voltage + 40.14))
        + upper * 0.6 * jnp.exp(0.057 * voltage) * sig(0.1 * (voltage + 32.0))
    )
    new_slow = settle_rate(sodium_slow, inact_steady, rate_slow)
    tau_calact = (1.4 * sig((voltage + 35.0) / 13.0) + 0.25) * 1.4 * sig(
        -(voltage + 5.0) / 5.0
    ) + sig((voltage - 50.0) / 20.0)
    new_calact = settle(calcium_act, sig((voltage + 8.0) / 7.5), tau_calact)
    tau_calinact = (
        1102.5 * jnp.exp(-((voltage + 27.0) ** 2) / 225.0)
        + 200.0 * sig((voltage - 13.0) / 10.0)
        + 180.0 * sig(-(voltage + 30.0) / 10.0)
        + 20.0
    )
    new_calinact = settle(calcium_inact, sig(-(voltage + 20.0) / 7.0), tau_calinact)
    tau_tract = 9.5 * jnp.exp(-((voltage + 40.0) ** 2) / 1800.0) + 0.8
    new_tract = settle(transient_act, sig((voltage - 20.0) / 6.0), tau_tract)
    tau_trinact = (
        85.0 * jnp.exp(-((voltage + 45.0) ** 2) / 320.0) + 5.0 * sig(-(voltage - 20.0) / 5.0) + 3.0
    )
    new_trinact = settle(transient_inact, sig(-(voltage + 20.0) / 5.0), tau_trinact)
    tau_rapact = 450.0 * sig((voltage + 45.0) / 10.0) * 6.0 * sig(-(voltage + 30.0) / 11.5)
    new_rapact = settle(rapid_act, sig((voltage + 26.0) / 7.0), tau_rapact)
    tau_rapinact = 3.0 * sig((voltage + 60.0) / 20.0) * 1.12 * sig(-(voltage - 60.0) / 20.0)
    new_rapinact = settle(rapid_inact, sig(-(voltage + 88.0) / 24.0), tau_rapinact)
    tau_slowact = (
        1400.0 * jnp.sqrt(sig((voltage - 5.0) / 6.0)) * sig(-(voltage - 35.0) / 15.0) + 80.0
    )
    new_slowact = settle(slow_act, sig((voltage + 5.0) / 14.0), tau_slowact)
    return jnp.stack(
        [
            new_voltage / 100.0,
            new_act,
            new_inact,
            new_slow,
            new_calact,
            new_calinact,
            new_tract,
            new_trinact,
            new_rapact,
            new_rapinact,
            new_slowact,
            new_calcium,
        ]
    )


def advance(state, inside):
    return jnp.where(inside[None], membrane(state), state)


def layer_tensor(layer_index, fibre):
    angle_in = fibre[0]
    angle_out = fibre[1]
    fibre_x = jnp.cos(angle_in) * jnp.cos(angle_out)
    fibre_y = jnp.sin(angle_in) * jnp.cos(angle_out)
    fibre_z = jnp.sin(angle_out)
    spread = longitudinal - transverse
    tensor_table = jnp.stack(
        [
            transverse + spread * fibre_x * fibre_x,
            transverse + spread * fibre_y * fibre_y,
            transverse + spread * fibre_z * fibre_z,
            spread * fibre_x * fibre_y,
            spread * fibre_x * fibre_z,
            spread * fibre_y * fibre_z,
        ]
    )
    layer_ids = jnp.arange(fibre.shape[1], dtype=jnp.int32)
    chosen = layer_index[:, None] == layer_ids[None, :]
    return jnp.sum(jnp.where(chosen[None], tensor_table[:, None, :], jnp.float32(0.0)), axis=2)


def weights(tensor, offset_x, offset_y, offset_z):
    if offset_z == 0:
        if offset_x != 0 and offset_y != 0:
            return offset_x * offset_y * tensor[3] / 2.0
        if offset_x != 0:
            return tensor[0]
        return tensor[1]
    extent_z = tensor.shape[1]
    padded_tensor = jnp.pad(tensor, ((0, 0), (1, 1)), mode="edge")
    averaged = (tensor + padded_tensor[:, 1 + offset_z : 1 + offset_z + extent_z]) / 2.0
    if offset_x == 0 and offset_y == 0:
        return averaged[2]
    if offset_x != 0:
        return offset_x * offset_z * averaged[4] / 2.0
    return offset_y * offset_z * averaged[5] / 2.0


def stencil(volt_shell, mask_shell, tensor):
    volt_padded = jnp.pad(volt_shell, ((0, 0), (1, 1), (0, 0)))
    mask_padded = jnp.pad(mask_shell, ((0, 0), (1, 1), (0, 0)))
    extent_x = volt_shell.shape[0] - 2
    extent_z = volt_shell.shape[1]
    extent_y = volt_shell.shape[2] - 2
    centre = volt_padded[1 : 1 + extent_x, 1 : 1 + extent_z, 1 : 1 + extent_y]
    mask_centre = mask_padded[1 : 1 + extent_x, 1 : 1 + extent_z, 1 : 1 + extent_y]
    flux_sum = jnp.zeros_like(centre)
    for offset_x in (-1, 0, 1):
        for offset_y in (-1, 0, 1):
            for offset_z in (-1, 0, 1):
                length = offset_x * offset_x + offset_y * offset_y + offset_z * offset_z
                if length == 0 or length > 2:
                    continue
                weight = weights(tensor, offset_x, offset_y, offset_z)[None, :, None]
                neighbour = volt_padded[
                    1 + offset_x : 1 + offset_x + extent_x,
                    1 + offset_z : 1 + offset_z + extent_z,
                    1 + offset_y : 1 + offset_y + extent_y,
                ]
                mask_near = mask_padded[
                    1 + offset_x : 1 + offset_x + extent_x,
                    1 + offset_z : 1 + offset_z + extent_z,
                    1 + offset_y : 1 + offset_y + extent_y,
                ]
                flux_sum = flux_sum + weight * mask_near * (neighbour - centre)
    return mask_centre * flux_sum


def double_steps(state, wide_inside, wide_float, inner_inside, inner_float, tensor, widen):
    for repeat in range(STEPS // 2):
        extended = widen(state)
        first = advance(extended, wide_inside)
        middle = first[:, 1:-1, :, 1:-1]
        middle = middle.at[0].set(middle[0] + stencil(first[0], wide_float, tensor))
        second = advance(middle, inner_inside)
        final_volt = second[0][1:-1, :, 1:-1] + stencil(second[0], inner_float, tensor)
        state = second[:, 1:-1, :, 1:-1].at[0].set(final_volt)
    return state


def shards(state, tissue_mask, layer_index, fibre):
    tensor = layer_tensor(layer_index, fibre)
    cells_x, extent_z, block_count = tissue_mask.shape
    spread = jnp.broadcast_to(
        tissue_mask[:, :, :, None], (cells_x, extent_z, block_count, MASK_BLOCK)
    )
    voxel_mask = spread.reshape(cells_x, extent_z, block_count * MASK_BLOCK)
    shelled = padded(voxel_mask, (("gx", 0), ("gy", 2)), 2)
    wide_inside = shelled > 0
    wide_float = wide_inside.astype(jnp.float32)
    inner_inside = wide_inside[1:-1, :, 1:-1]
    inner_float = wide_float[1:-1, :, 1:-1]

    def widen_whole(current):
        return padded(current, (("gx", 1), ("gy", 3)), 2)

    state = double_steps(
        state, wide_inside, wide_float, inner_inside, inner_float, tensor, widen_whole
    )
    return state


def solution(mesh):
    placed = (P(None, "gx", None, "gy"), P("gx", None, "gy"), P(), P())
    return jax.shard_map(
        shards, mesh=mesh, in_specs=placed, out_specs=P(None, "gx", None, "gy"), check_vma=False
    )
```

profile of v0, /device:TPU:121, one launch (start us, length us, event | category | flops | bytes accessed | tf_op | source)
XLA Modules:
  0.0 264.7 jit_solution(3571473226060023119)
XLA Ops:
  0.9 5.4 %collective-permute-start = (s32[2,16,256]{2,1,0:T(8,128)S(1)}, s32[2,16,256]{2,1,0:T(8,128)S(1)}, u32[]{:S(2)}, u32[]{:S(2)}) collective-permute-start(s32[2,16,256]{2,1,0:T(8,128)S(1)} %slice.1836), channel_id=1, source_target_pairs={{0,8},{8,16},{16,24},{24,32},{32,40},{40,48},{48,56},{56,64},{64,7... | collective-permute-start | bytes 98312 | tf_op jit(solution)/shard_map/ppermute | solution.py:30
  6.6 1.9 collective-permute-start.1
  8.5 1.9 fusion.850
  10.5 1.9 collective-permute-start.5
  12.4 7.9 %collective-permute-start.4 = (f32[12,2,16,256]{3,2,1,0:T(8,128)S(1)}, f32[12,2,16,256]{3,2,1,0:T(8,128)}, u32[]{:S(2)}, u32[]{:S(2)}) collective-permute-start(f32[12,2,16,256]{3,2,1,0:T(8,128)S(1)} %get-tuple-element.130), channel_id=1, source_target_pairs={{0,8},{8,16},{16,24},{24,32},{32,40},{40,48},{48,56},{56,64},{64,7... | collective-permute-start | bytes 1179656 | tf_op jit(solution)/shard_map/ppermute | solution.py:30
  23.4 3.6 %collective-permute-start.2 = (s32[12,16,2]{2,1,0:T(8,128)S(1)}, s32[12,16,2]{2,1,0:T(8,128)S(1)}, u32[]{:S(2)}, u32[]{:S(2)}) collective-permute-start(s32[12,16,2]{2,1,0:T(8,128)S(1)} %get-tuple-element.131), channel_id=1, source_target_pairs={{0,1},{1,2},{2,3},{3,4},{4,5},{5,6},{6,7},{8,9},{9,10},{10,11},{11... | collective-permute-start | bytes 4616 | tf_op jit(solution)/shard_map/ppermute | solution.py:30
  27.0 1.9 collective-permute-start.3
  29.9 1.6 constant_dynamic-update-slice_fusion.4
  31.6 1.8 fusion.846
  33.4 2.8 %copy.50 = f32[12,12,16,2]{2,3,1,0:T(2,128)} copy(f32[12,12,16,2]{3,2,1,0:T(8,128)} %get-tuple-element.121) | data formatting | bytes 36864
  36.2 2.2 copy.51
  38.4 3.7 %collective-permute-start.7 = (f32[12,12,16,2]{2,3,1,0:T(2,128)S(1)}, f32[12,12,16,2]{2,3,1,0:T(2,128)}, u32[]{:S(2)}, u32[]{:S(2)}) collective-permute-start(f32[12,12,16,2]{2,3,1,0:T(2,128)S(1)} %copy.51), channel_id=1, source_target_pairs={{1,0},{2,1},{3,2},{4,3},{5,4},{6,5},{7,6},{9,8},{10,9},{11,10},{12... | collective-permute-start | bytes 55304 | tf_op jit(solution)/shard_map/ppermute | solution.py:31
  42.1 4.2 %collective-permute-start.6 = (f32[12,12,16,2]{2,3,1,0:T(2,128)}, f32[12,12,16,2]{2,3,1,0:T(2,128)}, u32[]{:S(2)}, u32[]{:S(2)}) collective-permute-start(f32[12,12,16,2]{2,3,1,0:T(2,128)} %copy.50), channel_id=1, source_target_pairs={{0,1},{1,2},{2,3},{3,4},{4,5},{5,6},{6,7},{8,9},{9,10},{10,11},{11... | collective-permute-start | bytes 55304 | tf_op jit(solution)/shard_map/ppermute | solution.py:30
  48.5 2.9 %copy.36 = f32[12,12,16,2]{3,2,1,0:T(8,128)} copy(f32[12,12,16,2]{2,3,1,0:T(2,128)} %collective-permute-done.6) | data formatting | bytes 36864 | tf_op jit(solution)/shard_map/ppermute | solution.py:30
  51.3 2.8 %copy.37 = f32[12,12,16,2]{3,2,1,0:T(8,128)} copy(f32[12,12,16,2]{2,3,1,0:T(2,128)} %collective-permute-done.7) | data formatting | bytes 36864 | tf_op jit(solution)/shard_map/ppermute | solution.py:31
  54.2 2.9 %pad_maximum_fusion = f32[12,12,16,260]{3,2,1,0:T(8,128)S(1)} fusion(f32[12,12,16,2]{3,2,1,0:T(8,128)} %copy.37, f32[12,12,16,256]{3,2,1,0:T(8,128)S(1)} %constant_dynamic-update-slice_fusion.3, f32[12,12,16,2]{3,2,1,0:T(8,128)} %copy.36), kind=kLoop, calls=%fused_computation | loop fusion | flops 1198080 | bytes 4792320 | tf_op jit(solution)/shard_map/concatenate | solution.py:32
  62.6 1.4 broadcast_select_fusion.3
  64.9 2.5 bitcast_dynamic-update-slice_fusion.3
  74.2 10.0 %collective-permute-start.8 = (f32[12,2,16,256]{3,2,1,0:T(8,128)S(1)}, f32[12,2,16,256]{3,2,1,0:T(8,128)S(1)}, u32[]{:S(2)}, u32[]{:S(2)}) collective-permute-start(f32[12,2,16,256]{3,2,1,0:T(8,128)S(1)} %get-tuple-element.127), channel_id=1, source_target_pairs={{0,8},{8,16},{16,24},{24,32},{32,40},{40,48},{48,56},{56,64},{64,7... | collective-permute-start | bytes 1179656 | tf_op jit(solution)/shard_map/ppermute | solution.py:30
  84.3 1.9 collective-permute-start.9
  86.2 6.9 %collective-permute-done.8 = f32[12,2,16,256]{3,2,1,0:T(8,128)S(1)} collective-permute-done((f32[12,2,16,256]{3,2,1,0:T(8,128)S(1)}, f32[12,2,16,256]{3,2,1,0:T(8,128)S(1)}, u32[]{:S(2)}, u32[]{:S(2)}) %collective-permute-start.8) | collective-permute-done | bytes 393248 | tf_op jit(solution)/shard_map/ppermute | solution.py:30
  93.1 8.0 %collective-permute-done.9 = f32[12,2,16,256]{3,2,1,0:T(8,128)S(1)} collective-permute-done((f32[12,2,16,256]{3,2,1,0:T(8,128)S(1)}, f32[12,2,16,256]{3,2,1,0:T(8,128)S(1)}, u32[]{:S(2)}, u32[]{:S(2)}) %collective-permute-start.9) | collective-permute-done | bytes 393248 | tf_op jit(solution)/shard_map/ppermute | solution.py:31
  102.1 1.4 fusion.845
  103.5 2.8 %copy.52 = f32[12,12,16,2]{2,3,1,0:T(2,128)} copy(f32[12,12,16,2]{3,2,1,0:T(8,128)} %get-tuple-element.119) | data formatting | bytes 36864
  106.4 2.2 collective-permute-start.10
  108.6 1.6 copy.53
  110.2 3.9 %collective-permute-start.11 = (f32[12,12,16,2]{2,3,1,0:T(2,128)}, f32[12,12,16,2]{2,3,1,0:T(2,128)}, u32[]{:S(2)}, u32[]{:S(2)}) collective-permute-start(f32[12,12,16,2]{2,3,1,0:T(2,128)} %copy.53), channel_id=1, source_target_pairs={{1,0},{2,1},{3,2},{4,3},{5,4},{6,5},{7,6},{9,8},{10,9},{11,10},{12... | collective-permute-start | bytes 55304 | tf_op jit(solution)/shard_map/ppermute | solution.py:31
  114.0 1.8 copy.40
  115.9 5.3 %collective-permute-done.11 = f32[12,12,16,2]{2,3,1,0:T(2,128)} collective-permute-done((f32[12,12,16,2]{2,3,1,0:T(2,128)}, f32[12,12,16,2]{2,3,1,0:T(2,128)}, u32[]{:S(2)}, u32[]{:S(2)}) %collective-permute-start.11) | collective-permute-done | bytes 18464 | tf_op jit(solution)/shard_map/ppermute | solution.py:31
  121.2 2.8 %copy.41 = f32[12,12,16,2]{3,2,1,0:T(8,128)} copy(f32[12,12,16,2]{2,3,1,0:T(2,128)} %collective-permute-done.11) | data formatting | bytes 36864 | tf_op jit(solution)/shard_map/ppermute | solution.py:31
  124.0 2.7 %pad_maximum_fusion.1 = f32[12,12,16,260]{3,2,1,0:T(8,128)S(1)} fusion(f32[12,12,16,2]{3,2,1,0:T(8,128)} %copy.41, f32[12,2,16,256]{3,2,1,0:T(8,128)} %copy-done.13, f32[12,8,16,256]{3,2,1,0:T(8,128)S(1)} %bitcast_dynamic-update-slice_fusion.7, f32[12,2,16,256]{3,2,1,0:T(8,128)} %copy-done.7, f32[12,12,16,2]{3,2,1,0:T(8,128)S(1)} %copy.40), kind=kLoop, calls=%fused_computation.1 | loop fusion | flops 2396160 | bytes 4792320 | tf_op jit(solution)/shard_map/concatenate | solution.py:32
  132.3 1.3 broadcast_select_fusion.2
  134.5 1.9 bitcast_dynamic-update-slice_fusion.2
  143.6 2.9 %collective-permute-start.12 = (f32[12,2,16,256]{3,2,1,0:T(8,128)S(1)}, f32[12,2,16,256]{3,2,1,0:T(8,128)S(1)}, u32[]{:S(2)}, u32[]{:S(2)}) collective-permute-start(f32[12,2,16,256]{3,2,1,0:T(8,128)S(1)} %get-tuple-element.125), channel_id=1, source_target_pairs={{0,8},{8,16},{16,24},{24,32},{32,40},{40,48},{48,56},{56,64},{64,7... | collective-permute-start | bytes 1179656 | tf_op jit(solution)/shard_map/ppermute | solution.py:30
  146.5 1.9 collective-permute-start.13
  148.4 6.3 %collective-permute-done.12 = f32[12,2,16,256]{3,2,1,0:T(8,128)S(1)} collective-permute-done((f32[12,2,16,256]{3,2,1,0:T(8,128)S(1)}, f32[12,2,16,256]{3,2,1,0:T(8,128)S(1)}, u32[]{:S(2)}, u32[]{:S(2)}) %collective-permute-start.12) | collective-permute-done | bytes 393248 | tf_op jit(solution)/shard_map/ppermute | solution.py:30
  154.6 7.0 %collective-permute-done.13 = f32[12,2,16,256]{3,2,1,0:T(8,128)S(1)} collective-permute-done((f32[12,2,16,256]{3,2,1,0:T(8,128)S(1)}, f32[12,2,16,256]{3,2,1,0:T(8,128)S(1)}, u32[]{:S(2)}, u32[]{:S(2)}) %collective-permute-start.13) | collective-permute-done | bytes 393248 | tf_op jit(solution)/shard_map/ppermute | solution.py:31
  162.6 1.4 fusion.844
  164.0 2.8 %copy.54 = f32[12,12,16,2]{2,3,1,0:T(2,128)} copy(f32[12,12,16,2]{3,2,1,0:T(8,128)} %get-tuple-element.117) | data formatting | bytes 36864
  166.9 6.1 %collective-permute-start.14 = (f32[12,12,16,2]{2,3,1,0:T(2,128)}, f32[12,12,16,2]{2,3,1,0:T(2,128)}, u32[]{:S(2)}, u32[]{:S(2)}) collective-permute-start(f32[12,12,16,2]{2,3,1,0:T(2,128)} %copy.54), channel_id=1, source_target_pairs={{0,1},{1,2},{2,3},{3,4},{4,5},{5,6},{6,7},{8,9},{9,10},{10,11},{11... | collective-permute-start | bytes 55304 | tf_op jit(solution)/shard_map/ppermute | solution.py:30
  173.0 1.6 copy.55
  174.6 2.3 collective-permute-start.15
  176.9 1.8 copy.44
  178.7 2.9 %collective-permute-done.15 = f32[12,12,16,2]{2,3,1,0:T(2,128)} collective-permute-done((f32[12,12,16,2]{2,3,1,0:T(2,128)}, f32[12,12,16,2]{2,3,1,0:T(2,128)}, u32[]{:S(2)}, u32[]{:S(2)}) %collective-permute-start.15) | collective-permute-done | bytes 18464 | tf_op jit(solution)/shard_map/ppermute | solution.py:31
  181.6 2.8 %copy.45 = f32[12,12,16,2]{3,2,1,0:T(8,128)} copy(f32[12,12,16,2]{2,3,1,0:T(2,128)} %collective-permute-done.15) | data formatting | bytes 36864 | tf_op jit(solution)/shard_map/ppermute | solution.py:31
  184.5 2.7 %pad_maximum_fusion.2 = f32[12,12,16,260]{3,2,1,0:T(8,128)S(1)} fusion(f32[12,12,16,2]{3,2,1,0:T(8,128)} %copy.45, f32[12,2,16,256]{3,2,1,0:T(8,128)} %copy-done.15, f32[12,8,16,256]{3,2,1,0:T(8,128)S(1)} %bitcast_dynamic-update-slice_fusion.6, f32[12,2,16,256]{3,2,1,0:T(8,128)} %copy-done.9, f32[12,12,16,2]{3,2,1,0:T(8,128)S(1)} %copy.44), kind=kLoop, calls=%fused_computation.2 | loop fusion | flops 2396160 | bytes 4792320 | tf_op jit(solution)/shard_map/concatenate | solution.py:32
  192.8 1.3 broadcast_select_fusion.1
  195.0 1.9 bitcast_dynamic-update-slice_fusion.1
  204.0 3.1 %collective-permute-start.16 = (f32[12,2,16,256]{3,2,1,0:T(8,128)S(1)}, f32[12,2,16,256]{3,2,1,0:T(8,128)S(1)}, u32[]{:S(2)}, u32[]{:S(2)}) collective-permute-start(f32[12,2,16,256]{3,2,1,0:T(8,128)S(1)} %get-tuple-element.123), channel_id=1, source_target_pairs={{0,8},{8,16},{16,24},{24,32},{32,40},{40,48},{48,56},{56,64},{64,7... | collective-permute-start | bytes 1179656 | tf_op jit(solution)/shard_map/ppermute | solution.py:30
  207.1 1.9 collective-permute-start.17
  209.0 5.5 %collective-permute-done.16 = f32[12,2,16,256]{3,2,1,0:T(8,128)S(1)} collective-permute-done((f32[12,2,16,256]{3,2,1,0:T(8,128)S(1)}, f32[12,2,16,256]{3,2,1,0:T(8,128)S(1)}, u32[]{:S(2)}, u32[]{:S(2)}) %collective-permute-start.16) | collective-permute-done | bytes 393248 | tf_op jit(solution)/shard_map/ppermute | solution.py:30
  214.5 7.5 %collective-permute-done.17 = f32[12,2,16,256]{3,2,1,0:T(8,128)S(1)} collective-permute-done((f32[12,2,16,256]{3,2,1,0:T(8,128)S(1)}, f32[12,2,16,256]{3,2,1,0:T(8,128)S(1)}, u32[]{:S(2)}, u32[]{:S(2)}) %collective-permute-start.17) | collective-permute-done | bytes 393248 | tf_op jit(solution)/shard_map/ppermute | solution.py:31
  223.0 1.4 fusion.843
  224.4 2.8 %copy.56 = f32[12,12,16,2]{2,3,1,0:T(2,128)} copy(f32[12,12,16,2]{3,2,1,0:T(8,128)} %get-tuple-element.115) | data formatting | bytes 36864
  227.3 4.3 %collective-permute-start.18 = (f32[12,12,16,2]{2,3,1,0:T(2,128)}, f32[12,12,16,2]{2,3,1,0:T(2,128)}, u32[]{:S(2)}, u32[]{:S(2)}) collective-permute-start(f32[12,12,16,2]{2,3,1,0:T(2,128)} %copy.56), channel_id=1, source_target_pairs={{0,1},{1,2},{2,3},{3,4},{4,5},{5,6},{6,7},{8,9},{9,10},{10,11},{11... | collective-permute-start | bytes 55304 | tf_op jit(solution)/shard_map/ppermute | solution.py:30
  231.6 1.6 copy.57
  233.2 2.1 collective-permute-start.19
  235.3 1.8 copy.48
  237.1 3.1 %collective-permute-done.19 = f32[12,12,16,2]{2,3,1,0:T(2,128)} collective-permute-done((f32[12,12,16,2]{2,3,1,0:T(2,128)}, f32[12,12,16,2]{2,3,1,0:T(2,128)}, u32[]{:S(2)}, u32[]{:S(2)}) %collective-permute-start.19) | collective-permute-done | bytes 18464 | tf_op jit(solution)/shard_map/ppermute | solution.py:31
  240.3 2.8 %copy.49 = f32[12,12,16,2]{3,2,1,0:T(8,128)} copy(f32[12,12,16,2]{2,3,1,0:T(2,128)} %collective-permute-done.19) | data formatting | bytes 36864 | tf_op jit(solution)/shard_map/ppermute | solution.py:31
  243.1 2.7 %pad_maximum_fusion.3 = f32[12,12,16,260]{3,2,1,0:T(8,128)S(1)} fusion(f32[12,12,16,2]{3,2,1,0:T(8,128)} %copy.49, f32[12,2,16,256]{3,2,1,0:T(8,128)} %copy-done.11, f32[12,8,16,256]{3,2,1,0:T(8,128)S(1)} %bitcast_dynamic-update-slice_fusion.5, f32[12,2,16,256]{3,2,1,0:T(8,128)} %copy-done.5, f32[12,12,16,2]{3,2,1,0:T(8,128)S(1)} %copy.48), kind=kLoop, calls=%fused_computation.3 | loop fusion | flops 2396160 | bytes 4792320 | tf_op jit(solution)/shard_map/concatenate | solution.py:32
  253.6 1.9 bitcast_dynamic-update-slice_fusion
  261.0 1.6 slice.2387
  262.6 1.8 bitcast_dynamic-update-slice_fusion.4
  (199 shorter events, 62.9 us)
Async XLA Ops:
  0.9 22.3 %collective-permute-start = (s32[2,16,256]{2,1,0:T(8,128)S(1)}, s32[2,16,256]{2,1,0:T(8,128)S(1)}, u32[]{:S(2)}, u32[]{:S(2)}) collective-permute-start(s32[2,16,256]{2,1,0:T(8,128)S(1)} %slice.1836), channel_id=1, source_target_pairs={{0,8},{8,16},{16,24},{24,32},{32,40},{40,48},{48,56},{56,64},{64,7... | collective-permute-start | bytes 98312 | tf_op jit(solution)/shard_map/ppermute | solution.py:30
  6.6 16.7 %collective-permute-start.1 = (s32[2,16,256]{2,1,0:T(8,128)S(1)}, s32[2,16,256]{2,1,0:T(8,128)S(1)}, u32[]{:S(2)}, u32[]{:S(2)}) collective-permute-start(s32[2,16,256]{2,1,0:T(8,128)S(1)} %slice.1838), channel_id=1, source_target_pairs={{8,0},{16,8},{24,16},{32,24},{40,32},{48,40},{56,48},{64,56},{72,6... | collective-permute-start | bytes 98312 | tf_op jit(solution)/shard_map/ppermute | solution.py:31
  10.5 21.1 %collective-permute-start.5 = (f32[12,2,16,256]{3,2,1,0:T(8,128)}, f32[12,2,16,256]{3,2,1,0:T(8,128)S(1)}, u32[]{:S(2)}, u32[]{:S(2)}) collective-permute-start(f32[12,2,16,256]{3,2,1,0:T(8,128)} %get-tuple-element.129), channel_id=1, source_target_pairs={{8,0},{16,8},{24,16},{32,24},{40,32},{48,40},{56,48},{64,56},{72,6... | collective-permute-start | bytes 1179656 | tf_op jit(solution)/shard_map/ppermute | solution.py:31
  12.4 16.5 %collective-permute-start.4 = (f32[12,2,16,256]{3,2,1,0:T(8,128)S(1)}, f32[12,2,16,256]{3,2,1,0:T(8,128)}, u32[]{:S(2)}, u32[]{:S(2)}) collective-permute-start(f32[12,2,16,256]{3,2,1,0:T(8,128)S(1)} %get-tuple-element.130), channel_id=1, source_target_pairs={{0,8},{8,16},{16,24},{24,32},{32,40},{40,48},{48,56},{56,64},{64,7... | collective-permute-start | bytes 1179656 | tf_op jit(solution)/shard_map/ppermute | solution.py:30
  23.4 23.0 %collective-permute-start.2 = (s32[12,16,2]{2,1,0:T(8,128)S(1)}, s32[12,16,2]{2,1,0:T(8,128)S(1)}, u32[]{:S(2)}, u32[]{:S(2)}) collective-permute-start(s32[12,16,2]{2,1,0:T(8,128)S(1)} %get-tuple-element.131), channel_id=1, source_target_pairs={{0,1},{1,2},{2,3},{3,4},{4,5},{5,6},{6,7},{8,9},{9,10},{10,11},{11... | collective-permute-start | bytes 4616 | tf_op jit(solution)/shard_map/ppermute | solution.py:30
  27.0 19.4 %collective-permute-start.3 = (s32[12,16,2]{2,1,0:T(8,128)S(1)}, s32[12,16,2]{2,1,0:T(8,128)}, u32[]{:S(2)}, u32[]{:S(2)}) collective-permute-start(s32[12,16,2]{2,1,0:T(8,128)S(1)} %get-tuple-element.132), channel_id=1, source_target_pairs={{1,0},{2,1},{3,2},{4,3},{5,4},{6,5},{7,6},{9,8},{10,9},{11,10},{12... | collective-permute-start | bytes 4616 | tf_op jit(solution)/shard_map/ppermute | solution.py:31
  38.4 12.9 %collective-permute-start.7 = (f32[12,12,16,2]{2,3,1,0:T(2,128)S(1)}, f32[12,12,16,2]{2,3,1,0:T(2,128)}, u32[]{:S(2)}, u32[]{:S(2)}) collective-permute-start(f32[12,12,16,2]{2,3,1,0:T(2,128)S(1)} %copy.51), channel_id=1, source_target_pairs={{1,0},{2,1},{3,2},{4,3},{5,4},{6,5},{7,6},{9,8},{10,9},{11,10},{12... | collective-permute-start | bytes 55304 | tf_op jit(solution)/shard_map/ppermute | solution.py:31
  42.1 6.3 %collective-permute-start.6 = (f32[12,12,16,2]{2,3,1,0:T(2,128)}, f32[12,12,16,2]{2,3,1,0:T(2,128)}, u32[]{:S(2)}, u32[]{:S(2)}) collective-permute-start(f32[12,12,16,2]{2,3,1,0:T(2,128)} %copy.50), channel_id=1, source_target_pairs={{0,1},{1,2},{2,3},{3,4},{4,5},{5,6},{6,7},{8,9},{9,10},{10,11},{11... | collective-permute-start | bytes 55304 | tf_op jit(solution)/shard_map/ppermute | solution.py:30
  60.6 2.0 copy-start
  60.6 2.0 copy-start.4
  74.2 18.9 %collective-permute-start.8 = (f32[12,2,16,256]{3,2,1,0:T(8,128)S(1)}, f32[12,2,16,256]{3,2,1,0:T(8,128)S(1)}, u32[]{:S(2)}, u32[]{:S(2)}) collective-permute-start(f32[12,2,16,256]{3,2,1,0:T(8,128)S(1)} %get-tuple-element.127), channel_id=1, source_target_pairs={{0,8},{8,16},{16,24},{24,32},{32,40},{40,48},{48,56},{56,64},{64,7... | collective-permute-start | bytes 1179656 | tf_op jit(solution)/shard_map/ppermute | solution.py:30
  84.3 16.8 %collective-permute-start.9 = (f32[12,2,16,256]{3,2,1,0:T(8,128)S(1)}, f32[12,2,16,256]{3,2,1,0:T(8,128)S(1)}, u32[]{:S(2)}, u32[]{:S(2)}) collective-permute-start(f32[12,2,16,256]{3,2,1,0:T(8,128)S(1)} %get-tuple-element.128), channel_id=1, source_target_pairs={{8,0},{16,8},{24,16},{32,24},{40,32},{48,40},{56,48},{64,56},{72,6... | collective-permute-start | bytes 1179656 | tf_op jit(solution)/shard_map/ppermute | solution.py:31
  93.1 8.0 %copy-start.7 = (f32[12,2,16,256]{3,2,1,0:T(8,128)}, f32[12,2,16,256]{3,2,1,0:T(8,128)S(1)}, u32[]{:S(2)}) copy-start(f32[12,2,16,256]{3,2,1,0:T(8,128)S(1)} %collective-permute-done.8) | copy-start | bytes 1179652
  101.1 0.8 copy-start.13
  106.4 7.7 %collective-permute-start.10 = (f32[12,12,16,2]{2,3,1,0:T(2,128)}, f32[12,12,16,2]{2,3,1,0:T(2,128)}, u32[]{:S(2)}, u32[]{:S(2)}) collective-permute-start(f32[12,12,16,2]{2,3,1,0:T(2,128)} %copy.52), channel_id=1, source_target_pairs={{0,1},{1,2},{2,3},{3,4},{4,5},{5,6},{6,7},{8,9},{9,10},{10,11},{11... | collective-permute-start | bytes 55304 | tf_op jit(solution)/shard_map/ppermute | solution.py:30
  110.2 11.0 %collective-permute-start.11 = (f32[12,12,16,2]{2,3,1,0:T(2,128)}, f32[12,12,16,2]{2,3,1,0:T(2,128)}, u32[]{:S(2)}, u32[]{:S(2)}) collective-permute-start(f32[12,12,16,2]{2,3,1,0:T(2,128)} %copy.53), channel_id=1, source_target_pairs={{1,0},{2,1},{3,2},{4,3},{5,4},{6,5},{7,6},{9,8},{10,9},{11,10},{12... | collective-permute-start | bytes 55304 | tf_op jit(solution)/shard_map/ppermute | solution.py:31
  130.3 2.0 copy-start.2
  130.3 2.0 copy-start.8
  130.3 2.0 copy-start.14
  143.6 11.1 %collective-permute-start.12 = (f32[12,2,16,256]{3,2,1,0:T(8,128)S(1)}, f32[12,2,16,256]{3,2,1,0:T(8,128)S(1)}, u32[]{:S(2)}, u32[]{:S(2)}) collective-permute-start(f32[12,2,16,256]{3,2,1,0:T(8,128)S(1)} %get-tuple-element.125), channel_id=1, source_target_pairs={{0,8},{8,16},{16,24},{24,32},{32,40},{40,48},{48,56},{56,64},{64,7... | collective-permute-start | bytes 1179656 | tf_op jit(solution)/shard_map/ppermute | solution.py:30
  146.5 15.2 %collective-permute-start.13 = (f32[12,2,16,256]{3,2,1,0:T(8,128)S(1)}, f32[12,2,16,256]{3,2,1,0:T(8,128)S(1)}, u32[]{:S(2)}, u32[]{:S(2)}) collective-permute-start(f32[12,2,16,256]{3,2,1,0:T(8,128)S(1)} %get-tuple-element.126), channel_id=1, source_target_pairs={{8,0},{16,8},{24,16},{32,24},{40,32},{48,40},{56,48},{64,56},{72,6... | collective-permute-start | bytes 1179656 | tf_op jit(solution)/shard_map/ppermute | solution.py:31
  154.6 7.0 %copy-start.9 = (f32[12,2,16,256]{3,2,1,0:T(8,128)}, f32[12,2,16,256]{3,2,1,0:T(8,128)S(1)}, u32[]{:S(2)}) copy-start(f32[12,2,16,256]{3,2,1,0:T(8,128)S(1)} %collective-permute-done.12) | copy-start | bytes 1179652
  161.6 0.8 copy-start.15
  166.9 10.0 %collective-permute-start.14 = (f32[12,12,16,2]{2,3,1,0:T(2,128)}, f32[12,12,16,2]{2,3,1,0:T(2,128)}, u32[]{:S(2)}, u32[]{:S(2)}) collective-permute-start(f32[12,12,16,2]{2,3,1,0:T(2,128)} %copy.54), channel_id=1, source_target_pairs={{0,1},{1,2},{2,3},{3,4},{4,5},{5,6},{6,7},{8,9},{9,10},{10,11},{11... | collective-permute-start | bytes 55304 | tf_op jit(solution)/shard_map/ppermute | solution.py:30
  174.6 7.1 %collective-permute-start.15 = (f32[12,12,16,2]{2,3,1,0:T(2,128)}, f32[12,12,16,2]{2,3,1,0:T(2,128)}, u32[]{:S(2)}, u32[]{:S(2)}) collective-permute-start(f32[12,12,16,2]{2,3,1,0:T(2,128)} %copy.55), channel_id=1, source_target_pairs={{1,0},{2,1},{3,2},{4,3},{5,4},{6,5},{7,6},{9,8},{10,9},{11,10},{12... | collective-permute-start | bytes 55304 | tf_op jit(solution)/shard_map/ppermute | solution.py:31
  190.7 2.0 copy-start.3
  190.7 2.0 copy-start.10
  190.8 2.0 copy-start.16
  204.0 10.5 %collective-permute-start.16 = (f32[12,2,16,256]{3,2,1,0:T(8,128)S(1)}, f32[12,2,16,256]{3,2,1,0:T(8,128)S(1)}, u32[]{:S(2)}, u32[]{:S(2)}) collective-permute-start(f32[12,2,16,256]{3,2,1,0:T(8,128)S(1)} %get-tuple-element.123), channel_id=1, source_target_pairs={{0,8},{8,16},{16,24},{24,32},{32,40},{40,48},{48,56},{56,64},{64,7... | collective-permute-start | bytes 1179656 | tf_op jit(solution)/shard_map/ppermute | solution.py:30
  207.1 14.9 %collective-permute-start.17 = (f32[12,2,16,256]{3,2,1,0:T(8,128)S(1)}, f32[12,2,16,256]{3,2,1,0:T(8,128)S(1)}, u32[]{:S(2)}, u32[]{:S(2)}) collective-permute-start(f32[12,2,16,256]{3,2,1,0:T(8,128)S(1)} %get-tuple-element.124), channel_id=1, source_target_pairs={{8,0},{16,8},{24,16},{32,24},{40,32},{48,40},{56,48},{64,56},{72,6... | collective-permute-start | bytes 1179656 | tf_op jit(solution)/shard_map/ppermute | solution.py:31
  214.5 7.5 %copy-start.5 = (f32[12,2,16,256]{3,2,1,0:T(8,128)}, f32[12,2,16,256]{3,2,1,0:T(8,128)S(1)}, u32[]{:S(2)}) copy-start(f32[12,2,16,256]{3,2,1,0:T(8,128)S(1)} %collective-permute-done.16) | copy-start | bytes 1179652
  222.0 0.8 copy-start.11
  227.3 8.1 %collective-permute-start.18 = (f32[12,12,16,2]{2,3,1,0:T(2,128)}, f32[12,12,16,2]{2,3,1,0:T(2,128)}, u32[]{:S(2)}, u32[]{:S(2)}) collective-permute-start(f32[12,12,16,2]{2,3,1,0:T(2,128)} %copy.56), channel_id=1, source_target_pairs={{0,1},{1,2},{2,3},{3,4},{4,5},{5,6},{6,7},{8,9},{9,10},{10,11},{11... | collective-permute-start | bytes 55304 | tf_op jit(solution)/shard_map/ppermute | solution.py:30
  233.2 7.1 %collective-permute-start.19 = (f32[12,12,16,2]{2,3,1,0:T(2,128)}, f32[12,12,16,2]{2,3,1,0:T(2,128)}, u32[]{:S(2)}, u32[]{:S(2)}) collective-permute-start(f32[12,12,16,2]{2,3,1,0:T(2,128)} %copy.57), channel_id=1, source_target_pairs={{1,0},{2,1},{3,2},{4,3},{5,4},{6,5},{7,6},{9,8},{10,9},{11,10},{12... | collective-permute-start | bytes 55304 | tf_op jit(solution)/shard_map/ppermute | solution.py:31
  249.4 2.0 copy-start.1
  249.4 2.0 copy-start.6
  249.4 2.0 copy-start.12
where the time goes:
time: 268 us; the launch traced here: 265 us
  other arithmetic  76.3 us (28%)
  starting transfers between devices  73.2 us (27%)
  local copies, waits for them, and re-layouts  60.3 us (22%)
  waiting for transfers between devices  53.4 us (20%)
    ppermute x10, starting transfers between devices, padded(): before = lax.ppermute(last, axis, up)  49.7 us
    unnamed x88, other arithmetic  37.8 us
    ppermute x10, waiting for transfers between devices, padded(): after = lax.ppermute(leading, axis, down)  33.9 us
    unnamed x47, local copies, waits for them, and re-layouts  24.1 us
    ppermute x10, starting transfers between devices, padded(): after = lax.ppermute(leading, axis, down)  23.5 us
    ppermute x10, waiting for transfers between devices, padded(): before = lax.ppermute(last, axis, up)  19.4 us
    concatenate x7, other arithmetic, padded(): x = jnp.concatenate([before, x, after], axis=dim)  11.8 us
    ppermute x4, local copies, waits for them, and re-layouts, padded(): after = lax.ppermute(leading, axis, down)  11.3 us
  transfers between devices with their start and end apart: 20, of which 10 were waited for; matrix products, arithmetic and copies ran while one was open for 11% of the time, Pallas kernels for 0%

commit v1 on v0

v1 whole, which is shorter than its diff:
```python
import functools
import math

import jax
import jax.numpy as jnp
from jax import lax
from jax.experimental import pallas as pl
from jax.experimental.pallas import tpu as pltpu
from jax.sharding import PartitionSpec as P

STEPS = 8
MASK_BLOCK = 128
COMPS = 12
EDGE = 8
GROUP = 2 * EDGE
LANES = 128

time_step = 0.02
thermal_volt = 8314.472 * 310.0 / 96485.3415
potassium_out = 5.4
sodium_out = 140.0
calcium_out = 2.0
potassium_in = 138.3
sodium_in = 7.67
transverse = 0.04
longitudinal = 0.12
LOG2E = math.log2(math.e)


def react(state):
    (x, act, inact, slow, calact, calinact, tract, trinact, rapact, rapinact, slowact, calcium) = state

    def power(rate, offset=0.0, scale=1.0):
        shift = offset * LOG2E + math.log2(scale)
        scaled = x * (100.0 * rate * LOG2E)
        return jnp.exp2(scaled + shift if shift else scaled)

    def bell(centre, width, scale):
        root = math.sqrt(LOG2E / width)
        away = x * (100.0 * root) + centre * root
        return jnp.exp2(math.log2(scale) - away * away)

    def inverse(value):
        return 1.0 / value

    def moved(gate, steady, exponent):
        return steady + (gate - steady) * jnp.exp2(exponent)

    e = math.exp
    decay = -time_step * LOG2E
    voltage = 100.0 * x
    rev_potassium = thermal_volt * math.log(potassium_out / potassium_in)
    rev_sodium = thermal_volt * math.log(sodium_out / sodium_in)
    rev_slow = thermal_volt * math.log((potassium_out + 0.03 * sodium_out) / (potassium_in + 0.03 * sodium_in))
    up20 = power(1 / 20)
    up10 = up20 * up20
    up5 = up10 * up10
    down20 = power(-1 / 20)
    down10 = down20 * down20
    down5 = down10 * down10
    up15 = power(1 / 15)
    down6 = power(-1 / 6)
    down14 = power(-1 / 14)
    down7 = down14 * down14
    fall = jnp.exp2(jnp.minimum(x * (-50.0 * LOG2E) - 20.0 * LOG2E, 120.0))
    upper = inverse(1.0 + fall)
    lower = fall * upper

    above = voltage - rev_potassium
    cam = jnp.maximum(calcium, 0.02)
    past_calcium = voltage - 0.5 * thermal_volt * math.log(calcium_out / 0.001) + (0.5 * thermal_volt) * jnp.log(cam)
    past_sodium = voltage - rev_sodium
    inward_x = 1.0 + power(0.06, -0.06 * (rev_potassium + 200.0))
    inward_y = 1.0 + fall * e(20.0 + 0.5 * rev_potassium)
    inward_b = power(0.0002, 0.0002 * (100.0 - rev_potassium), 30.0) + up10 * (10.0 * e(-0.1 * rev_potassium - 1.0))
    inward = (5.405 * inward_y) * inverse(inward_y + inward_b * inward_x)
    plateau = 0.0146 * inverse(1.0 + power(-1 / 5.98, 25.0 / 5.98))
    pump = (2.724 * potassium_out / (potassium_out + 1.0) * sodium_in / (sodium_in + 40.0)) * inverse(
        1.0 + power(-0.1 / thermal_volt, 0.0, 0.1245) + power(-1.0 / thermal_volt, 0.0, 0.0353))
    whole = 1000.0 / ((87.5**3 + sodium_out**3) * (1.38 + calcium_out))
    back = power(-0.65 / thermal_volt, 0.0, 0.1)
    exchange = (power(0.35 / thermal_volt, 0.0, whole * sodium_in**3 * calcium_out)
                - back * (cam * (10.0 * 2.5 * 0.001 * whole * sodium_out**3))) * inverse(1.0 + back)
    pump_calcium = (0.1238 * cam) * inverse(cam + 0.5)
    calcium_sum = (0.08 * calact * calinact + 0.000592) * past_calcium
    ionic = (
        (14.838 * act * (act * act) * inact * slow + 0.00029) * past_sodium
        + calcium_sum
        + (0.294 * tract * trinact + 0.153 * rapact * rapinact + inward + plateau) * above
        + (0.392 * slowact * slowact) * (voltage - rev_slow)
        + pump
        + exchange
        + pump_calcium
    )
    new_x = x - (time_step / 100.0) * ionic
    new_calcium = calcium - (time_step * 0.05) * (calcium_sum + pump_calcium - 2.0 * exchange)

    a = up5 * e(7.0)
    b = power(1 / 200, -0.25)
    root = inverse(1.0 + power(-1 / 9.03, -56.86 / 9.03))
    rate = (((1.0 + e(-5.0)) * 10.0 * decay + a * (10.0 * decay)) + down5 * (e(-12.0) * 10.0 * decay)) * (1.0 + b) * inverse(2.0 + a + b)
    new_act = moved(act, root * root, rate)

    root = inverse(1.0 + power(1 / 7.43, 71.55 / 7.43))
    steady = root * root
    rate = lower * (power(-1 / 6.8, -80.0 / 6.8, 0.057 * -decay) + power(0.079, 0.0, 2.7 * -decay) + power(0.3485, 0.0, 310000.0 * -decay)) + (
        upper * (0.77 / 0.13 * -decay)) * inverse(1.0 + power(-1 / 11.1, -10.66 / 11.1))
    new_inact = moved(inact, steady, -rate)
    rate = lower * (
        (power(0.2444, 0.0, 25428.0 * -decay) + power(-0.04391, 0.0, 6.948e-06 * -decay)) * (voltage + 37.78) * inverse(1.0 + power(0.311, 0.311 * 79.23))
        - power(-0.01052, 0.0, 0.02424 * -decay) * inverse(1.0 + power(-0.1378, -0.1378 * 40.14))
    ) - upper * power(0.057, 0.0, 0.6 * -decay) * inverse(1.0 + down10 * e(-3.2))
    new_slow = moved(slow, steady, rate)

    p = 1.0 + power(-1 / 13, -35.0 / 13)
    r = 1.0 + down20 * e(2.5)
    pq = p * (1.0 + up5 * e(1.0))
    rate = (decay * pq) * r * inverse((1.96 + 0.35 * p) * r + pq)
    new_calact = moved(calact, inverse(1.0 + power(-1 / 7.5, -8.0 / 7.5)), rate)

    a = down10 * e(1.3)
    b = up10 * e(3.0)
    den = (1.0 + e(4.3)) + a + b
    rate = (decay * den) * inverse((bell(27.0, 225.0, 1102.5) + 20.0) * den + (380.0 + 200.0 * b + 180.0 * a))
    new_calinact = moved(calinact, down7 * inverse(down7 + e(20.0 / 7)), rate)

    rate = decay * inverse(bell(40.0, 1800.0, 9.5) + 0.8)
    new_tract = moved(tract, inverse(1.0 + down6 * e(20.0 / 6)), rate)

    t = 1.0 + up5 * e(-4.0)
    rate = (decay * t) * inverse((bell(45.0, 320.0, 85.0) + 3.0) * t + 5.0)
    new_trinact = moved(trinact, inverse(1.0 + up5 * e(4.0)), rate)

    rate = (decay / 2700.0 + down10 * (e(-4.5) * decay / 2700.0)) * (1.0 + power(1 / 11.5, 30.0 / 11.5))
    new_rapact = moved(rapact, inverse(1.0 + down7 * e(-26.0 / 7)), rate)

    rate = (1.0 + e(-6.0)) * decay / 3.36 + (up20 + down20) * (e(-3.0) * decay / 3.36)
    new_rapinact = moved(rapinact, inverse(1.0 + power(1 / 24, 88.0 / 24)), rate)

    y = 1.0 + up15 * e(-35.0 / 15)
    rate = (decay * y) * inverse(1400.0 * lax.rsqrt(1.0 + down6 * e(5.0 / 6)) + 80.0 * y)
    new_slowact = moved(slowact, inverse(1.0 + down14 * e(-5.0 / 14)), rate)
    return (new_x, new_act, new_inact, new_slow, new_calact, new_calinact, new_tract, new_trinact, new_rapact, new_rapinact, new_slowact, new_calcium)


def layer_tensor(layer_index, fibre):
    angle_in = fibre[0]
    angle_out = fibre[1]
    fibre_x = jnp.cos(angle_in) * jnp.cos(angle_out)
    fibre_y = jnp.sin(angle_in) * jnp.cos(angle_out)
    fibre_z = jnp.sin(angle_out)
    spread = longitudinal - transverse
    tensor_table = jnp.stack(
        [
            transverse + spread * fibre_x * fibre_x,
            transverse + spread * fibre_y * fibre_y,
            transverse + spread * fibre_z * fibre_z,
            spread * fibre_x * fibre_y,
            spread * fibre_x * fibre_z,
            spread * fibre_y * fibre_z,
        ]
    )
    layer_ids = jnp.arange(fibre.shape[1], dtype=jnp.int32)
    chosen = layer_index[:, None] == layer_ids[None, :]
    return jnp.sum(jnp.where(chosen[None], tensor_table[:, None, :], jnp.float32(0.0)), axis=2)


def level_weights(tensor, lanes):
    between = (tensor[:, 1:] + tensor[:, :-1]) / 2.0
    upward = jnp.pad(between, ((0, 0), (0, 1)))
    downward = jnp.pad(between, ((0, 0), (1, 0)))
    rows = jnp.stack(
        [
            tensor[0],
            tensor[1],
            tensor[3] / 2.0,
            upward[2],
            upward[4] / 2.0,
            upward[5] / 2.0,
            downward[2],
            downward[4] / 2.0,
            downward[5] / 2.0,
        ]
    )
    return jnp.broadcast_to(rows[:, :, None], rows.shape + (lanes,))


def edge_kernel(state_ref, mask_ref, edge_ref):
    depth, width = state_ref.shape[2], state_ref.shape[3]
    cells = state_ref.shape[1]
    lane = lax.broadcasted_iota(jnp.int32, (depth, LANES), 1)

    def packed(first, last):
        total = jnp.zeros((depth, LANES), jnp.float32)
        for i in range(cells):
            joined = jnp.where(lane < EDGE, first(i), last(i))
            turned = pltpu.roll(joined, i * GROUP + EDGE, 1)
            total = jnp.where(lane // GROUP == i, turned, total)
        return total

    def one(c, carry):
        edge_ref[c] = packed(
            lambda i: state_ref[c, i, :, :LANES], lambda i: state_ref[c, i, :, width - LANES :]
        )
        return carry

    lax.fori_loop(0, COMPS, one, 0)
    spread = lambda i, b: jnp.broadcast_to(mask_ref[:, 2 * i + b : 2 * i + b + 1], (depth, LANES))
    edge_ref[COMPS] = packed(lambda i: spread(i, 0), lambda i: spread(i, 1))


def steps_kernel(
    left_hbm,
    state_hbm,
    right_hbm,
    strip_left_ref,
    strip_ref,
    strip_right_ref,
    weight_ref,
    out_hbm,
    main,
    inside,
    total,
    pot,
    dy_ref,
    sy_ref,
    strip,
    strip_inside,
    strip_total,
    strip_pot,
    sems,
):
    cells, depth, width = state_hbm.shape[1:]
    span = 3 * cells
    sides = (0, 1)
    long = 3 * LANES
    copies = [
        pltpu.make_async_copy(source, main.at[:, pl.ds(i * cells, cells)], sems.at[i])
        for i, source in enumerate((left_hbm, state_hbm, right_hbm))
    ]
    for copy in copies:
        copy.start()
    lane = lax.broadcasted_iota(jnp.int32, (depth, LANES), 1)
    first_lane = lane == 0
    last_lane = lane == LANES - 1

    for i, source in enumerate((strip_left_ref, strip_ref, strip_right_ref)):
        part = pl.ds(i * LANES, LANES)
        for side in sides:
            for c in range(COMPS):
                strip[c, side, :, part] = source[side * (COMPS + 1) + c]
            strip_inside[side, :, part] = source[side * (COMPS + 1) + COMPS]
            strip_pot[side, :, part] = source[side * (COMPS + 1) + COMPS]
        codes = source[2 * (COMPS + 1)]
        for x in range(cells):
            for b in range(2):
                value = jnp.broadcast_to(codes[:, 2 * x + b : 2 * x + b + 1], (depth, LANES))
                inside[i * cells + x, :, b * LANES : (b + 1) * LANES] = value
                pot[i * cells + x, :, b * LANES : (b + 1) * LANES] = value

    def shift_row(x, carry):
        block = pl.ds(pl.multiple_of(x // 8 * LANES, LANES), LANES)
        place = lax.rem(x, 8) * GROUP
        before = pltpu.roll(strip_pot[0, :, block], lax.rem(2 * LANES - place - (EDGE - 1), LANES), 1)
        after = pltpu.roll(strip_pot[1, :, block], lax.rem(2 * LANES - 1 - place - EDGE, LANES), 1)
        near, far = pot[x, :, :LANES], pot[x, :, LANES:]
        near_up, far_up = pltpu.roll(near, 1, 1), pltpu.roll(far, 1, 1)
        near_down, far_down = pltpu.roll(near, LANES - 1, 1), pltpu.roll(far, LANES - 1, 1)
        lower = jnp.where(first_lane, before, near_up)
        upper = jnp.where(last_lane, far_down, near_down)
        dy_ref[x, :, :LANES] = upper - lower
        sy_ref[x, :, :LANES] = upper + lower
        lower = jnp.where(first_lane, near_up, far_up)
        upper = jnp.where(last_lane, after, far_down)
        dy_ref[x, :, LANES:] = upper - lower
        sy_ref[x, :, LANES:] = upper + lower
        return carry

    def spread(p, dx, sx, dy, sy, cross, lanes):
        w = [weight_ref[i, :, :lanes] for i in range(9)]
        rising = w[3] * p - w[4] * dx - w[5] * dy
        falling = w[6] * p + w[7] * dx + w[8] * dy
        return (
            w[0] * sx
            + w[1] * sy
            + w[2] * cross
            + pltpu.roll(rising, 1, 0)
            + pltpu.roll(falling, depth - 1, 0)
        )

    def row_spread(x):
        before, after = pot[x - 1], pot[x + 1]
        return spread(
            pot[x], after - before, after + before, dy_ref[x], sy_ref[x], dy_ref[x + 1] - dy_ref[x - 1], width
        )

    def strip_spread(side):
        p = strip_pot[side]
        lower, upper = pltpu.roll(p, 1, 1), pltpu.roll(p, long - 1, 1)
        before, after = pltpu.roll(p, GROUP, 1), pltpu.roll(p, long - GROUP, 1)
        dy = upper - lower
        cross = pltpu.roll(dy, long - GROUP, 1) - pltpu.roll(dy, GROUP, 1)
        return spread(p, after - before, after + before, dy, upper + lower, cross, long)

    lax.fori_loop(0, span, shift_row, 0)

    def total_row(x, carry):
        total[x] = row_spread(x)
        return carry

    lax.fori_loop(1, span - 1, total_row, 0)
    for side in sides:
        strip_total[side] = strip_spread(side)
    for copy in copies:
        copy.wait()

    def react_tile(store, held, place, level, part):
        rows = pl.ds(level * 8, 8)
        old = [store[c, place, rows, part] for c in range(COMPS)]
        live = held[place, rows, part]
        new = react(old)
        new = [jnp.where(live > 0.5, a, b) for a, b in zip(new, old)]
        for c in range(COMPS):
            store[c, place, rows, part] = new[c]
        return live * new[0]

    def step(s, carry):
        for side in sides:
            for level in range(depth // 8):
                for i in range(3):
                    part = pl.ds(i * LANES, LANES)
                    value = react_tile(strip, strip_inside, side, level, part)
                    strip_pot[side, pl.ds(level * 8, 8), part] = value

        def react_row(x, carry):
            for level in range(depth // 8):
                for i in range(2):
                    part = pl.ds(i * LANES, LANES)
                    pot[x, pl.ds(level * 8, 8), part] = react_tile(main, inside, x, level, part)
            return carry

        lax.fori_loop(s, span - s, react_row, 0)
        lax.fori_loop(s, span - s, shift_row, 0)

        def diffuse_row(x, carry):
            u = main[0, x]
            main[0, x] = u + inside[x] * (row_spread(x) - u * total[x])
            return carry

        lax.fori_loop(s + 1, span - 1 - s, diffuse_row, 0)
        for side in sides:
            u = strip[0, side]
            strip[0, side] = u + strip_inside[side] * (strip_spread(side) - u * strip_total[side])
        return carry

    lax.fori_loop(0, STEPS, step, 0)
    copy = pltpu.make_async_copy(main.at[:, pl.ds(cells, cells)], out_hbm, sems.at[0])
    copy.start()
    copy.wait()


def shards(state, tissue_mask, layer_index, fibre):
    comps, cells, depth, width = state.shape
    across, along = lax.axis_size("gx"), lax.axis_size("gy")

    def passed(value, axis, size):
        up = [(i, i + 1) for i in range(size - 1)]
        return lax.ppermute(value, axis, up), lax.ppermute(value, axis, [(j, i) for i, j in up])

    vmem = pl.BlockSpec(memory_space=pltpu.VMEM)
    hbm = pl.BlockSpec(memory_space=pl.ANY)
    from_left, from_right = passed(state, "gx", across)

    blocks = tissue_mask.shape[2]
    codes = (tissue_mask > 0).astype(jnp.float32).transpose(1, 0, 2).reshape(depth, cells * blocks)
    codes = jnp.pad(codes, ((0, 0), (0, LANES - cells * blocks)))
    edge = pl.pallas_call(
        edge_kernel,
        out_shape=jax.ShapeDtypeStruct((comps + 1, depth, LANES), jnp.float32),
        in_specs=[vmem, vmem],
        out_specs=vmem,
        compiler_params=pltpu.CompilerParams(vmem_limit_bytes=32 << 20),
        name="edges",
    )(state, codes)
    edge_before, edge_after = passed(edge, "gy", along)
    outer = lax.broadcasted_iota(jnp.int32, edge.shape, 2) % GROUP < EDGE
    strips = jnp.concatenate(
        [jnp.where(outer, edge_before, edge), jnp.where(outer, edge, edge_after), codes[None]]
    )
    strips_left, strips_right = passed(strips, "gx", across)

    weights = level_weights(layer_tensor(layer_index, fibre), 3 * LANES)
    span = 3 * cells
    plane = pltpu.VMEM((span, depth, width), jnp.float32)
    side_plane = pltpu.VMEM((2, depth, 3 * LANES), jnp.float32)
    return pl.pallas_call(
        steps_kernel,
        out_shape=jax.ShapeDtypeStruct(state.shape, state.dtype),
        in_specs=[hbm, hbm, hbm, vmem, vmem, vmem, vmem],
        out_specs=hbm,
        scratch_shapes=[
            pltpu.VMEM((comps, span, depth, width), jnp.float32),
            plane,
            plane,
            plane,
            plane,
            plane,
            pltpu.VMEM((comps, 2, depth, 3 * LANES), jnp.float32),
            side_plane,
            side_plane,
            side_plane,
            pltpu.SemaphoreType.DMA((3,)),
        ],
        compiler_params=pltpu.CompilerParams(vmem_limit_bytes=48 << 20),
        name="steps",
    )(from_left, state, from_right, strips_left, strips, strips_right, weights)


def solution(mesh):
    placed = (P(None, "gx", None, "gy"), P("gx", None, "gy"), P(), P())
    return jax.shard_map(
        shards, mesh=mesh, in_specs=placed, out_specs=P(None, "gx", None, "gy"), check_vma=False
    )
```

time: 268 us -> 114 us (0.43)
  the two profiles are of different devices: /device:TPU:121 before, /device:TPU:160 now
where the time goes in v1:
time: 114 us; the launch traced here: 112 us
  Pallas kernels  55.8 us (49%)
  waiting for transfers between devices  32.6 us (29%)
  starting transfers between devices  22.2 us (19%)
    pallas_call x1, Pallas kernels, shards(): pl.pallas_call(steps_kernel, out_shape=jax.ShapeDtypeStruct(state.shape,...  53.2 us
    ppermute x3, waiting for transfers between devices, passed(): lax.ppermute(value, axis, up)  22.9 us
    ppermute x3, starting transfers between devices, passed(): lax.ppermute(value, axis, [(j, i) for i, j in up])  14.6 us
    ppermute x3, waiting for transfers between devices, passed(): lax.ppermute(value, axis, [(j, i) for i, j in up])  9.72 us
    ppermute x3, starting transfers between devices, passed(): lax.ppermute(value, axis, up)  7.67 us
    pallas_call x1, Pallas kernels, shards(): pl.pallas_call(edge_kernel, out_shape=jax.ShapeDtypeStruct((comps + 1, de...  2.54 us
  transfers between devices with their start and end apart: 6, of which 2 were waited for; matrix products, arithmetic and copies ran while one was open for 0% of the time, Pallas kernels for 0%

profile of v1, /device:TPU:160, one launch (start us, length us, event | category | flops | bytes accessed | tf_op | source)
XLA Modules:
  0.0 112.1 jit_solution(4664899836157264925)
XLA Ops:
  0.0 0.0 copy-start
  0.0 0.0 copy-start.1
  0.0 0.7 compare_bitcast_fusion
  0.8 0.1 copy.7
  0.9 2.5 %edges.1 = f32[13,16,128]{2,1,0:T(8,128)S(1)} custom-call(f32[12,8,16,256]{3,2,1,0:T(8,128)} %state_hbm.1, f32[16,128]{1,0:T(8,128)S(1)} %get-tuple-element.17.mask_ref), custom_call_target="tpu_custom_call" | custom-call | tf_op jit(solution)/shard_map/edges/pallas_call | solution.py:377
  3.4 2.9 %collective-permute-start.3 = (f32[13,16,128]{2,1,0:T(8,128)S(1)}, f32[13,16,128]{2,1,0:T(8,128)S(1)}, u32[]{:S(2)}, u32[]{:S(2)}) collective-permute-start(f32[13,16,128]{2,1,0:T(8,128)S(1)} %edges.1), channel_id=1, source_target_pairs={{1,0},{2,1},{3,2},{4,3},{5,4},{6,5},{7,6},{9,8},{10,9},{11,10},{12... | collective-permute-start | bytes 319496 | tf_op jit(solution)/shard_map/ppermute | solution.py:368
  6.3 3.8 %collective-permute-start.2 = (f32[13,16,128]{2,1,0:T(8,128)S(1)}, f32[13,16,128]{2,1,0:T(8,128)S(1)}, u32[]{:S(2)}, u32[]{:S(2)}) collective-permute-start(f32[13,16,128]{2,1,0:T(8,128)S(1)} %edges.1), channel_id=1, source_target_pairs={{0,1},{1,2},{2,3},{3,4},{4,5},{5,6},{6,7},{8,9},{9,10},{10,11},{11... | collective-permute-start | bytes 319496 | tf_op jit(solution)/shard_map/ppermute | solution.py:368
  10.2 3.8 %collective-permute-start.1 = (f32[12,8,16,256]{3,2,1,0:T(8,128)}, f32[12,8,16,256]{3,2,1,0:T(8,128)S(1)}, u32[]{:S(2)}, u32[]{:S(2)}) collective-permute-start(f32[12,8,16,256]{3,2,1,0:T(8,128)} %state_hbm.1), channel_id=1, source_target_pairs={{8,0},{16,8},{24,16},{32,24},{40,32},{48,40},{56,48},{64,56},{72,6... | collective-permute-start | bytes 4718600 | tf_op jit(solution)/shard_map/ppermute | solution.py:368
  14.0 1.9 %collective-permute-start = (f32[12,8,16,256]{3,2,1,0:T(8,128)}, f32[12,8,16,256]{3,2,1,0:T(8,128)S(1)}, u32[]{:S(2)}, u32[]{:S(2)}) collective-permute-start(f32[12,8,16,256]{3,2,1,0:T(8,128)} %state_hbm.1), channel_id=1, source_target_pairs={{0,8},{8,16},{16,24},{24,32},{32,40},{40,48},{48,56},{56,64},{64,7... | collective-permute-start | bytes 4718600 | tf_op jit(solution)/shard_map/ppermute | solution.py:368
  15.9 0.0 copy-done
  15.9 0.1 multiply_multiply_fusion.1
  16.0 0.0 copy-done.1
  16.0 0.1 select_reduce_fusion
  16.1 0.1 add_multiply_fusion
  16.2 0.0 collective-permute-done.3
  16.2 0.0 collective-permute-done.2
  16.3 7.9 %collective-permute-start.5 = (f32[27,16,128]{2,1,0:T(8,128)S(1)}, f32[27,16,128]{2,1,0:T(8,128)}, u32[]{:S(2)}, u32[]{:S(2)}) collective-permute-start(f32[27,16,128]{2,1,0:T(8,128)S(1)} %pad_maximum_fusion.strip_ref), channel_id=1, source_target_pairs={{8,0},{16,8},{24,16},{32,24},{40,32},{48,40},{56,48},{64,56},{72,6... | collective-permute-start | bytes 663560 | tf_op jit(solution)/shard_map/ppermute | solution.py:368
  24.1 1.9 %collective-permute-start.4 = (f32[27,16,128]{2,1,0:T(8,128)S(1)}, f32[27,16,128]{2,1,0:T(8,128)}, u32[]{:S(2)}, u32[]{:S(2)}) collective-permute-start(f32[27,16,128]{2,1,0:T(8,128)S(1)} %pad_maximum_fusion.strip_ref), channel_id=1, source_target_pairs={{0,8},{8,16},{16,24},{24,32},{32,40},{40,48},{48,56},{56,64},{64,7... | collective-permute-start | bytes 663560 | tf_op jit(solution)/shard_map/ppermute | solution.py:368
  26.1 0.1 fusion.8
  26.2 9.7 %collective-permute-done.5.strip_right_ref = f32[27,16,128]{2,1,0:T(8,128)} collective-permute-done((f32[27,16,128]{2,1,0:T(8,128)S(1)}, f32[27,16,128]{2,1,0:T(8,128)}, u32[]{:S(2)}, u32[]{:S(2)}) %collective-permute-start.5) | collective-permute-done | bytes 221216 | tf_op jit(solution)/shard_map/ppermute | solution.py:368
  35.9 22.9 %collective-permute-done.4.strip_left_ref = f32[27,16,128]{2,1,0:T(8,128)} collective-permute-done((f32[27,16,128]{2,1,0:T(8,128)S(1)}, f32[27,16,128]{2,1,0:T(8,128)}, u32[]{:S(2)}, u32[]{:S(2)}) %collective-permute-start.4) | collective-permute-done | bytes 221216 | tf_op jit(solution)/shard_map/ppermute | solution.py:368
  58.8 0.0 collective-permute-done.1.right_hbm
  58.8 0.0 collective-permute-done.left_hbm
  58.8 0.1 broadcast_in_dim.37.weight_ref
  58.9 53.2 %steps.1 = f32[12,8,16,256]{3,2,1,0:T(8,128)} custom-call(f32[12,8,16,256]{3,2,1,0:T(8,128)S(1)} %collective-permute-done.left_hbm, f32[12,8,16,256]{3,2,1,0:T(8,128)} %state_hbm.1, f32[12,8,16,256]{3,2,1,0:T(8,128)S(1)} %collective-permute-done.1.right_hbm, f32[27,16,128]{2,1,0:T(8,128)} %collective-permute-done.4.strip_left_ref, ...), custom_call_target="tpu_custom_call" | custom-call | tf_op jit(solution)/shard_map/steps/pallas_call | solution.py:396
  (11 shorter events, 0.2 us)
Async XLA Ops:
  0.0 15.9 %copy-start = (f32[2,8]{1,0:T(2,128)S(1)}, f32[2,8]{1,0:T(2,128)}, u32[]{:S(2)}) copy-start(f32[2,8]{1,0:T(2,128)} %param.7) | copy-start | bytes 196
  0.0 16.0 %copy-start.1 = (s32[16]{0:T(128)S(1)}, s32[16]{0:T(128)}, u32[]{:S(2)}) copy-start(s32[16]{0:T(128)} %param.6) | copy-start | bytes 196
  3.4 12.8 %collective-permute-start.3 = (f32[13,16,128]{2,1,0:T(8,128)S(1)}, f32[13,16,128]{2,1,0:T(8,128)S(1)}, u32[]{:S(2)}, u32[]{:S(2)}) collective-permute-start(f32[13,16,128]{2,1,0:T(8,128)S(1)} %edges.1), channel_id=1, source_target_pairs={{1,0},{2,1},{3,2},{4,3},{5,4},{6,5},{7,6},{9,8},{10,9},{11,10},{12... | collective-permute-start | bytes 319496 | tf_op jit(solution)/shard_map/ppermute | solution.py:368
  6.3 9.9 %collective-permute-start.2 = (f32[13,16,128]{2,1,0:T(8,128)S(1)}, f32[13,16,128]{2,1,0:T(8,128)S(1)}, u32[]{:S(2)}, u32[]{:S(2)}) collective-permute-start(f32[13,16,128]{2,1,0:T(8,128)S(1)} %edges.1), channel_id=1, source_target_pairs={{0,1},{1,2},{2,3},{3,4},{4,5},{5,6},{6,7},{8,9},{9,10},{10,11},{11... | collective-permute-start | bytes 319496 | tf_op jit(solution)/shard_map/ppermute | solution.py:368
  10.2 48.6 %collective-permute-start.1 = (f32[12,8,16,256]{3,2,1,0:T(8,128)}, f32[12,8,16,256]{3,2,1,0:T(8,128)S(1)}, u32[]{:S(2)}, u32[]{:S(2)}) collective-permute-start(f32[12,8,16,256]{3,2,1,0:T(8,128)} %state_hbm.1), channel_id=1, source_target_pairs={{8,0},{16,8},{24,16},{32,24},{40,32},{48,40},{56,48},{64,56},{72,6... | collective-permute-start | bytes 4718600 | tf_op jit(solution)/shard_map/ppermute | solution.py:368
  14.0 44.8 %collective-permute-start = (f32[12,8,16,256]{3,2,1,0:T(8,128)}, f32[12,8,16,256]{3,2,1,0:T(8,128)S(1)}, u32[]{:S(2)}, u32[]{:S(2)}) collective-permute-start(f32[12,8,16,256]{3,2,1,0:T(8,128)} %state_hbm.1), channel_id=1, source_target_pairs={{0,8},{8,16},{16,24},{24,32},{32,40},{40,48},{48,56},{56,64},{64,7... | collective-permute-start | bytes 4718600 | tf_op jit(solution)/shard_map/ppermute | solution.py:368
  16.3 19.6 %collective-permute-start.5 = (f32[27,16,128]{2,1,0:T(8,128)S(1)}, f32[27,16,128]{2,1,0:T(8,128)}, u32[]{:S(2)}, u32[]{:S(2)}) collective-permute-start(f32[27,16,128]{2,1,0:T(8,128)S(1)} %pad_maximum_fusion.strip_ref), channel_id=1, source_target_pairs={{8,0},{16,8},{24,16},{32,24},{40,32},{48,40},{56,48},{64,56},{72,6... | collective-permute-start | bytes 663560 | tf_op jit(solution)/shard_map/ppermute | solution.py:368
  24.1 34.7 %collective-permute-start.4 = (f32[27,16,128]{2,1,0:T(8,128)S(1)}, f32[27,16,128]{2,1,0:T(8,128)}, u32[]{:S(2)}, u32[]{:S(2)}) collective-permute-start(f32[27,16,128]{2,1,0:T(8,128)S(1)} %pad_maximum_fusion.strip_ref), channel_id=1, source_target_pairs={{0,8},{8,16},{16,24},{24,32},{32,40},{40,48},{48,56},{56,64},{64,7... | collective-permute-start | bytes 663560 | tf_op jit(solution)/shard_map/ppermute | solution.py:368

commit v2 on v1

--- a/solution.py
+++ b/solution.py
@@ -198,18 +198,96 @@
             total = jnp.where(lane // GROUP == i, turned, total)
         return total
 
-    def one(c, carry):
-        edge_ref[c] = packed(
-            lambda i: state_ref[c, i, :, :LANES], lambda i: state_ref[c, i, :, width - LANES :]
-        )
+    def some(k, carry):
+        for q in range(3):
+            c = 3 * k + q
+            edge_ref[c] = packed(
+                lambda i: state_ref[c, i, :, :LANES], lambda i: state_ref[c, i, :, width - LANES :]
+            )
         return carry
 
-    lax.fori_loop(0, COMPS, one, 0)
+    lax.fori_loop(0, COMPS // 3, some, 0)
     spread = lambda i, b: jnp.broadcast_to(mask_ref[:, 2 * i + b : 2 * i + b + 1], (depth, LANES))
     edge_ref[COMPS] = packed(lambda i: spread(i, 0), lambda i: spread(i, 1))
 
 
-def steps_kernel(
+def react_tile(store, held, place, level, part):
+    rows = pl.ds(level * 8, 8)
+    live = held[place, rows, part]
+    new = react([store[c, place, rows, part] for c in range(COMPS)])
+    for c in range(1, COMPS):
+        pltpu.store(store.at[c, place, rows, part], new[c], mask=live > 0.5)
+    return live, new[0]
+
+
+def react_rows(main, inside, pot, rows):
+    for x in rows:
+        for level in range(main.shape[2] // 8):
+            for i in range(main.shape[3] // LANES):
+                part = pl.ds(i * LANES, LANES)
+                live, u = react_tile(main, inside, x, level, part)
+                pltpu.store(main.at[0, x, pl.ds(level * 8, 8), part], u, mask=live > 0.5)
+                pot[x, pl.ds(level * 8, 8), part] = live * u
+
+
+def shift_row(pot, dy_ref, sy_ref, x, ext, strip_row):
+    shape = (pot.shape[1], LANES)
+    lane = lax.broadcasted_iota(jnp.int32, shape, 1)
+    first_lane, last_lane = lane == 0, lane == LANES - 1
+    block = pl.ds(pl.multiple_of(ext // 8 * LANES, LANES), LANES)
+    place = lax.rem(ext, 8) * GROUP
+    before = pltpu.roll(strip_row(0, block), lax.rem(2 * LANES - place - (EDGE - 1), LANES), 1)
+    after = pltpu.roll(strip_row(1, block), lax.rem(2 * LANES - 1 - place - EDGE, LANES), 1)
+    near, far = pot[x, :, :LANES], pot[x, :, LANES:]
+    near_up, far_up = pltpu.roll(near, 1, 1), pltpu.roll(far, 1, 1)
+    near_down, far_down = pltpu.roll(near, LANES - 1, 1), pltpu.roll(far, LANES - 1, 1)
+    lower = jnp.where(first_lane, before, near_up)
+    upper = jnp.where(last_lane, far_down, near_down)
+    dy_ref[x, :, :LANES] = upper - lower
+    sy_ref[x, :, :LANES] = upper + lower
+    lower = jnp.where(first_lane, near_up, far_up)
+    upper = jnp.where(last_lane, after, far_down)
+    dy_ref[x, :, LANES:] = upper - lower
+    sy_ref[x, :, LANES:] = upper + lower
+
+
+def spread(weight_ref, p, dx, sx, dy, sy, cross):
+    depth, lanes = p.shape
+    w = [weight_ref[i, :, :lanes] for i in range(9)]
+    rising = w[3] * p - w[4] * dx - w[5] * dy
+    falling = w[6] * p + w[7] * dx + w[8] * dy
+    return (
+        w[0] * sx
+        + w[1] * sy
+        + w[2] * cross
+        + pltpu.roll(rising, 1, 0)
+        + pltpu.roll(falling, depth - 1, 0)
+    )
+
+
+def row_spread(weight_ref, pot, dy_ref, sy_ref, x):
+    before, after = pot[x - 1], pot[x + 1]
+    return spread(
+        weight_ref,
+        pot[x],
+        after - before,
+        after + before,
+        dy_ref[x],
+        sy_ref[x],
+        dy_ref[x + 1] - dy_ref[x - 1],
+    )
+
+
+def strip_spread(weight_ref, p):
+    long = p.shape[1]
+    lower, upper = pltpu.roll(p, 1, 1), pltpu.roll(p, long - 1, 1)
+    before, after = pltpu.roll(p, GROUP, 1), pltpu.roll(p, long - GROUP, 1)
+    dy = upper - lower
+    cross = pltpu.roll(dy, long - GROUP, 1) - pltpu.roll(dy, GROUP, 1)
+    return spread(weight_ref, p, after - before, after + before, dy, upper + lower, cross)
+
+
+def near_kernel(
     left_hbm,
     state_hbm,
     right_hbm,
@@ -217,32 +295,35 @@
     strip_ref,
     strip_right_ref,
     weight_ref,
-    out_hbm,
-    main,
+    main_out,
     inside,
     total,
+    strip_track,
+    track,
+    main,
     pot,
     dy_ref,
     sy_ref,
     strip,
     strip_inside,
     strip_total,
-    strip_pot,
     sems,
+    out_sems,
 ):
     cells, depth, width = state_hbm.shape[1:]
+    near = left_hbm.shape[1]
     span = 3 * cells
+    skip = cells - near
+    count = cells + 2 * near
     sides = (0, 1)
-    long = 3 * LANES
     copies = [
-        pltpu.make_async_copy(source, main.at[:, pl.ds(i * cells, cells)], sems.at[i])
-        for i, source in enumerate((left_hbm, state_hbm, right_hbm))
+        pltpu.make_async_copy(source, main.at[:, pl.ds(start, source.shape[1])], sems.at[i])
+        for i, (start, source) in enumerate(
+            ((0, left_hbm), (near, state_hbm), (near + cells, right_hbm))
+        )
     ]
     for copy in copies:
         copy.start()
-    lane = lax.broadcasted_iota(jnp.int32, (depth, LANES), 1)
-    first_lane = lane == 0
-    last_lane = lane == LANES - 1
 
     for i, source in enumerate((strip_left_ref, strip_ref, strip_right_ref)):
         part = pl.ds(i * LANES, LANES)
@@ -250,107 +331,148 @@
             for c in range(COMPS):
                 strip[c, side, :, part] = source[side * (COMPS + 1) + c]
             strip_inside[side, :, part] = source[side * (COMPS + 1) + COMPS]
-            strip_pot[side, :, part] = source[side * (COMPS + 1) + COMPS]
         codes = source[2 * (COMPS + 1)]
         for x in range(cells):
-            for b in range(2):
+            for b in range(width // LANES):
                 value = jnp.broadcast_to(codes[:, 2 * x + b : 2 * x + b + 1], (depth, LANES))
                 inside[i * cells + x, :, b * LANES : (b + 1) * LANES] = value
-                pot[i * cells + x, :, b * LANES : (b + 1) * LANES] = value
-
-    def shift_row(x, carry):
-        block = pl.ds(pl.multiple_of(x // 8 * LANES, LANES), LANES)
-        place = lax.rem(x, 8) * GROUP
-        before = pltpu.roll(strip_pot[0, :, block], lax.rem(2 * LANES - place - (EDGE - 1), LANES), 1)
-        after = pltpu.roll(strip_pot[1, :, block], lax.rem(2 * LANES - 1 - place - EDGE, LANES), 1)
-        near, far = pot[x, :, :LANES], pot[x, :, LANES:]
-        near_up, far_up = pltpu.roll(near, 1, 1), pltpu.roll(far, 1, 1)
-        near_down, far_down = pltpu.roll(near, LANES - 1, 1), pltpu.roll(far, LANES - 1, 1)
-        lower = jnp.where(first_lane, before, near_up)
-        upper = jnp.where(last_lane, far_down, near_down)
-        dy_ref[x, :, :LANES] = upper - lower
-        sy_ref[x, :, :LANES] = upper + lower
-        lower = jnp.where(first_lane, near_up, far_up)
-        upper = jnp.where(last_lane, after, far_down)
-        dy_ref[x, :, LANES:] = upper - lower
-        sy_ref[x, :, LANES:] = upper + lower
+
+    def shift_mask(k, carry):
+        for q in range(4):
+            x = 4 * k + q
+            shift_row(inside, dy_ref, sy_ref, x, x, lambda side, block: strip_inside[side, :, block])
         return carry
 
-    def spread(p, dx, sx, dy, sy, cross, lanes):
-        w = [weight_ref[i, :, :lanes] for i in range(9)]
-        rising = w[3] * p - w[4] * dx - w[5] * dy
-        falling = w[6] * p + w[7] * dx + w[8] * dy
-        return (
-            w[0] * sx
-            + w[1] * sy
-            + w[2] * cross
-            + pltpu.roll(rising, 1, 0)
-            + pltpu.roll(falling, depth - 1, 0)
-        )
-
-    def row_spread(x):
-        before, after = pot[x - 1], pot[x + 1]
-        return spread(
-            pot[x], after - before, after + before, dy_ref[x], sy_ref[x], dy_ref[x + 1] - dy_ref[x - 1], width
-        )
-
-    def strip_spread(side):
-        p = strip_pot[side]
-        lower, upper = pltpu.roll(p, 1, 1), pltpu.roll(p, long - 1, 1)
-        before, after = pltpu.roll(p, GROUP, 1), pltpu.roll(p, long - GROUP, 1)
-        dy = upper - lower
-        cross = pltpu.roll(dy, long - GROUP, 1) - pltpu.roll(dy, GROUP, 1)
-        return spread(p, after - before, after + before, dy, upper + lower, cross, long)
-
-    lax.fori_loop(0, span, shift_row, 0)
-
-    def total_row(x, carry):
-        total[x] = row_spread(x)
+    lax.fori_loop(0, span // 4, shift_mask, 0)
+
+    def total_rows(k, carry):
+        for q in range(2):
+            x = 1 + 2 * k + q
+            total[x] = row_spread(weight_ref, inside, dy_ref, sy_ref, x)
         return carry
 
-    lax.fori_loop(1, span - 1, total_row, 0)
+    lax.fori_loop(0, span // 2 - 1, total_rows, 0)
     for side in sides:
-        strip_total[side] = strip_spread(side)
+        strip_total[side] = strip_spread(weight_ref, strip_inside[side])
     for copy in copies:
         copy.wait()
 
-    def react_tile(store, held, place, level, part):
-        rows = pl.ds(level * 8, 8)
-        old = [store[c, place, rows, part] for c in range(COMPS)]
-        live = held[place, rows, part]
-        new = react(old)
-        new = [jnp.where(live > 0.5, a, b) for a, b in zip(new, old)]
-        for c in range(COMPS):
-            store[c, place, rows, part] = new[c]
-        return live * new[0]
+    def finished(s, wait):
+        for q, row in enumerate((s, count - 1 - s)):
+            copy = pltpu.make_async_copy(
+                main.at[:, pl.ds(row, 1)], main_out.at[:, pl.ds(row, 1)], out_sems.at[2 * s + q]
+            )
+            if wait:
+                copy.wait()
+            else:
+                copy.start()
 
     def step(s, carry):
         for side in sides:
             for level in range(depth // 8):
                 for i in range(3):
                     part = pl.ds(i * LANES, LANES)
-                    value = react_tile(strip, strip_inside, side, level, part)
-                    strip_pot[side, pl.ds(level * 8, 8), part] = value
-
-        def react_row(x, carry):
-            for level in range(depth // 8):
-                for i in range(2):
-                    part = pl.ds(i * LANES, LANES)
-                    pot[x, pl.ds(level * 8, 8), part] = react_tile(main, inside, x, level, part)
+                    rows = pl.ds(level * 8, 8)
+                    live, u = react_tile(strip, strip_inside, side, level, part)
+                    pltpu.store(strip.at[0, side, rows, part], u, mask=live > 0.5)
+                    strip_track[s, side, rows, part] = live * u
+
+        def react_some(k, carry):
+            react_rows(main, inside.at[pl.ds(skip, count)], pot, (s + 2 * k, s + 2 * k + 1))
             return carry
 
-        lax.fori_loop(s, span - s, react_row, 0)
-        lax.fori_loop(s, span - s, shift_row, 0)
-
-        def diffuse_row(x, carry):
-            u = main[0, x]
-            main[0, x] = u + inside[x] * (row_spread(x) - u * total[x])
+        lax.fori_loop(0, count // 2 - s, react_some, 0)
+
+        def shift_some(k, carry):
+            for q in range(4):
+                x = 4 * k + q
+                shift_row(
+                    pot, dy_ref, sy_ref, x, skip + x, lambda side, block: strip_track[s, side, :, block]
+                )
             return carry
 
-        lax.fori_loop(s + 1, span - 1 - s, diffuse_row, 0)
+        lax.fori_loop(0, count // 4, shift_some, 0)
+        for q, row in enumerate((s + 1, count - 2 - s)):
+            track[s, q, 0] = pot[row]
+            track[s, q, 1] = dy_ref[row]
+
+        def diffuse_some(k, carry):
+            for q in range(2):
+                x = s + 1 + 2 * k + q
+                u = main[0, x]
+                flow = row_spread(weight_ref, pot, dy_ref, sy_ref, x) - u * total[skip + x]
+                main[0, x] = u + inside[skip + x] * flow
+            return carry
+
+        lax.fori_loop(0, count // 2 - 1 - s, diffuse_some, 0)
         for side in sides:
             u = strip[0, side]
-            strip[0, side] = u + strip_inside[side] * (strip_spread(side) - u * strip_total[side])
+            flow = strip_spread(weight_ref, strip_track[s, side]) - u * strip_total[side]
+            strip[0, side] = u + strip_inside[side] * flow
+        finished(s, False)
+        return carry
+
+    lax.fori_loop(0, STEPS, step, 0)
+    lax.fori_loop(0, STEPS, lambda s, carry: finished(s, True) or carry, 0)
+
+
+def far_kernel(
+    left_hbm,
+    main_hbm,
+    right_hbm,
+    inside,
+    total,
+    strip_track,
+    track,
+    weight_ref,
+    out_hbm,
+    main,
+    pot,
+    dy_ref,
+    sy_ref,
+    sems,
+):
+    cells, depth, width = out_hbm.shape[1:]
+    far = left_hbm.shape[1]
+    count = main_hbm.shape[1]
+    span = far + count + far
+    copies = [
+        pltpu.make_async_copy(source, main.at[:, pl.ds(start, source.shape[1])], sems.at[i])
+        for i, (start, source) in enumerate(
+            ((0, left_hbm), (far, main_hbm), (far + count, right_hbm))
+        )
+    ]
+    for copy in copies:
+        copy.start()
+    for copy in copies:
+        copy.wait()
+
+    def step(s, carry):
+        starts = (s, span - far - s)
+
+        def react_some(k, carry):
+            row = jnp.where(k < far // 2, s + 2 * k, span - 2 * far - s + 2 * k)
+            react_rows(main, inside, pot, (row, row + 1))
+            return carry
+
+        lax.fori_loop(0, far, react_some, 0)
+        for q, row in enumerate((s + far, span - 1 - far - s)):
+            pot[row] = inside[row] * main[0, row]
+        for first in (s, span - 1 - far - s):
+            for q in range(far + 1):
+                x = first + q
+                shift_row(
+                    pot, dy_ref, sy_ref, x, x, lambda side, block: strip_track[s, side, :, block]
+                )
+        for q, row in enumerate((s + far + 1, span - 2 - far - s)):
+            pot[row] = track[s, q, 0]
+            dy_ref[row] = track[s, q, 1]
+        for first in (s + 1, span - 1 - far - s):
+            for q in range(far):
+                x = first + q
+                u = main[0, x]
+                flow = row_spread(weight_ref, pot, dy_ref, sy_ref, x) - u * total[x]
+                main[0, x] = u + inside[x] * flow
         return carry
 
     lax.fori_loop(0, STEPS, step, 0)
@@ -362,58 +484,86 @@
 def shards(state, tissue_mask, layer_index, fibre):
     comps, cells, depth, width = state.shape
     across, along = lax.axis_size("gx"), lax.axis_size("gy")
-
-    def passed(value, axis, size):
+    half = cells // 2
+    span = 3 * cells
+    f32 = jnp.float32
+
+    def passed(upward, downward, axis, size):
         up = [(i, i + 1) for i in range(size - 1)]
-        return lax.ppermute(value, axis, up), lax.ppermute(value, axis, [(j, i) for i, j in up])
+        down = [(j, i) for i, j in up]
+        return lax.ppermute(upward, axis, up), lax.ppermute(downward, axis, down)
 
     vmem = pl.BlockSpec(memory_space=pltpu.VMEM)
     hbm = pl.BlockSpec(memory_space=pl.ANY)
-    from_left, from_right = passed(state, "gx", across)
+    params = pltpu.CompilerParams(vmem_limit_bytes=40 << 20)
+    low, high = state[:, :half], state[:, half:]
+    near_left, near_right = passed(high, low, "gx", across)
 
     blocks = tissue_mask.shape[2]
-    codes = (tissue_mask > 0).astype(jnp.float32).transpose(1, 0, 2).reshape(depth, cells * blocks)
+    codes = (tissue_mask > 0).astype(f32).transpose(1, 0, 2).reshape(depth, cells * blocks)
     codes = jnp.pad(codes, ((0, 0), (0, LANES - cells * blocks)))
     edge = pl.pallas_call(
         edge_kernel,
-        out_shape=jax.ShapeDtypeStruct((comps + 1, depth, LANES), jnp.float32),
+        out_shape=jax.ShapeDtypeStruct((comps + 1, depth, LANES), f32),
         in_specs=[vmem, vmem],
         out_specs=vmem,
-        compiler_params=pltpu.CompilerParams(vmem_limit_bytes=32 << 20),
+        compiler_params=params,
         name="edges",
     )(state, codes)
-    edge_before, edge_after = passed(edge, "gy", along)
+    edge_before, edge_after = passed(edge, edge, "gy", along)
     outer = lax.broadcasted_iota(jnp.int32, edge.shape, 2) % GROUP < EDGE
     strips = jnp.concatenate(
         [jnp.where(outer, edge_before, edge), jnp.where(outer, edge, edge_after), codes[None]]
     )
-    strips_left, strips_right = passed(strips, "gx", across)
+    strips_left, strips_right = passed(strips, strips, "gx", across)
+    low, high, strips = lax.optimization_barrier((low, high, strips))
+    far_left, far_right = passed(low, high, "gx", across)
 
     weights = level_weights(layer_tensor(layer_index, fibre), 3 * LANES)
-    span = 3 * cells
-    plane = pltpu.VMEM((span, depth, width), jnp.float32)
-    side_plane = pltpu.VMEM((2, depth, 3 * LANES), jnp.float32)
+    count = cells + 2 * half
+    row_cost = comps * depth * width * 60
+    main, inside, total, strip_track, track = pl.pallas_call(
+        near_kernel,
+        out_shape=[
+            jax.ShapeDtypeStruct((comps, count, depth, width), f32),
+            jax.ShapeDtypeStruct((span, depth, width), f32),
+            jax.ShapeDtypeStruct((span, depth, width), f32),
+            jax.ShapeDtypeStruct((STEPS, 2, depth, 3 * LANES), f32),
+            jax.ShapeDtypeStruct((STEPS, 2, 2, depth, width), f32),
+        ],
+        in_specs=[hbm, hbm, hbm, vmem, vmem, vmem, vmem],
+        out_specs=[hbm, vmem, vmem, vmem, vmem],
+        scratch_shapes=[
+            pltpu.VMEM((comps, count, depth, width), f32),
+            pltpu.VMEM((count, depth, width), f32),
+            pltpu.VMEM((span, depth, width), f32),
+            pltpu.VMEM((span, depth, width), f32),
+            pltpu.VMEM((comps, 2, depth, 3 * LANES), f32),
+            pltpu.VMEM((2, depth, 3 * LANES), f32),
+            pltpu.VMEM((2, depth, 3 * LANES), f32),
+            pltpu.SemaphoreType.DMA((3,)),
+            pltpu.SemaphoreType.DMA((2 * STEPS,)),
+        ],
+        compiler_params=params,
+        cost_estimate=pl.CostEstimate(flops=96 * row_cost, bytes_accessed=8 << 20, transcendentals=0),
+        name="near",
+    )(near_left, state, near_right, strips_left, strips, strips_right, weights)
     return pl.pallas_call(
-        steps_kernel,
+        far_kernel,
         out_shape=jax.ShapeDtypeStruct(state.shape, state.dtype),
-        in_specs=[hbm, hbm, hbm, vmem, vmem, vmem, vmem],
+        in_specs=[hbm, hbm, hbm, vmem, vmem, vmem, vmem, vmem],
         out_specs=hbm,
         scratch_shapes=[
-            pltpu.VMEM((comps, span, depth, width), jnp.float32),
-            plane,
-            plane,
-            plane,
-            plane,
-            plane,
-            pltpu.VMEM((comps, 2, depth, 3 * LANES), jnp.float32),
-            side_plane,
-            side_plane,
-            side_plane,
+            pltpu.VMEM((comps, span, depth, width), f32),
+            pltpu.VMEM((span, depth, width), f32),
+            pltpu.VMEM((span, depth, width), f32),
+            pltpu.VMEM((span, depth, width), f32),
             pltpu.SemaphoreType.DMA((3,)),
         ],
-        compiler_params=pltpu.CompilerParams(vmem_limit_bytes=48 << 20),
-        name="steps",
-    )(from_left, state, from_right, strips_left, strips, strips_right, weights)
+        compiler_params=params,
+        cost_estimate=pl.CostEstimate(flops=64 * row_cost, bytes_accessed=8 << 20, transcendentals=0),
+        name="far",
+    )(far_left, main, far_right, inside, total, strip_track, track, weights)
 
 
 def solution(mesh):

time: 114 us -> 119 us (1.044); the launches traced: 112 us -> 119 us
  Pallas kernels: 55.8 us -> 44.6 us
  starting transfers between devices: 22.2 us -> 30.3 us
  waiting for transfers between devices: 32.6 us -> 37.8 us
  local copies, waits for them, and re-layouts: 0.27 us -> 4.66 us
    pallas_call x1 -> x2, Pallas kernels: 53.2 us -> 43.9 us  [the longest x1 27.9 us: shards(): pl.pallas_call(near_kernel, out_shape=[jax.ShapeDtypeStruct((comps, count...]
    ppermute x6 -> x8, starting transfers between devices: 22.2 us -> 30.3 us  [passed(): return (lax.ppermute(upward, axis, up), lax.ppermute(downward, axis, down))]
    ppermute x6 -> x8, waiting for transfers between devices: 32.6 us -> 37.8 us  [passed(): return (lax.ppermute(upward, axis, up), lax.ppermute(downward, axis, down))]
    unnamed x4 -> x12, local copies, waits for them, and re-layouts: 0.01 us -> 3.05 us
    pallas_call x1, Pallas kernels: 2.54 us -> 0.63 us  [shards(): pl.pallas_call(edge_kernel, out_shape=jax.ShapeDtypeStruct((comps + 1, de...]
    slice x0 -> x1, local copies, waits for them, and re-layouts: none -> 1.34 us  [shards(): low, high = (state[:, :half], state[:, half:])]
  transfers between devices with their start and end apart: 6 -> 8, of which waited for: 2 -> 2; matrix products, arithmetic and copies ran while one was open for 0% -> 2% of each run, Pallas kernels for 0% -> 23%
where the time goes in v2:
time: 119 us
  Pallas kernels  44.6 us (37%)
  waiting for transfers between devices  37.8 us (32%)
  starting transfers between devices  30.3 us (25%)
  local copies, waits for them, and re-layouts  4.66 us (4%)
    ppermute x8, waiting for transfers between devices, passed(): return (lax.ppermute(upward, axis, up), lax.ppermute(downward, axis, down))  37.8 us
    ppermute x8, starting transfers between devices, passed(): return (lax.ppermute(upward, axis, up), lax.ppermute(downward, axis, down))  30.3 us
    pallas_call x1, Pallas kernels, shards(): pl.pallas_call(near_kernel, out_shape=[jax.ShapeDtypeStruct((comps, count...  27.9 us
    pallas_call x1, Pallas kernels, shards(): pl.pallas_call(far_kernel, out_shape=jax.ShapeDtypeStruct(state.shape, st...  16.1 us
    unnamed x12, local copies, waits for them, and re-layouts  3.05 us
  transfers between devices with their start and end apart: 8, of which 2 were waited for; matrix products, arithmetic and copies ran while one was open for 2% of the time, Pallas kernels for 23%

profile of v2, /device:TPU:160, one launch (start us, length us, event | category | flops | bytes accessed | tf_op | source)
XLA Modules:
  0.0 118.6 jit_solution(5697529364913062048)
XLA Ops:
  0.0 0.7 compare_bitcast_fusion
  0.7 0.1 copy.7
  0.8 0.0 copy-start
  0.8 1.4 %copy-done = f32[12,8,16,256]{3,2,1,0:T(8,128)S(1)} copy-done((f32[12,8,16,256]{3,2,1,0:T(8,128)S(1)}, f32[12,8,16,256]{3,2,1,0:T(8,128)}, u32[]{:S(2)}) %copy-start) | copy-done | bytes 1572888
  2.2 0.6 edges.1
  2.9 0.0 copy-start.4
  2.9 0.0 copy-start.5
  2.9 0.0 copy-start.1
  2.9 3.0 %collective-permute-start.1 = (f32[13,16,128]{2,1,0:T(8,128)S(1)}, f32[13,16,128]{2,1,0:T(8,128)S(1)}, u32[]{:S(2)}, u32[]{:S(2)}) collective-permute-start(f32[13,16,128]{2,1,0:T(8,128)S(1)} %edges.1), channel_id=1, source_target_pairs={{1,0},{2,1},{3,2},{4,3},{5,4},{6,5},{7,6},{9,8},{10,9},{11,10},{12... | collective-permute-start | bytes 319496 | tf_op jit(solution)/shard_map/ppermute | solution.py:494
  6.0 3.8 %collective-permute-start = (f32[13,16,128]{2,1,0:T(8,128)S(1)}, f32[13,16,128]{2,1,0:T(8,128)S(1)}, u32[]{:S(2)}, u32[]{:S(2)}) collective-permute-start(f32[13,16,128]{2,1,0:T(8,128)S(1)} %edges.1), channel_id=1, source_target_pairs={{0,1},{1,2},{2,3},{3,4},{4,5},{5,6},{6,7},{8,9},{9,10},{10,11},{11... | collective-permute-start | bytes 319496 | tf_op jit(solution)/shard_map/ppermute | solution.py:494
  9.8 1.3 %fusion.9 = (f32[12,4,16,256]{3,2,1,0:T(8,128)}, f32[12,4,16,256]{3,2,1,0:T(8,128)}) fusion(f32[12,8,16,256]{3,2,1,0:T(8,128)S(1)} %copy-done), kind=kLoop, calls=%fused_computation.36 | loop fusion | bytes 3145728 | tf_op jit(solution)/shard_map/slice | solution.py:499
  11.1 1.9 %collective-permute-start.3 = (f32[12,4,16,256]{3,2,1,0:T(8,128)}, f32[12,4,16,256]{3,2,1,0:T(8,128)}, u32[]{:S(2)}, u32[]{:S(2)}) collective-permute-start(f32[12,4,16,256]{3,2,1,0:T(8,128)} %get-tuple-element.16), channel_id=1, source_target_pairs={{0,8},{8,16},{16,24},{24,32},{32,40},{40,48},{48,56},{56,64},{64,7... | collective-permute-start | bytes 2359304 | tf_op jit(solution)/shard_map/ppermute | solution.py:494
  13.0 7.9 %collective-permute-start.4 = (f32[12,4,16,256]{3,2,1,0:T(8,128)}, f32[12,4,16,256]{3,2,1,0:T(8,128)}, u32[]{:S(2)}, u32[]{:S(2)}) collective-permute-start(f32[12,4,16,256]{3,2,1,0:T(8,128)} %get-tuple-element.13), channel_id=1, source_target_pairs={{8,0},{16,8},{24,16},{32,24},{40,32},{48,40},{56,48},{64,56},{72,6... | collective-permute-start | bytes 2359304 | tf_op jit(solution)/shard_map/ppermute | solution.py:494
  20.9 0.0 copy-done.4
  20.9 0.1 multiply_multiply_fusion.1
  21.0 0.0 collective-permute-done.1
  21.1 0.0 collective-permute-done
  21.1 1.9 %collective-permute-start.2 = (f32[12,4,16,256]{3,2,1,0:T(8,128)}, f32[12,4,16,256]{3,2,1,0:T(8,128)S(1)}, u32[]{:S(2)}, u32[]{:S(2)}) collective-permute-start(f32[12,4,16,256]{3,2,1,0:T(8,128)} %get-tuple-element.13), channel_id=1, source_target_pairs={{0,8},{8,16},{16,24},{24,32},{32,40},{40,48},{48,56},{56,64},{64,7... | collective-permute-start | bytes 2359304 | tf_op jit(solution)/shard_map/ppermute | solution.py:494
  23.0 7.9 %collective-permute-start.7 = (f32[12,4,16,256]{3,2,1,0:T(8,128)}, f32[12,4,16,256]{3,2,1,0:T(8,128)S(1)}, u32[]{:S(2)}, u32[]{:S(2)}) collective-permute-start(f32[12,4,16,256]{3,2,1,0:T(8,128)} %get-tuple-element.16), channel_id=1, source_target_pairs={{8,0},{16,8},{24,16},{32,24},{40,32},{48,40},{56,48},{64,56},{72,6... | collective-permute-start | bytes 2359304 | tf_op jit(solution)/shard_map/ppermute | solution.py:494
  30.9 0.0 copy-done.5
  30.9 0.1 select_reduce_fusion
  31.0 1.9 %collective-permute-start.6 = (f32[27,16,128]{2,1,0:T(8,128)S(1)}, f32[27,16,128]{2,1,0:T(8,128)S(1)}, u32[]{:S(2)}, u32[]{:S(2)}) collective-permute-start(f32[27,16,128]{2,1,0:T(8,128)S(1)} %pad_maximum_fusion.strip_ref), channel_id=1, source_target_pairs={{8,0},{16,8},{24,16},{32,24},{40,32},{48,40},{56,48},{64,56},{72,6... | collective-permute-start | bytes 663560 | tf_op jit(solution)/shard_map/ppermute | solution.py:494
  33.0 0.1 add_multiply_fusion
  33.0 27.5 %collective-permute-done.6.strip_right_ref = f32[27,16,128]{2,1,0:T(8,128)S(1)} collective-permute-done((f32[27,16,128]{2,1,0:T(8,128)S(1)}, f32[27,16,128]{2,1,0:T(8,128)S(1)}, u32[]{:S(2)}, u32[]{:S(2)}) %collective-permute-start.6) | collective-permute-done | bytes 221216 | tf_op jit(solution)/shard_map/ppermute | solution.py:494
  60.5 0.0 copy-start.2
  60.5 0.7 copy-done.2
  61.2 1.9 %collective-permute-start.5 = (f32[27,16,128]{2,1,0:T(8,128)S(1)}, f32[27,16,128]{2,1,0:T(8,128)}, u32[]{:S(2)}, u32[]{:S(2)}) collective-permute-start(f32[27,16,128]{2,1,0:T(8,128)S(1)} %pad_maximum_fusion.strip_ref), channel_id=1, source_target_pairs={{0,8},{8,16},{16,24},{24,32},{32,40},{40,48},{48,56},{56,64},{64,7... | collective-permute-start | bytes 663560 | tf_op jit(solution)/shard_map/ppermute | solution.py:494
  63.2 0.1 fusion.8
  63.3 10.3 %collective-permute-done.5.strip_left_ref = f32[27,16,128]{2,1,0:T(8,128)} collective-permute-done((f32[27,16,128]{2,1,0:T(8,128)S(1)}, f32[27,16,128]{2,1,0:T(8,128)}, u32[]{:S(2)}, u32[]{:S(2)}) %collective-permute-start.5) | collective-permute-done | bytes 221216 | tf_op jit(solution)/shard_map/ppermute | solution.py:494
  73.5 0.0 collective-permute-done.3.left_hbm
  73.5 0.0 collective-permute-done.4.right_hbm
  73.6 0.1 broadcast_in_dim.37.weight_ref
  73.6 0.0 copy-done.1
  73.7 0.0 copy-start.3
  73.7 0.9 copy-done.3
  74.6 27.9 %near.1 = (f32[12,16,16,256]{3,2,1,0:T(8,128)S(1)}, f32[24,16,256]{2,1,0:T(8,128)S(1)}, f32[24,16,256]{2,1,0:T(8,128)S(1)}, f32[8,2,16,384]{3,2,1,0:T(8,128)S(1)}, f32[8,2,2,16,256]{4,3,2,1,0:T(8,128)S(1)}) custom-call(f32[12,4,16,256]{3,2,1,0:T(8,128)} %collective-permute-done.3.left_hbm, f32[12,8,16,256]{3,2,1,0:T(8,128)S(1)} %copy-done.1, ...), custom_call_target="tpu_custom_call" | custom-call | flops 283115520 | bytes 8388608 | tf_op jit(solution)/shard_map/near/pallas_call | solution.py:525
  102.5 0.0 collective-permute-done.2.left_hbm
  102.5 0.0 collective-permute-done.7.right_hbm
  102.5 16.1 %far.1 = f32[12,8,16,256]{3,2,1,0:T(8,128)} custom-call(f32[12,4,16,256]{3,2,1,0:T(8,128)S(1)} %collective-permute-done.2.left_hbm, f32[12,16,16,256]{3,2,1,0:T(8,128)S(1)} %get-tuple-element.15.main_hbm, f32[12,4,16,256]{3,2,1,0:T(8,128)S(1)} %collective-permute-done.7.right_hbm, f32[24,16,256]{2,1,0:T(8,128)S(1)} %get-tuple-element.17.inside, ...), custom_call_target="tpu_custom_call" | custom-call | flops 188743680 | bytes 8388608 | tf_op jit(solution)/shard_map/far/pallas_call | solution.py:551
  (11 shorter events, 0.2 us)
Async XLA Ops:
  0.8 1.4 %copy-start = (f32[12,8,16,256]{3,2,1,0:T(8,128)S(1)}, f32[12,8,16,256]{3,2,1,0:T(8,128)}, u32[]{:S(2)}) copy-start(f32[12,8,16,256]{3,2,1,0:T(8,128)} %state_hbm.1) | copy-start | bytes 4718596
  2.9 18.1 %copy-start.4 = (f32[2,8]{1,0:T(2,128)S(1)}, f32[2,8]{1,0:T(2,128)}, u32[]{:S(2)}) copy-start(f32[2,8]{1,0:T(2,128)} %param.7) | copy-start | bytes 196
  2.9 28.0 %copy-start.5 = (s32[16]{0:T(128)S(1)}, s32[16]{0:T(128)}, u32[]{:S(2)}) copy-start(s32[16]{0:T(128)} %param.6) | copy-start | bytes 196
  2.9 70.8 %copy-start.1 = (f32[12,8,16,256]{3,2,1,0:T(8,128)S(1)}, f32[12,8,16,256]{3,2,1,0:T(8,128)}, u32[]{:S(2)}) copy-start(f32[12,8,16,256]{3,2,1,0:T(8,128)} %state_hbm.1) | copy-start | bytes 4718596
  2.9 18.1 %collective-permute-start.1 = (f32[13,16,128]{2,1,0:T(8,128)S(1)}, f32[13,16,128]{2,1,0:T(8,128)S(1)}, u32[]{:S(2)}, u32[]{:S(2)}) collective-permute-start(f32[13,16,128]{2,1,0:T(8,128)S(1)} %edges.1), channel_id=1, source_target_pairs={{1,0},{2,1},{3,2},{4,3},{5,4},{6,5},{7,6},{9,8},{10,9},{11,10},{12... | collective-permute-start | bytes 319496 | tf_op jit(solution)/shard_map/ppermute | solution.py:494
  6.0 15.1 %collective-permute-start = (f32[13,16,128]{2,1,0:T(8,128)S(1)}, f32[13,16,128]{2,1,0:T(8,128)S(1)}, u32[]{:S(2)}, u32[]{:S(2)}) collective-permute-start(f32[13,16,128]{2,1,0:T(8,128)S(1)} %edges.1), channel_id=1, source_target_pairs={{0,1},{1,2},{2,3},{3,4},{4,5},{5,6},{6,7},{8,9},{9,10},{10,11},{11... | collective-permute-start | bytes 319496 | tf_op jit(solution)/shard_map/ppermute | solution.py:494
  11.1 62.4 %collective-permute-start.3 = (f32[12,4,16,256]{3,2,1,0:T(8,128)}, f32[12,4,16,256]{3,2,1,0:T(8,128)}, u32[]{:S(2)}, u32[]{:S(2)}) collective-permute-start(f32[12,4,16,256]{3,2,1,0:T(8,128)} %get-tuple-element.16), channel_id=1, source_target_pairs={{0,8},{8,16},{16,24},{24,32},{32,40},{40,48},{48,56},{56,64},{64,7... | collective-permute-start | bytes 2359304 | tf_op jit(solution)/shard_map/ppermute | solution.py:494
  13.0 60.5 %collective-permute-start.4 = (f32[12,4,16,256]{3,2,1,0:T(8,128)}, f32[12,4,16,256]{3,2,1,0:T(8,128)}, u32[]{:S(2)}, u32[]{:S(2)}) collective-permute-start(f32[12,4,16,256]{3,2,1,0:T(8,128)} %get-tuple-element.13), channel_id=1, source_target_pairs={{8,0},{16,8},{24,16},{32,24},{40,32},{48,40},{56,48},{64,56},{72,6... | collective-permute-start | bytes 2359304 | tf_op jit(solution)/shard_map/ppermute | solution.py:494
  21.1 81.3 %collective-permute-start.2 = (f32[12,4,16,256]{3,2,1,0:T(8,128)}, f32[12,4,16,256]{3,2,1,0:T(8,128)S(1)}, u32[]{:S(2)}, u32[]{:S(2)}) collective-permute-start(f32[12,4,16,256]{3,2,1,0:T(8,128)} %get-tuple-element.13), channel_id=1, source_target_pairs={{0,8},{8,16},{16,24},{24,32},{32,40},{40,48},{48,56},{56,64},{64,7... | collective-permute-start | bytes 2359304 | tf_op jit(solution)/shard_map/ppermute | solution.py:494
  23.0 79.4 %collective-permute-start.7 = (f32[12,4,16,256]{3,2,1,0:T(8,128)}, f32[12,4,16,256]{3,2,1,0:T(8,128)S(1)}, u32[]{:S(2)}, u32[]{:S(2)}) collective-permute-start(f32[12,4,16,256]{3,2,1,0:T(8,128)} %get-tuple-element.16), channel_id=1, source_target_pairs={{8,0},{16,8},{24,16},{32,24},{40,32},{48,40},{56,48},{64,56},{72,6... | collective-permute-start | bytes 2359304 | tf_op jit(solution)/shard_map/ppermute | solution.py:494
  31.0 29.5 %collective-permute-start.6 = (f32[27,16,128]{2,1,0:T(8,128)S(1)}, f32[27,16,128]{2,1,0:T(8,128)S(1)}, u32[]{:S(2)}, u32[]{:S(2)}) collective-permute-start(f32[27,16,128]{2,1,0:T(8,128)S(1)} %pad_maximum_fusion.strip_ref), channel_id=1, source_target_pairs={{8,0},{16,8},{24,16},{32,24},{40,32},{48,40},{56,48},{64,56},{72,6... | collective-permute-start | bytes 663560 | tf_op jit(solution)/shard_map/ppermute | solution.py:494
  60.5 0.7 copy-start.2
  61.2 12.3 %collective-permute-start.5 = (f32[27,16,128]{2,1,0:T(8,128)S(1)}, f32[27,16,128]{2,1,0:T(8,128)}, u32[]{:S(2)}, u32[]{:S(2)}) collective-permute-start(f32[27,16,128]{2,1,0:T(8,128)S(1)} %pad_maximum_fusion.strip_ref), channel_id=1, source_target_pairs={{0,8},{8,16},{16,24},{24,32},{32,40},{40,48},{48,56},{56,64},{64,7... | collective-permute-start | bytes 663560 | tf_op jit(solution)/shard_map/ppermute | solution.py:494
  73.7 0.9 copy-start.3

commit v3 on v2

--- a/solution.py
+++ b/solution.py
@@ -1,4 +1,3 @@
-import functools
 import math
 
 import jax
@@ -8,8 +7,8 @@
 from jax.experimental.pallas import tpu as pltpu
 from jax.sharding import PartitionSpec as P
 
+
 STEPS = 8
-MASK_BLOCK = 128
 COMPS = 12
 EDGE = 8
 GROUP = 2 * EDGE
@@ -40,6 +39,9 @@
         away = x * (100.0 * root) + centre * root
         return jnp.exp2(math.log2(scale) - away * away)
 
+    def step(rate, offset):
+        return jax.nn.sigmoid(x * (100.0 * rate) + offset)
+
     def inverse(value):
         return 1.0 / value
 
@@ -47,11 +49,13 @@
         return steady + (gate - steady) * jnp.exp2(exponent)
 
     e = math.exp
-    decay = -time_step * LOG2E
+    speed = time_step * LOG2E
     voltage = 100.0 * x
     rev_potassium = thermal_volt * math.log(potassium_out / potassium_in)
     rev_sodium = thermal_volt * math.log(sodium_out / sodium_in)
-    rev_slow = thermal_volt * math.log((potassium_out + 0.03 * sodium_out) / (potassium_in + 0.03 * sodium_in))
+    rev_slow = thermal_volt * math.log(
+        (potassium_out + 0.03 * sodium_out) / (potassium_in + 0.03 * sodium_in)
+    )
     up20 = power(1 / 20)
     up10 = up20 * up20
     up5 = up10 * up10
@@ -63,26 +67,35 @@
     down14 = power(-1 / 14)
     down7 = down14 * down14
     fall = jnp.exp2(jnp.minimum(x * (-50.0 * LOG2E) - 20.0 * LOG2E, 120.0))
-    upper = inverse(1.0 + fall)
-    lower = fall * upper
+    minus_upper = inverse(-1.0 - fall)
+    minus_lower = fall * minus_upper
 
     above = voltage - rev_potassium
     cam = jnp.maximum(calcium, 0.02)
-    past_calcium = voltage - 0.5 * thermal_volt * math.log(calcium_out / 0.001) + (0.5 * thermal_volt) * jnp.log(cam)
+    past_calcium = (voltage - 0.5 * thermal_volt * math.log(calcium_out / 0.001)) + (
+        0.5 * thermal_volt
+    ) * jnp.log(cam)
     past_sodium = voltage - rev_sodium
     inward_x = 1.0 + power(0.06, -0.06 * (rev_potassium + 200.0))
     inward_y = 1.0 + fall * e(20.0 + 0.5 * rev_potassium)
-    inward_b = power(0.0002, 0.0002 * (100.0 - rev_potassium), 30.0) + up10 * (10.0 * e(-0.1 * rev_potassium - 1.0))
+    inward_b = power(0.0002, 0.0002 * (100.0 - rev_potassium), 30.0) + up10 * (
+        10.0 * e(-0.1 * rev_potassium - 1.0)
+    )
     inward = (5.405 * inward_y) * inverse(inward_y + inward_b * inward_x)
-    plateau = 0.0146 * inverse(1.0 + power(-1 / 5.98, 25.0 / 5.98))
-    pump = (2.724 * potassium_out / (potassium_out + 1.0) * sodium_in / (sodium_in + 40.0)) * inverse(
-        1.0 + power(-0.1 / thermal_volt, 0.0, 0.1245) + power(-1.0 / thermal_volt, 0.0, 0.0353))
+    plateau = inverse(1.0 / 0.0146 + power(-1 / 5.98, 25.0 / 5.98, 1.0 / 0.0146))
+    full = power(-1.0 / thermal_volt)
+    pump_top = 2.724 * potassium_out / (potassium_out + 1.0) * sodium_in / (sodium_in + 40.0)
+    pump = inverse(
+        (power(-0.1 / thermal_volt, 0.0, 0.1245 / pump_top) + 1.0 / pump_top)
+        + full * (0.0353 / pump_top)
+    )
     whole = 1000.0 / ((87.5**3 + sodium_out**3) * (1.38 + calcium_out))
-    back = power(-0.65 / thermal_volt, 0.0, 0.1)
-    exchange = (power(0.35 / thermal_volt, 0.0, whole * sodium_in**3 * calcium_out)
-                - back * (cam * (10.0 * 2.5 * 0.001 * whole * sodium_out**3))) * inverse(1.0 + back)
-    pump_calcium = (0.1238 * cam) * inverse(cam + 0.5)
-    calcium_sum = (0.08 * calact * calinact + 0.000592) * past_calcium
+    inner = whole * sodium_in**3 * calcium_out
+    exchange = (inner - (cam * (2.5 * 0.001 * whole * sodium_out**3)) * full) * inverse(
+        power(-0.35 / thermal_volt) + 0.1 * full
+    )
+    pump_calcium = 0.1238 - 0.0619 * inverse(cam + 0.5)
+    calcium_sum = (0.08 * calact * calinact + 0.000592) * past_calcium + pump_calcium
     ionic = (
         (14.838 * act * (act * act) * inact * slow + 0.00029) * past_sodium
         + calcium_sum
@@ -90,57 +103,85 @@
         + (0.392 * slowact * slowact) * (voltage - rev_slow)
         + pump
         + exchange
-        + pump_calcium
     )
     new_x = x - (time_step / 100.0) * ionic
-    new_calcium = calcium - (time_step * 0.05) * (calcium_sum + pump_calcium - 2.0 * exchange)
-
-    a = up5 * e(7.0)
+    new_calcium = calcium - (time_step * 0.05) * (calcium_sum - 2.0 * exchange)
+
+    a = up5 * (e(7.0))
     b = power(1 / 200, -0.25)
-    root = inverse(1.0 + power(-1 / 9.03, -56.86 / 9.03))
-    rate = (((1.0 + e(-5.0)) * 10.0 * decay + a * (10.0 * decay)) + down5 * (e(-12.0) * 10.0 * decay)) * (1.0 + b) * inverse(2.0 + a + b)
+    root = step(1 / 9.03, 56.86 / 9.03)
+    rate = ((a * (-10.0 * speed) - (1.0 + e(-5.0)) * 10.0 * speed) - down5 * (e(-12.0) * 10.0 * speed)) * (
+        (1.0 + b) * inverse(2.0 + a + b)
+    )
     new_act = moved(act, root * root, rate)
 
-    root = inverse(1.0 + power(1 / 7.43, 71.55 / 7.43))
+    root = step(-1 / 7.43, -71.55 / 7.43)
     steady = root * root
-    rate = lower * (power(-1 / 6.8, -80.0 / 6.8, 0.057 * -decay) + power(0.079, 0.0, 2.7 * -decay) + power(0.3485, 0.0, 310000.0 * -decay)) + (
-        upper * (0.77 / 0.13 * -decay)) * inverse(1.0 + power(-1 / 11.1, -10.66 / 11.1))
-    new_inact = moved(inact, steady, -rate)
-    rate = lower * (
-        (power(0.2444, 0.0, 25428.0 * -decay) + power(-0.04391, 0.0, 6.948e-06 * -decay)) * (voltage + 37.78) * inverse(1.0 + power(0.311, 0.311 * 79.23))
-        - power(-0.01052, 0.0, 0.02424 * -decay) * inverse(1.0 + power(-0.1378, -0.1378 * 40.14))
-    ) - upper * power(0.057, 0.0, 0.6 * -decay) * inverse(1.0 + down10 * e(-3.2))
+    rate = minus_lower * (
+        power(-1 / 6.8, -80.0 / 6.8, 0.057 * speed)
+        + power(0.079, 0.0, 2.7 * speed)
+        + power(0.3485, 0.0, 310000.0 * speed)
+    ) + minus_upper * inverse(
+        1.0 / (0.77 / 0.13 * speed) + power(-1 / 11.1, -10.66 / 11.1, 1.0 / (0.77 / 0.13 * speed))
+    )
+    new_inact = moved(inact, steady, rate)
+    rate = minus_lower * (
+        power(-0.01052, 0.0, 0.02424 * speed) * step(0.1378, 0.1378 * 40.14)
+        - (power(0.2444, 0.0, 25428.0 * speed) + power(-0.04391, 0.0, 6.948e-06 * speed))
+        * ((voltage + 37.78) * step(-0.311, -0.311 * 79.23))
+    ) + minus_upper * (
+        power(0.057) * inverse(1.0 / (0.6 * speed) + down10 * (e(-3.2) / (0.6 * speed)))
+    )
     new_slow = moved(slow, steady, rate)
 
     p = 1.0 + power(-1 / 13, -35.0 / 13)
-    r = 1.0 + down20 * e(2.5)
+    r = down20 * (-speed * e(2.5)) - speed
     pq = p * (1.0 + up5 * e(1.0))
-    rate = (decay * pq) * r * inverse((1.96 + 0.35 * p) * r + pq)
-    new_calact = moved(calact, inverse(1.0 + power(-1 / 7.5, -8.0 / 7.5)), rate)
-
-    a = down10 * e(1.3)
-    b = up10 * e(3.0)
-    den = (1.0 + e(4.3)) + a + b
-    rate = (decay * den) * inverse((bell(27.0, 225.0, 1102.5) + 20.0) * den + (380.0 + 200.0 * b + 180.0 * a))
+    rate = pq * (r * inverse((-1.96 / speed - (0.35 / speed) * p) * r + pq))
+    new_calact = moved(calact, step(1 / 7.5, 8.0 / 7.5), rate)
+
+    b = up10 * (-speed * e(3.0))
+    den = (down10 * (-speed * e(1.3)) - speed * (1.0 + e(4.3))) + b
+    rate = den * inverse(
+        (380.0 - 180.0 * (1.0 + e(4.3)) - (20.0 / speed) * b)
+        - (bell(27.0, 225.0, 1102.5 / speed) + 200.0 / speed) * den
+    )
     new_calinact = moved(calinact, down7 * inverse(down7 + e(20.0 / 7)), rate)
 
-    rate = decay * inverse(bell(40.0, 1800.0, 9.5) + 0.8)
+    rate = inverse(-0.8 / speed - bell(40.0, 1800.0, 9.5 / speed))
     new_tract = moved(tract, inverse(1.0 + down6 * e(20.0 / 6)), rate)
 
-    t = 1.0 + up5 * e(-4.0)
-    rate = (decay * t) * inverse((bell(45.0, 320.0, 85.0) + 3.0) * t + 5.0)
+    t = up5 * (-speed * e(-4.0)) - speed
+    rate = t * inverse(5.0 - (bell(45.0, 320.0, 85.0 / speed) + 3.0 / speed) * t)
     new_trinact = moved(trinact, inverse(1.0 + up5 * e(4.0)), rate)
 
-    rate = (decay / 2700.0 + down10 * (e(-4.5) * decay / 2700.0)) * (1.0 + power(1 / 11.5, 30.0 / 11.5))
+    rate = (down10 * (-speed * e(-4.5) / 2700.0) - speed / 2700.0) * (
+        1.0 + power(1 / 11.5, 30.0 / 11.5)
+    )
     new_rapact = moved(rapact, inverse(1.0 + down7 * e(-26.0 / 7)), rate)
 
-    rate = (1.0 + e(-6.0)) * decay / 3.36 + (up20 + down20) * (e(-3.0) * decay / 3.36)
-    new_rapinact = moved(rapinact, inverse(1.0 + power(1 / 24, 88.0 / 24)), rate)
-
-    y = 1.0 + up15 * e(-35.0 / 15)
-    rate = (decay * y) * inverse(1400.0 * lax.rsqrt(1.0 + down6 * e(5.0 / 6)) + 80.0 * y)
+    rate = (up20 + down20) * (-speed * e(-3.0) / 3.36) - speed * (1.0 + e(-6.0)) / 3.36
+    new_rapinact = moved(rapinact, step(-1 / 24, -88.0 / 24), rate)
+
+    y = up15 * (-speed * e(-35.0 / 15)) - speed
+    rate = y * inverse(
+        lax.rsqrt(1.0 / 1400.0**2 + down6 * (e(5.0 / 6) / 1400.0**2)) - (80.0 / speed) * y
+    )
     new_slowact = moved(slowact, inverse(1.0 + down14 * e(-5.0 / 14)), rate)
-    return (new_x, new_act, new_inact, new_slow, new_calact, new_calinact, new_tract, new_trinact, new_rapact, new_rapinact, new_slowact, new_calcium)
+    return (
+        new_x,
+        new_act,
+        new_inact,
+        new_slow,
+        new_calact,
+        new_calinact,
+        new_tract,
+        new_trinact,
+        new_rapact,
+        new_rapinact,
+        new_slowact,
+        new_calcium,
+    )
 
 
 def layer_tensor(layer_index, fibre):
@@ -185,9 +226,30 @@
     return jnp.broadcast_to(rows[:, :, None], rows.shape + (lanes,))
 
 
-def edge_kernel(state_ref, mask_ref, edge_ref):
-    depth, width = state_ref.shape[2], state_ref.shape[3]
-    cells = state_ref.shape[1]
+def first_kernel(state_hbm, mask_ref, inner_hbm, outer_hbm, edge_ref, main, inside, sems):
+    cells, depth, width = state_hbm.shape[1:]
+    half = cells // 2
+    odd = lax.rem(lax.axis_index("gx"), 2)
+    copies = [
+        pltpu.make_async_copy(state_hbm.at[:, pl.ds(2 * i, 2)], main.at[:, pl.ds(2 * i, 2)], sems.at[i])
+        for i in range(cells // 2)
+    ]
+    for copy in copies:
+        copy.start()
+    for x in range(cells):
+        for b in range(width // LANES):
+            part = pl.ds(b * LANES, LANES)
+            code = mask_ref[:, 2 * x + b : 2 * x + b + 1]
+            inside[x, :, part] = jnp.broadcast_to(code, (depth, LANES))
+    for i, copy in enumerate(copies):
+        copy.wait()
+        react_rows(main, inside, None, (2 * i, 2 * i + 1))
+    copies = [
+        pltpu.make_async_copy(main.at[:, pl.ds((1 - odd) * half, half)], inner_hbm, sems.at[0]),
+        pltpu.make_async_copy(main.at[:, pl.ds(odd * half, half)], outer_hbm, sems.at[1]),
+    ]
+    for copy in copies:
+        copy.start()
     lane = lax.broadcasted_iota(jnp.int32, (depth, LANES), 1)
 
     def packed(first, last):
@@ -202,13 +264,16 @@
         for q in range(3):
             c = 3 * k + q
             edge_ref[c] = packed(
-                lambda i: state_ref[c, i, :, :LANES], lambda i: state_ref[c, i, :, width - LANES :]
+                lambda i: main[c, i, :, :LANES], lambda i: main[c, i, :, width - LANES :]
             )
         return carry
 
     lax.fori_loop(0, COMPS // 3, some, 0)
-    spread = lambda i, b: jnp.broadcast_to(mask_ref[:, 2 * i + b : 2 * i + b + 1], (depth, LANES))
-    edge_ref[COMPS] = packed(lambda i: spread(i, 0), lambda i: spread(i, 1))
+    edge_ref[COMPS] = packed(
+        lambda i: inside[i, :, :LANES], lambda i: inside[i, :, width - LANES :]
+    )
+    for copy in copies:
+        copy.wait()
 
 
 def react_tile(store, held, place, level, part):
@@ -227,7 +292,8 @@
                 part = pl.ds(i * LANES, LANES)
                 live, u = react_tile(main, inside, x, level, part)
                 pltpu.store(main.at[0, x, pl.ds(level * 8, 8), part], u, mask=live > 0.5)
-                pot[x, pl.ds(level * 8, 8), part] = live * u
+                if pot is not None:
+                    pot[x, pl.ds(level * 8, 8), part] = live * u
 
 
 def shift_row(pot, dy_ref, sy_ref, x, ext, strip_row):
@@ -288,12 +354,13 @@
 
 
 def near_kernel(
-    left_hbm,
-    state_hbm,
-    right_hbm,
-    strip_left_ref,
+    inner_hbm,
+    facing_inner_hbm,
+    facing_outer_hbm,
+    outer_hbm,
+    strip_inner_ref,
     strip_ref,
-    strip_right_ref,
+    strip_outer_ref,
     weight_ref,
     main_out,
     inside,
@@ -310,8 +377,9 @@
     sems,
     out_sems,
 ):
-    cells, depth, width = state_hbm.shape[1:]
-    near = left_hbm.shape[1]
+    near, depth, width = inner_hbm.shape[1:]
+    cells = 2 * near
+    odd = lax.rem(lax.axis_index("gx"), 2)
     span = 3 * cells
     skip = cells - near
     count = cells + 2 * near
@@ -319,14 +387,23 @@
     copies = [
         pltpu.make_async_copy(source, main.at[:, pl.ds(start, source.shape[1])], sems.at[i])
         for i, (start, source) in enumerate(
-            ((0, left_hbm), (near, state_hbm), (near + cells, right_hbm))
+            (
+                (3 * near - 3 * near * odd, inner_hbm),
+                (2 * near - near * odd, facing_inner_hbm),
+                (near + near * odd, facing_outer_hbm),
+                (3 * near * odd, outer_hbm),
+            )
         )
     ]
     for copy in copies:
         copy.start()
 
-    for i, source in enumerate((strip_left_ref, strip_ref, strip_right_ref)):
-        part = pl.ds(i * LANES, LANES)
+    for i, source in (
+        (2 - 2 * odd, strip_inner_ref),
+        (1, strip_ref),
+        (2 * odd, strip_outer_ref),
+    ):
+        part = pl.ds(pl.multiple_of(i * LANES, LANES), LANES)
         for side in sides:
             for c in range(COMPS):
                 strip[c, side, :, part] = source[side * (COMPS + 1) + c]
@@ -367,22 +444,15 @@
             else:
                 copy.start()
 
+    def start_row(x, carry):
+        pot[x] = inside[skip + x] * main[0, x]
+        return carry
+
+    lax.fori_loop(0, count, start_row, 0)
+    for side in sides:
+        strip_track[0, side] = strip_inside[side] * strip[0, side]
+
     def step(s, carry):
-        for side in sides:
-            for level in range(depth // 8):
-                for i in range(3):
-                    part = pl.ds(i * LANES, LANES)
-                    rows = pl.ds(level * 8, 8)
-                    live, u = react_tile(strip, strip_inside, side, level, part)
-                    pltpu.store(strip.at[0, side, rows, part], u, mask=live > 0.5)
-                    strip_track[s, side, rows, part] = live * u
-
-        def react_some(k, carry):
-            react_rows(main, inside.at[pl.ds(skip, count)], pot, (s + 2 * k, s + 2 * k + 1))
-            return carry
-
-        lax.fori_loop(0, count // 2 - s, react_some, 0)
-
         def shift_some(k, carry):
             for q in range(4):
                 x = 4 * k + q
@@ -405,11 +475,34 @@
             return carry
 
         lax.fori_loop(0, count // 2 - 1 - s, diffuse_some, 0)
-        for side in sides:
-            u = strip[0, side]
-            flow = strip_spread(weight_ref, strip_track[s, side]) - u * strip_total[side]
-            strip[0, side] = u + strip_inside[side] * flow
         finished(s, False)
+
+        @pl.when(s < STEPS - 1)
+        def _():
+            for side in sides:
+                u = strip[0, side]
+                flow = strip_spread(weight_ref, strip_track[s, side]) - u * strip_total[side]
+                strip[0, side] = u + strip_inside[side] * flow
+
+            def react_strip(side, carry):
+                for level in range(depth // 8):
+                    for i in range(3):
+                        part = pl.ds(i * LANES, LANES)
+                        rows = pl.ds(level * 8, 8)
+                        live, u = react_tile(strip, strip_inside, side, level, part)
+                        pltpu.store(strip.at[0, side, rows, part], u, mask=live > 0.5)
+                        strip_track[s + 1, side, rows, part] = live * u
+                return carry
+
+            lax.fori_loop(0, 2, react_strip, 0)
+
+            def react_some(k, carry):
+                x = s + 1 + 2 * k
+                react_rows(main, inside.at[pl.ds(skip, count)], pot, (x, x + 1))
+                return carry
+
+            lax.fori_loop(0, count // 2 - 1 - s, react_some, 0)
+
         return carry
 
     lax.fori_loop(0, STEPS, step, 0)
@@ -417,9 +510,9 @@
 
 
 def far_kernel(
-    left_hbm,
+    inner_hbm,
     main_hbm,
-    right_hbm,
+    outer_hbm,
     inside,
     total,
     strip_track,
@@ -432,14 +525,19 @@
     sy_ref,
     sems,
 ):
-    cells, depth, width = out_hbm.shape[1:]
-    far = left_hbm.shape[1]
+    cells, _, _ = out_hbm.shape[1:]
+    far = inner_hbm.shape[1]
+    odd = lax.rem(lax.axis_index("gx"), 2)
     count = main_hbm.shape[1]
     span = far + count + far
     copies = [
         pltpu.make_async_copy(source, main.at[:, pl.ds(start, source.shape[1])], sems.at[i])
         for i, (start, source) in enumerate(
-            ((0, left_hbm), (far, main_hbm), (far + count, right_hbm))
+            (
+                ((1 - odd) * (far + count), inner_hbm),
+                (far, main_hbm),
+                (odd * (far + count), outer_hbm),
+            )
         )
     ]
     for copy in copies:
@@ -447,16 +545,12 @@
     for copy in copies:
         copy.wait()
 
+    for q in range(far):
+        for x in (q, span - 1 - q):
+            pot[x] = inside[x] * main[0, x]
+
     def step(s, carry):
-        starts = (s, span - far - s)
-
-        def react_some(k, carry):
-            row = jnp.where(k < far // 2, s + 2 * k, span - 2 * far - s + 2 * k)
-            react_rows(main, inside, pot, (row, row + 1))
-            return carry
-
-        lax.fori_loop(0, far, react_some, 0)
-        for q, row in enumerate((s + far, span - 1 - far - s)):
+        for row in (s + far, span - 1 - far - s):
             pot[row] = inside[row] * main[0, row]
         for first in (s, span - 1 - far - s):
             for q in range(far + 1):
@@ -473,6 +567,13 @@
                 u = main[0, x]
                 flow = row_spread(weight_ref, pot, dy_ref, sy_ref, x) - u * total[x]
                 main[0, x] = u + inside[x] * flow
+
+        def react_some(k, carry):
+            row = jnp.where(k < far // 2, s + 1 + 2 * k, span - 2 * far - s - 1 + 2 * k)
+            react_rows(main, inside, pot, (row, row + 1))
+            return carry
+
+        lax.fori_loop(0, jnp.where(s < STEPS - 1, far, 0), react_some, 0)
         return carry
 
     lax.fori_loop(0, STEPS, step, 0)
@@ -488,36 +589,45 @@
     span = 3 * cells
     f32 = jnp.float32
 
-    def passed(upward, downward, axis, size):
-        up = [(i, i + 1) for i in range(size - 1)]
-        down = [(j, i) for i, j in up]
-        return lax.ppermute(upward, axis, up), lax.ppermute(downward, axis, down)
+    def swapped(value, axis, size, first):
+        pairs = [(i, i + 1) for i in range(first, size - 1, 2)]
+        return lax.ppermute(value, axis, pairs + [(j, i) for i, j in pairs])
 
     vmem = pl.BlockSpec(memory_space=pltpu.VMEM)
     hbm = pl.BlockSpec(memory_space=pl.ANY)
     params = pltpu.CompilerParams(vmem_limit_bytes=40 << 20)
-    low, high = state[:, :half], state[:, half:]
-    near_left, near_right = passed(high, low, "gx", across)
-
     blocks = tissue_mask.shape[2]
     codes = (tissue_mask > 0).astype(f32).transpose(1, 0, 2).reshape(depth, cells * blocks)
     codes = jnp.pad(codes, ((0, 0), (0, LANES - cells * blocks)))
-    edge = pl.pallas_call(
-        edge_kernel,
-        out_shape=jax.ShapeDtypeStruct((comps + 1, depth, LANES), f32),
-        in_specs=[vmem, vmem],
-        out_specs=vmem,
+    face = jax.ShapeDtypeStruct((comps, half, depth, width), f32)
+    facing_inner, facing_outer, edge = pl.pallas_call(
+        first_kernel,
+        out_shape=[face, face, jax.ShapeDtypeStruct((comps + 1, depth, LANES), f32)],
+        in_specs=[hbm, vmem],
+        out_specs=[hbm, hbm, vmem],
+        scratch_shapes=[
+            pltpu.VMEM((comps, cells, depth, width), f32),
+            pltpu.VMEM((cells, depth, width), f32),
+            pltpu.SemaphoreType.DMA((cells // 2,)),
+        ],
         compiler_params=params,
-        name="edges",
+        name="first",
     )(state, codes)
-    edge_before, edge_after = passed(edge, edge, "gy", along)
+    edge_outer = swapped(edge, "gy", along, 1)
+    edge_inner = swapped(edge, "gy", along, 0)
+    near_outer = swapped(facing_outer, "gx", across, 1)
+    near_inner = swapped(facing_inner, "gx", across, 0)
+    odd_along = lax.rem(lax.axis_index("gy"), 2) == 1
+    edge_before = jnp.where(odd_along, edge_inner, edge_outer)
+    edge_after = jnp.where(odd_along, edge_outer, edge_inner)
     outer = lax.broadcasted_iota(jnp.int32, edge.shape, 2) % GROUP < EDGE
     strips = jnp.concatenate(
         [jnp.where(outer, edge_before, edge), jnp.where(outer, edge, edge_after), codes[None]]
     )
-    strips_left, strips_right = passed(strips, strips, "gx", across)
-    low, high, strips = lax.optimization_barrier((low, high, strips))
-    far_left, far_right = passed(low, high, "gx", across)
+    strip_outer = swapped(strips, "gx", across, 1)
+    strip_inner = swapped(strips, "gx", across, 0)
+    far_outer = swapped(facing_inner, "gx", across, 1)
+    far_inner = swapped(facing_outer, "gx", across, 0)
 
     weights = level_weights(layer_tensor(layer_index, fibre), 3 * LANES)
     count = cells + 2 * half
@@ -531,7 +641,7 @@
             jax.ShapeDtypeStruct((STEPS, 2, depth, 3 * LANES), f32),
             jax.ShapeDtypeStruct((STEPS, 2, 2, depth, width), f32),
         ],
-        in_specs=[hbm, hbm, hbm, vmem, vmem, vmem, vmem],
+        in_specs=[hbm, hbm, hbm, hbm, vmem, vmem, vmem, vmem],
         out_specs=[hbm, vmem, vmem, vmem, vmem],
         scratch_shapes=[
             pltpu.VMEM((comps, count, depth, width), f32),
@@ -541,13 +651,22 @@
             pltpu.VMEM((comps, 2, depth, 3 * LANES), f32),
             pltpu.VMEM((2, depth, 3 * LANES), f32),
             pltpu.VMEM((2, depth, 3 * LANES), f32),
-            pltpu.SemaphoreType.DMA((3,)),
+            pltpu.SemaphoreType.DMA((4,)),
             pltpu.SemaphoreType.DMA((2 * STEPS,)),
         ],
         compiler_params=params,
         cost_estimate=pl.CostEstimate(flops=96 * row_cost, bytes_accessed=8 << 20, transcendentals=0),
         name="near",
-    )(near_left, state, near_right, strips_left, strips, strips_right, weights)
+    )(
+        near_inner,
+        facing_inner,
+        facing_outer,
+        near_outer,
+        strip_inner,
+        strips,
+        strip_outer,
+        weights,
+    )
     return pl.pallas_call(
         far_kernel,
         out_shape=jax.ShapeDtypeStruct(state.shape, state.dtype),
@@ -563,11 +682,12 @@
         compiler_params=params,
         cost_estimate=pl.CostEstimate(flops=64 * row_cost, bytes_accessed=8 << 20, transcendentals=0),
         name="far",
-    )(far_left, main, far_right, inside, total, strip_track, track, weights)
+    )(far_inner, main, far_outer, inside, total, strip_track, track, weights)
 
 
 def solution(mesh):
     placed = (P(None, "gx", None, "gy"), P("gx", None, "gy"), P(), P())
+
     return jax.shard_map(
         shards, mesh=mesh, in_specs=placed, out_specs=P(None, "gx", None, "gy"), check_vma=False
     )

time: 119 us -> 95.1 us (0.80)
  the two profiles are of different devices: /device:TPU:160 before, /device:TPU:130 now
where the time goes in v3:
time: 95.1 us; the launch traced here: 94.8 us
  Pallas kernels  39.7 us (42%)
  waiting for transfers between devices  32.8 us (34%)
  starting transfers between devices  17.6 us (19%)
  local copies, waits for them, and re-layouts  3.29 us (3%)
  other arithmetic  1.1 us (1%)
    ppermute x8, waiting for transfers between devices, swapped(): return lax.ppermute(value, axis, pairs + [(j, i) for i, j in pairs])  32.8 us
    pallas_call x1, Pallas kernels, shards(): pl.pallas_call(near_kernel, out_shape=[jax.ShapeDtypeStruct((comps, count...  23.4 us
    ppermute x8, starting transfers between devices, swapped(): return lax.ppermute(value, axis, pairs + [(j, i) for i, j in pairs])  17.6 us
    pallas_call x1, Pallas kernels, shards(): pl.pallas_call(far_kernel, out_shape=jax.ShapeDtypeStruct(state.shape, st...  14 us
    unnamed x10, local copies, waits for them, and re-layouts  3.03 us
    pallas_call x1, Pallas kernels, shards(): pl.pallas_call(first_kernel, out_shape=[face, face, jax.ShapeDtypeStruct(...  2.31 us
  transfers between devices with their start and end apart: 8, of which 2 were waited for; matrix products, arithmetic and copies ran while one was open for 1% of the time, Pallas kernels for 25%

profile of v3, /device:TPU:130, one launch (start us, length us, event | category | flops | bytes accessed | tf_op | source)
XLA Modules:
  0.0 94.8 jit_solution(8680100566833609030)
XLA Ops:
  0.0 0.0 copy-start.3
  0.0 0.0 copy-start.4
  0.0 0.7 compare_bitcast_fusion
  0.8 0.1 copy.7
  0.9 0.0 copy-start
  0.9 1.4 %copy-done = f32[12,8,16,256]{3,2,1,0:T(8,128)S(1)} copy-done((f32[12,8,16,256]{3,2,1,0:T(8,128)S(1)}, f32[12,8,16,256]{3,2,1,0:T(8,128)}, u32[]{:S(2)}) %copy-start) | copy-done | bytes 1572888
  2.3 2.3 %first.1 = (f32[12,4,16,256]{3,2,1,0:T(8,128)S(1)}, f32[12,4,16,256]{3,2,1,0:T(8,128)S(1)}, f32[13,16,128]{2,1,0:T(8,128)S(1)}) custom-call(f32[12,8,16,256]{3,2,1,0:T(8,128)S(1)} %copy-done, f32[16,128]{1,0:T(8,128)S(1)} %get-tuple-element.34.mask_ref), custom_call_target="tpu_custom_call" | custom-call | tf_op jit(solution)/shard_map/first/pallas_call | solution.py:603
  4.6 1.1 %collective-permute-start.3 = (f32[13,16,128]{2,1,0:T(8,128)S(1)}, f32[13,16,128]{2,1,0:T(8,128)S(1)}, u32[]{:S(2)}, u32[]{:S(2)}) collective-permute-start(f32[13,16,128]{2,1,0:T(8,128)S(1)} %get-tuple-element.15), channel_id=1, source_target_pairs={{0,1},{2,3},{4,5},{6,7},{1,0},{3,2},{5,4},{7,6},{8,9},{10,11},{12,... | collective-permute-start | bytes 319496 | tf_op jit(solution)/shard_map/ppermute | solution.py:594
  5.7 2.9 %collective-permute-start.4 = (f32[13,16,128]{2,1,0:T(8,128)S(1)}, f32[13,16,128]{2,1,0:T(8,128)S(1)}, u32[]{:S(2)}, u32[]{:S(2)}) collective-permute-start(f32[13,16,128]{2,1,0:T(8,128)S(1)} %get-tuple-element.15), channel_id=1, source_target_pairs={{1,2},{3,4},{5,6},{2,1},{4,3},{6,5},{9,10},{11,12},{13,14},{10,9},... | collective-permute-start | bytes 319496 | tf_op jit(solution)/shard_map/ppermute | solution.py:594
  8.6 3.1 %collective-permute-start.2 = (f32[12,4,16,256]{3,2,1,0:T(8,128)S(1)}, f32[12,4,16,256]{3,2,1,0:T(8,128)}, u32[]{:S(2)}, u32[]{:S(2)}) collective-permute-start(f32[12,4,16,256]{3,2,1,0:T(8,128)S(1)} %get-tuple-element.13.facing_outer_hbm), channel_id=1, source_target_pairs={{8,16},{24,32},{40,48},{56,64},{72,80},{88,96},{104,112},{120,128}... | collective-permute-start | bytes 2359304 | tf_op jit(solution)/shard_map/ppermute | solution.py:594
  11.7 0.6 collective-permute-start
  12.3 0.1 collective-permute-start.1
  12.4 0.0 copy-done.3
  12.4 0.1 multiply_multiply_fusion.1
  12.4 0.0 copy-done.4
  12.5 0.1 select_reduce_fusion
  12.6 0.0 collective-permute-done.3
  12.6 6.6 %collective-permute-start.7 = (f32[12,4,16,256]{3,2,1,0:T(8,128)S(1)}, f32[12,4,16,256]{3,2,1,0:T(8,128)S(1)}, u32[]{:S(2)}, u32[]{:S(2)}) collective-permute-start(f32[12,4,16,256]{3,2,1,0:T(8,128)S(1)} %get-tuple-element.14.facing_inner_hbm), channel_id=1, source_target_pairs={{8,16},{24,32},{40,48},{56,64},{72,80},{88,96},{104,112},{120,128}... | collective-permute-start | bytes 2359304 | tf_op jit(solution)/shard_map/ppermute | solution.py:594
  19.2 0.0 collective-permute-done.4
  19.3 0.1 collective-permute-start.5
  19.4 0.1 add_multiply_fusion
  19.5 1.4 %collective-permute-done.5.strip_inner_ref = f32[27,16,128]{2,1,0:T(8,128)S(1)} collective-permute-done((f32[27,16,128]{2,1,0:T(8,128)S(1)}, f32[27,16,128]{2,1,0:T(8,128)S(1)}, u32[]{:S(2)}, u32[]{:S(2)}) %collective-permute-start.5) | collective-permute-done | bytes 221216 | tf_op jit(solution)/shard_map/ppermute | solution.py:594
  20.9 0.0 copy-start.1
  20.9 0.7 copy-done.1
  21.5 3.2 %collective-permute-start.6 = (f32[27,16,128]{2,1,0:T(8,128)S(1)}, f32[27,16,128]{2,1,0:T(8,128)}, u32[]{:S(2)}, u32[]{:S(2)}) collective-permute-start(f32[27,16,128]{2,1,0:T(8,128)S(1)} %pad_maximum_fusion.strip_ref), channel_id=1, source_target_pairs={{8,16},{24,32},{40,48},{56,64},{72,80},{88,96},{104,112},{120,128}... | collective-permute-start | bytes 663560 | tf_op jit(solution)/shard_map/ppermute | solution.py:594
  24.7 0.1 fusion.6
  24.8 31.4 %collective-permute-done.6.strip_outer_ref = f32[27,16,128]{2,1,0:T(8,128)} collective-permute-done((f32[27,16,128]{2,1,0:T(8,128)S(1)}, f32[27,16,128]{2,1,0:T(8,128)}, u32[]{:S(2)}, u32[]{:S(2)}) %collective-permute-start.6) | collective-permute-done | bytes 221216 | tf_op jit(solution)/shard_map/ppermute | solution.py:594
  56.3 0.0 collective-permute-done.1.inner_hbm
  56.3 0.0 collective-permute-done.2.outer_hbm
  56.3 0.1 broadcast_in_dim.37.weight_ref
  56.4 0.0 copy-start.2
  56.4 0.9 copy-done.2
  57.3 23.4 %near.1 = (f32[12,16,16,256]{3,2,1,0:T(8,128)S(1)}, f32[24,16,256]{2,1,0:T(8,128)S(1)}, f32[24,16,256]{2,1,0:T(8,128)S(1)}, f32[8,2,16,384]{3,2,1,0:T(8,128)S(1)}, f32[8,2,2,16,256]{4,3,2,1,0:T(8,128)S(1)}) custom-call(f32[12,4,16,256]{3,2,1,0:T(8,128)} %collective-permute-done.1.inner_hbm, f32[12,4,16,256]{3,2,1,0:T(8,128)S(1)} %get-tuple-element.14.facing_inner_hbm, ...), custom_call_target="tpu_custom_call" | custom-call | flops 283115520 | bytes 8388608 | tf_op jit(solution)/shard_map/near/pallas_call | solution.py:635
  80.8 0.0 collective-permute-done.inner_hbm
  80.8 0.0 collective-permute-done.7.outer_hbm
  80.8 14.0 %far.1 = f32[12,8,16,256]{3,2,1,0:T(8,128)} custom-call(f32[12,4,16,256]{3,2,1,0:T(8,128)S(1)} %collective-permute-done.inner_hbm, f32[12,16,16,256]{3,2,1,0:T(8,128)S(1)} %get-tuple-element.16.main_hbm, f32[12,4,16,256]{3,2,1,0:T(8,128)S(1)} %collective-permute-done.7.outer_hbm, f32[24,16,256]{2,1,0:T(8,128)S(1)} %get-tuple-element.17.inside, ...), custom_call_target="tpu_custom_call" | custom-call | flops 188743680 | bytes 8388608 | tf_op jit(solution)/shard_map/far/pallas_call | solution.py:670
  (11 shorter events, 0.2 us)
Async XLA Ops:
  0.0 12.4 %copy-start.3 = (f32[2,8]{1,0:T(2,128)S(1)}, f32[2,8]{1,0:T(2,128)}, u32[]{:S(2)}) copy-start(f32[2,8]{1,0:T(2,128)} %param.7) | copy-start | bytes 196
  0.0 12.4 %copy-start.4 = (s32[16]{0:T(128)S(1)}, s32[16]{0:T(128)}, u32[]{:S(2)}) copy-start(s32[16]{0:T(128)} %param.6) | copy-start | bytes 196
  0.9 1.4 %copy-start = (f32[12,8,16,256]{3,2,1,0:T(8,128)S(1)}, f32[12,8,16,256]{3,2,1,0:T(8,128)}, u32[]{:S(2)}) copy-start(f32[12,8,16,256]{3,2,1,0:T(8,128)} %state_hbm.1) | copy-start | bytes 4718596
  4.6 8.0 %collective-permute-start.3 = (f32[13,16,128]{2,1,0:T(8,128)S(1)}, f32[13,16,128]{2,1,0:T(8,128)S(1)}, u32[]{:S(2)}, u32[]{:S(2)}) collective-permute-start(f32[13,16,128]{2,1,0:T(8,128)S(1)} %get-tuple-element.15), channel_id=1, source_target_pairs={{0,1},{2,3},{4,5},{6,7},{1,0},{3,2},{5,4},{7,6},{8,9},{10,11},{12,... | collective-permute-start | bytes 319496 | tf_op jit(solution)/shard_map/ppermute | solution.py:594
  5.7 13.5 %collective-permute-start.4 = (f32[13,16,128]{2,1,0:T(8,128)S(1)}, f32[13,16,128]{2,1,0:T(8,128)S(1)}, u32[]{:S(2)}, u32[]{:S(2)}) collective-permute-start(f32[13,16,128]{2,1,0:T(8,128)S(1)} %get-tuple-element.15), channel_id=1, source_target_pairs={{1,2},{3,4},{5,6},{2,1},{4,3},{6,5},{9,10},{11,12},{13,14},{10,9},... | collective-permute-start | bytes 319496 | tf_op jit(solution)/shard_map/ppermute | solution.py:594
  8.6 47.7 %collective-permute-start.2 = (f32[12,4,16,256]{3,2,1,0:T(8,128)S(1)}, f32[12,4,16,256]{3,2,1,0:T(8,128)}, u32[]{:S(2)}, u32[]{:S(2)}) collective-permute-start(f32[12,4,16,256]{3,2,1,0:T(8,128)S(1)} %get-tuple-element.13.facing_outer_hbm), channel_id=1, source_target_pairs={{8,16},{24,32},{40,48},{56,64},{72,80},{88,96},{104,112},{120,128}... | collective-permute-start | bytes 2359304 | tf_op jit(solution)/shard_map/ppermute | solution.py:594
  11.7 69.1 %collective-permute-start = (f32[12,4,16,256]{3,2,1,0:T(8,128)S(1)}, f32[12,4,16,256]{3,2,1,0:T(8,128)S(1)}, u32[]{:S(2)}, u32[]{:S(2)}) collective-permute-start(f32[12,4,16,256]{3,2,1,0:T(8,128)S(1)} %get-tuple-element.13.facing_outer_hbm), channel_id=1, source_target_pairs={{0,8},{16,24},{32,40},{48,56},{64,72},{80,88},{96,104},{112,120},{... | collective-permute-start | bytes 2359304 | tf_op jit(solution)/shard_map/ppermute | solution.py:594
  12.3 44.0 %collective-permute-start.1 = (f32[12,4,16,256]{3,2,1,0:T(8,128)S(1)}, f32[12,4,16,256]{3,2,1,0:T(8,128)}, u32[]{:S(2)}, u32[]{:S(2)}) collective-permute-start(f32[12,4,16,256]{3,2,1,0:T(8,128)S(1)} %get-tuple-element.14.facing_inner_hbm), channel_id=1, source_target_pairs={{0,8},{16,24},{32,40},{48,56},{64,72},{80,88},{96,104},{112,120},{... | collective-permute-start | bytes 2359304 | tf_op jit(solution)/shard_map/ppermute | solution.py:594
  12.6 68.1 %collective-permute-start.7 = (f32[12,4,16,256]{3,2,1,0:T(8,128)S(1)}, f32[12,4,16,256]{3,2,1,0:T(8,128)S(1)}, u32[]{:S(2)}, u32[]{:S(2)}) collective-permute-start(f32[12,4,16,256]{3,2,1,0:T(8,128)S(1)} %get-tuple-element.14.facing_inner_hbm), channel_id=1, source_target_pairs={{8,16},{24,32},{40,48},{56,64},{72,80},{88,96},{104,112},{120,128}... | collective-permute-start | bytes 2359304 | tf_op jit(solution)/shard_map/ppermute | solution.py:594
  19.3 1.6 %collective-permute-start.5 = (f32[27,16,128]{2,1,0:T(8,128)S(1)}, f32[27,16,128]{2,1,0:T(8,128)S(1)}, u32[]{:S(2)}, u32[]{:S(2)}) collective-permute-start(f32[27,16,128]{2,1,0:T(8,128)S(1)} %pad_maximum_fusion.strip_ref), channel_id=1, source_target_pairs={{0,8},{16,24},{32,40},{48,56},{64,72},{80,88},{96,104},{112,120},{... | collective-permute-start | bytes 663560 | tf_op jit(solution)/shard_map/ppermute | solution.py:594
  20.9 0.7 copy-start.1
  21.5 34.7 %collective-permute-start.6 = (f32[27,16,128]{2,1,0:T(8,128)S(1)}, f32[27,16,128]{2,1,0:T(8,128)}, u32[]{:S(2)}, u32[]{:S(2)}) collective-permute-start(f32[27,16,128]{2,1,0:T(8,128)S(1)} %pad_maximum_fusion.strip_ref), channel_id=1, source_target_pairs={{8,16},{24,32},{40,48},{56,64},{72,80},{88,96},{104,112},{120,128}... | collective-permute-start | bytes 663560 | tf_op jit(solution)/shard_map/ppermute | solution.py:594
  56.4 0.9 copy-start.2

commit v4 on v3

v4 whole, which is shorter than its diff:
```python
import functools
import math

import jax
import jax.numpy as jnp
from jax import lax
from jax.experimental import pallas as pl
from jax.experimental.pallas import tpu as pltpu
from jax.sharding import PartitionSpec as P


STEPS = 8
COMPS = 12
CHUNKS = (4, 4)
PLANE = 8
EDGE = 8
GROUP = 2 * EDGE
LANES = 128

time_step = 0.02
thermal_volt = 8314.472 * 310.0 / 96485.3415
potassium_out = 5.4
sodium_out = 140.0
calcium_out = 2.0
potassium_in = 138.3
sodium_in = 7.67
transverse = 0.04
longitudinal = 0.12
LOG2E = math.log2(math.e)


def react(state):
    (x, act, inact, slow, calact, calinact, tract, trinact, rapact, rapinact, slowact, calcium) = state

    def power(rate, offset=0.0, scale=1.0):
        shift = offset * LOG2E + math.log2(scale)
        scaled = x * (100.0 * rate * LOG2E)
        return jnp.exp2(scaled + shift if shift else scaled)

    def bell(centre, width, scale):
        root = math.sqrt(LOG2E / width)
        away = x * (100.0 * root) + centre * root
        return jnp.exp2(math.log2(scale) - away * away)

    def step(rate, offset):
        return jax.nn.sigmoid(x * (100.0 * rate) + offset)

    def inverse(value):
        return 1.0 / value

    def moved(gate, steady, exponent):
        return steady + (gate - steady) * jnp.exp2(exponent)

    e = math.exp
    speed = time_step * LOG2E
    voltage = 100.0 * x
    rev_potassium = thermal_volt * math.log(potassium_out / potassium_in)
    rev_sodium = thermal_volt * math.log(sodium_out / sodium_in)
    rev_slow = thermal_volt * math.log(
        (potassium_out + 0.03 * sodium_out) / (potassium_in + 0.03 * sodium_in)
    )
    up20 = power(1 / 20)
    up10 = up20 * up20
    up5 = up10 * up10
    down20 = power(-1 / 20)
    down10 = down20 * down20
    down5 = down10 * down10
    up15 = power(1 / 15)
    down6 = power(-1 / 6)
    down14 = power(-1 / 14)
    down7 = down14 * down14
    fall = jnp.exp2(jnp.minimum(x * (-50.0 * LOG2E) - 20.0 * LOG2E, 120.0))
    minus_upper = inverse(-1.0 - fall)
    minus_lower = fall * minus_upper

    above = voltage - rev_potassium
    cam = jnp.maximum(calcium, 0.02)
    past_calcium = (voltage - 0.5 * thermal_volt * math.log(calcium_out / 0.001)) + (
        0.5 * thermal_volt
    ) * jnp.log(cam)
    past_sodium = voltage - rev_sodium
    inward_x = 1.0 + power(0.06, -0.06 * (rev_potassium + 200.0))
    inward_y = 1.0 + fall * e(20.0 + 0.5 * rev_potassium)
    inward_b = power(0.0002, 0.0002 * (100.0 - rev_potassium), 30.0) + up10 * (
        10.0 * e(-0.1 * rev_potassium - 1.0)
    )
    inward = (5.405 * inward_y) * inverse(inward_y + inward_b * inward_x)
    plateau = inverse(1.0 / 0.0146 + power(-1 / 5.98, 25.0 / 5.98, 1.0 / 0.0146))
    full = power(-1.0 / thermal_volt)
    pump_top = 2.724 * potassium_out / (potassium_out + 1.0) * sodium_in / (sodium_in + 40.0)
    pump = inverse(
        (power(-0.1 / thermal_volt, 0.0, 0.1245 / pump_top) + 1.0 / pump_top)
        + full * (0.0353 / pump_top)
    )
    whole = 1000.0 / ((87.5**3 + sodium_out**3) * (1.38 + calcium_out))
    inner = whole * sodium_in**3 * calcium_out
    exchange = (inner - (cam * (2.5 * 0.001 * whole * sodium_out**3)) * full) * inverse(
        power(-0.35 / thermal_volt) + 0.1 * full
    )
    pump_calcium = 0.1238 - 0.0619 * inverse(cam + 0.5)
    calcium_sum = (0.08 * calact * calinact + 0.000592) * past_calcium + pump_calcium
    ionic = (
        (14.838 * act * (act * act) * inact * slow + 0.00029) * past_sodium
        + calcium_sum
        + (0.294 * tract * trinact + 0.153 * rapact * rapinact + inward + plateau) * above
        + (0.392 * slowact * slowact) * (voltage - rev_slow)
        + pump
        + exchange
    )
    new_x = x - (time_step / 100.0) * ionic
    new_calcium = calcium - (time_step * 0.05) * (calcium_sum - 2.0 * exchange)

    a = up5 * (e(7.0))
    b = power(1 / 200, -0.25)
    root = step(1 / 9.03, 56.86 / 9.03)
    rate = ((a * (-10.0 * speed) - (1.0 + e(-5.0)) * 10.0 * speed) - down5 * (e(-12.0) * 10.0 * speed)) * (
        (1.0 + b) * inverse(2.0 + a + b)
    )
    new_act = moved(act, root * root, rate)

    root = step(-1 / 7.43, -71.55 / 7.43)
    steady = root * root
    rate = minus_lower * (
        power(-1 / 6.8, -80.0 / 6.8, 0.057 * speed)
        + power(0.079, 0.0, 2.7 * speed)
        + power(0.3485, 0.0, 310000.0 * speed)
    ) + minus_upper * inverse(
        1.0 / (0.77 / 0.13 * speed) + power(-1 / 11.1, -10.66 / 11.1, 1.0 / (0.77 / 0.13 * speed))
    )
    new_inact = moved(inact, steady, rate)
    rate = minus_lower * (
        power(-0.01052, 0.0, 0.02424 * speed) * step(0.1378, 0.1378 * 40.14)
        - (power(0.2444, 0.0, 25428.0 * speed) + power(-0.04391, 0.0, 6.948e-06 * speed))
        * ((voltage + 37.78) * step(-0.311, -0.311 * 79.23))
    ) + minus_upper * (
        power(0.057) * inverse(1.0 / (0.6 * speed) + down10 * (e(-3.2) / (0.6 * speed)))
    )
    new_slow = moved(slow, steady, rate)

    p = 1.0 + power(-1 / 13, -35.0 / 13)
    r = down20 * (-speed * e(2.5)) - speed
    pq = p * (1.0 + up5 * e(1.0))
    rate = pq * (r * inverse((-1.96 / speed - (0.35 / speed) * p) * r + pq))
    new_calact = moved(calact, step(1 / 7.5, 8.0 / 7.5), rate)

    b = up10 * (-speed * e(3.0))
    den = (down10 * (-speed * e(1.3)) - speed * (1.0 + e(4.3))) + b
    rate = den * inverse(
        (380.0 - 180.0 * (1.0 + e(4.3)) - (20.0 / speed) * b)
        - (bell(27.0, 225.0, 1102.5 / speed) + 200.0 / speed) * den
    )
    new_calinact = moved(calinact, down7 * inverse(down7 + e(20.0 / 7)), rate)

    rate = inverse(-0.8 / speed - bell(40.0, 1800.0, 9.5 / speed))
    new_tract = moved(tract, inverse(1.0 + down6 * e(20.0 / 6)), rate)

    t = up5 * (-speed * e(-4.0)) - speed
    rate = t * inverse(5.0 - (bell(45.0, 320.0, 85.0 / speed) + 3.0 / speed) * t)
    new_trinact = moved(trinact, inverse(1.0 + up5 * e(4.0)), rate)

    rate = (down10 * (-speed * e(-4.5) / 2700.0) - speed / 2700.0) * (
        1.0 + power(1 / 11.5, 30.0 / 11.5)
    )
    new_rapact = moved(rapact, inverse(1.0 + down7 * e(-26.0 / 7)), rate)

    rate = (up20 + down20) * (-speed * e(-3.0) / 3.36) - speed * (1.0 + e(-6.0)) / 3.36
    new_rapinact = moved(rapinact, step(-1 / 24, -88.0 / 24), rate)

    y = up15 * (-speed * e(-35.0 / 15)) - speed
    rate = y * inverse(
        lax.rsqrt(1.0 / 1400.0**2 + down6 * (e(5.0 / 6) / 1400.0**2)) - (80.0 / speed) * y
    )
    new_slowact = moved(slowact, inverse(1.0 + down14 * e(-5.0 / 14)), rate)
    return (
        new_x,
        new_act,
        new_inact,
        new_slow,
        new_calact,
        new_calinact,
        new_tract,
        new_trinact,
        new_rapact,
        new_rapinact,
        new_slowact,
        new_calcium,
    )


def layer_tensor(layer_index, fibre):
    angle_in = fibre[0]
    angle_out = fibre[1]
    fibre_x = jnp.cos(angle_in) * jnp.cos(angle_out)
    fibre_y = jnp.sin(angle_in) * jnp.cos(angle_out)
    fibre_z = jnp.sin(angle_out)
    spread = longitudinal - transverse
    tensor_table = jnp.stack(
        [
            transverse + spread * fibre_x * fibre_x,
            transverse + spread * fibre_y * fibre_y,
            transverse + spread * fibre_z * fibre_z,
            spread * fibre_x * fibre_y,
            spread * fibre_x * fibre_z,
            spread * fibre_y * fibre_z,
        ]
    )
    layer_ids = jnp.arange(fibre.shape[1], dtype=jnp.int32)
    chosen = layer_index[:, None] == layer_ids[None, :]
    return jnp.sum(jnp.where(chosen[None], tensor_table[:, None, :], jnp.float32(0.0)), axis=2)


def level_weights(tensor, lanes):
    between = (tensor[:, 1:] + tensor[:, :-1]) / 2.0
    upward = jnp.pad(between, ((0, 0), (0, 1)))
    downward = jnp.pad(between, ((0, 0), (1, 0)))
    rows = jnp.stack(
        [
            tensor[0],
            tensor[1],
            tensor[3] / 2.0,
            upward[2],
            upward[4] / 2.0,
            upward[5] / 2.0,
            downward[2],
            downward[4] / 2.0,
            downward[5] / 2.0,
        ]
    )
    return jnp.broadcast_to(rows[:, :, None], rows.shape + (lanes,))


def first_kernel(chunks, state_ref, mask_ref, *refs):
    faces, (edge_ref, main, inside, sems) = refs[: 2 * len(chunks)], refs[2 * len(chunks) :]
    cells, depth, width = state_ref.shape[1:]
    odd = lax.rem(lax.axis_index("gx"), 2)
    lane = lax.broadcasted_iota(jnp.int32, (depth, LANES), 1)
    diagonal = lax.broadcasted_iota(jnp.int32, (depth, depth), 0) == lax.broadcasted_iota(
        jnp.int32, (depth, depth), 1
    )
    codes = jnp.zeros((depth, LANES), jnp.float32)
    for x in range(cells):
        for b in range(width // LANES):
            code = jnp.where(mask_ref[x, b : b + 1, :] > 0, jnp.float32(1.0), jnp.float32(0.0))
            code = jnp.where(diagonal, jnp.broadcast_to(code, (depth, depth)), jnp.float32(0.0))
            code = jnp.broadcast_to(jnp.sum(code, axis=1, keepdims=True), (depth, LANES))
            inside[x, :, pl.ds(b * LANES, LANES)] = code
            codes = jnp.where(lane == 2 * x + b, code, codes)
    edge_ref[COMPS + 1] = codes

    def react_pair(k, carry):
        for x in (2 * k, 2 * k + 1):
            for level in range(depth // 8):
                for i in range(width // LANES):
                    place = (x, pl.ds(level * 8, 8), pl.ds(i * LANES, LANES))
                    old = [state_ref[(c,) + place] for c in range(COMPS)]
                    live = inside[place] > 0.5
                    for c, new in enumerate(react(old)):
                        main[(c,) + place] = jnp.where(live, new, old[c])
        return carry

    lax.fori_loop(0, cells // 2, react_pair, 0)
    copies = []
    start = 0
    for i, rows in enumerate(chunks):
        above, below = cells - start - rows, start
        inner = above + odd * (below - above)
        outer = below + odd * (above - below)
        for face, row, sem in ((faces[2 * i], inner, 2 * i), (faces[2 * i + 1], outer, 2 * i + 1)):
            copies.append(pltpu.make_async_copy(main.at[:, pl.ds(row, rows)], face, sems.at[sem]))
        start += rows
    for copy in copies:
        copy.start()

    def packed(first, last):
        total = jnp.zeros((depth, LANES), jnp.float32)
        for i in range(cells):
            joined = jnp.where(lane < EDGE, first(i), last(i))
            turned = pltpu.roll(joined, i * GROUP + EDGE, 1)
            total = jnp.where(lane // GROUP == i, turned, total)
        return total

    def some(k, carry):
        for q in range(3):
            c = 3 * k + q
            edge_ref[c] = packed(
                lambda i: main[c, i, :, :LANES], lambda i: main[c, i, :, width - LANES :]
            )
        return carry

    lax.fori_loop(0, COMPS // 3, some, 0)
    edge_ref[COMPS] = packed(
        lambda i: inside[i, :, :LANES], lambda i: inside[i, :, width - LANES :]
    )
    for copy in copies:
        copy.wait()


def react_tile(at, live):
    new = react([at(c)[...] for c in range(COMPS)])
    for c in range(COMPS):
        pltpu.store(at(c), new[c], mask=live > 0.5)
    return live * new[0]


def react_rows(main, inside, pot, rows):
    for x in rows:
        for level in range(main.shape[2] // 8):
            for i in range(main.shape[3] // LANES):
                place = (x, pl.ds(level * 8, 8), pl.ds(i * LANES, LANES))
                held = react_tile(lambda c: main.at[(c,) + place], inside[place])
                if pot is not None:
                    pot[place] = held


def shift_row(pot, dy_ref, sy_ref, x, ext, strip_row):
    shape = (pot.shape[1], LANES)
    lane = lax.broadcasted_iota(jnp.int32, shape, 1)
    first_lane, last_lane = lane == 0, lane == LANES - 1
    block = pl.ds(pl.multiple_of(ext // 8 * LANES, LANES), LANES)
    place = lax.rem(ext, 8) * GROUP
    before = pltpu.roll(strip_row(0, block), lax.rem(2 * LANES - place - (EDGE - 1), LANES), 1)
    after = pltpu.roll(strip_row(1, block), lax.rem(2 * LANES - 1 - place - EDGE, LANES), 1)
    near, far = pot[x, :, :LANES], pot[x, :, LANES:]
    near_up, far_up = pltpu.roll(near, 1, 1), pltpu.roll(far, 1, 1)
    near_down, far_down = pltpu.roll(near, LANES - 1, 1), pltpu.roll(far, LANES - 1, 1)
    lower = jnp.where(first_lane, before, near_up)
    upper = jnp.where(last_lane, far_down, near_down)
    dy_ref[x, :, :LANES] = upper - lower
    sy_ref[x, :, :LANES] = upper + lower
    lower = jnp.where(first_lane, near_up, far_up)
    upper = jnp.where(last_lane, after, far_down)
    dy_ref[x, :, LANES:] = upper - lower
    sy_ref[x, :, LANES:] = upper + lower


def spread(weight_ref, p, dx, sx, dy, sy, cross):
    depth, lanes = p.shape
    w = [weight_ref[i, :, :lanes] for i in range(9)]
    rising = w[3] * p - w[4] * dx - w[5] * dy
    falling = w[6] * p + w[7] * dx + w[8] * dy
    return (
        w[0] * sx
        + w[1] * sy
        + w[2] * cross
        + pltpu.roll(rising, 1, 0)
        + pltpu.roll(falling, depth - 1, 0)
    )


def row_spread(weight_ref, pot, dy_ref, sy_ref, x):
    before, after = pot[x - 1], pot[x + 1]
    return spread(
        weight_ref,
        pot[x],
        after - before,
        after + before,
        dy_ref[x],
        sy_ref[x],
        dy_ref[x + 1] - dy_ref[x - 1],
    )


def strip_spread(weight_ref, p):
    long = p.shape[1]
    lower, upper = pltpu.roll(p, 1, 1), pltpu.roll(p, long - 1, 1)
    before, after = pltpu.roll(p, GROUP, 1), pltpu.roll(p, long - GROUP, 1)
    dy = upper - lower
    cross = pltpu.roll(dy, long - GROUP, 1) - pltpu.roll(dy, GROUP, 1)
    return spread(weight_ref, p, after - before, after + before, dy, upper + lower, cross)


def strip_kernel(
    strip_inner_hbm,
    strip_hbm,
    strip_outer_hbm,
    weight_ref,
    inside,
    total,
    strip_track,
    dy_ref,
    sy_ref,
    strip,
    code_ref,
    strip_total,
    sems,
):
    span, depth, width = inside.shape
    cells = span // 3
    odd = lax.rem(lax.axis_index("gx"), 2)
    sides = (0, 1)
    copies = []
    for q, (i, source) in enumerate(
        ((2 - 2 * odd, strip_inner_hbm), (1, strip_hbm), (2 * odd, strip_outer_hbm))
    ):
        part = pl.ds(pl.multiple_of(i * LANES, LANES), LANES)
        for side in sides:
            held = source.at[pl.ds(side * (COMPS + 1), COMPS + 1)]
            copies.append(
                pltpu.make_async_copy(held, strip.at[side, :, :, part], sems.at[3 * q + side])
            )
        copies.append(
            pltpu.make_async_copy(
                source.at[pl.ds(2 * (COMPS + 1), 1)], code_ref.at[pl.ds(i, 1)], sems.at[3 * q + 2]
            )
        )
    for copy in copies:
        copy.start()
    for copy in copies:
        copy.wait()
    for i in range(3):
        codes = code_ref[i]
        for x in range(cells):
            for b in range(width // LANES):
                value = jnp.broadcast_to(codes[:, 2 * x + b : 2 * x + b + 1], (depth, LANES))
                inside[i * cells + x, :, b * LANES : (b + 1) * LANES] = value

    def shift_mask(k, carry):
        for q in range(4):
            x = 4 * k + q
            shift_row(inside, dy_ref, sy_ref, x, x, lambda side, block: strip[side, COMPS, :, block])
        return carry

    lax.fori_loop(0, span // 4, shift_mask, 0)

    def total_rows(k, carry):
        for q in range(2):
            x = 1 + 2 * k + q
            total[x] = row_spread(weight_ref, inside, dy_ref, sy_ref, x)
        return carry

    lax.fori_loop(0, span // 2 - 1, total_rows, 0)
    for side in sides:
        strip_total[side] = strip_spread(weight_ref, strip[side, COMPS])
        strip_track[0, side] = strip[side, COMPS] * strip[side, 0]

    def step(s, carry):
        for side in sides:
            u = strip[side, 0]
            flow = strip_spread(weight_ref, strip_track[s, side]) - u * strip_total[side]
            strip[side, 0] = u + strip[side, COMPS] * flow

        for side in sides:
            for level in range(depth // 8):
                for i in range(3):
                    place = (pl.ds(level * 8, 8), pl.ds(i * LANES, LANES))
                    held = react_tile(
                        lambda c: strip.at[(side, c) + place], strip[(side, COMPS) + place]
                    )
                    strip_track[(s + 1, side) + place] = held
        return carry

    lax.fori_loop(0, STEPS - 1, step, 0)


def finished(main, main_out, sems, s, wait):
    count = main.shape[1]
    for q, row in enumerate((s, count - 1 - s)):
        copy = pltpu.make_async_copy(
            main.at[:, pl.ds(row, 1)], main_out.at[:, pl.ds(row, 1)], sems.at[2 * s + q]
        )
        if wait:
            copy.wait()
        else:
            copy.start()


def near_kernel(pieces, near, *refs):
    sources, refs = refs[: pieces + 2], refs[pieces + 2 :]
    inside, total, strip_track, weight_ref, main_out, track = refs[:6]
    main, pot, dy_ref, sy_ref, sems, out_sems = refs[6:]
    count, _, _ = pot.shape
    cells = count - 2 * near
    skip = cells - near
    odd = lax.rem(lax.axis_index("gx"), 2)
    inner_hbm, outer_hbm = sources[:2]
    places = [(near + cells - odd * (near + cells), inner_hbm), (odd * (near + cells), outer_hbm)]
    start = 0
    for source in sources[2:]:
        rows = source.shape[1]
        above, below = cells - start - rows, start
        places.append((near + above + odd * (below - above), source))
        start += rows
    copies = [
        pltpu.make_async_copy(source, main.at[:, pl.ds(row, source.shape[1])], sems.at[i])
        for i, (row, source) in enumerate(places)
    ]
    for copy in copies:
        copy.start()
    for copy in copies:
        copy.wait()

    group = 4 if count % 4 == 0 else 2

    def start_row(k, carry):
        for q in range(2):
            pot[2 * k + q] = inside[skip + 2 * k + q] * main[0, 2 * k + q]
        return carry

    lax.fori_loop(0, count // 2, start_row, 0)

    def step(s, carry):
        def shift_some(k, carry):
            for q in range(group):
                x = group * k + q
                shift_row(
                    pot, dy_ref, sy_ref, x, skip + x, lambda side, block: strip_track[s, side, :, block]
                )
            return carry

        lax.fori_loop(s // group, (count - 1 - s) // group + 1, shift_some, 0)
        for q, row in enumerate((s + 1, count - 2 - s)):
            track[s, q, 0] = pot[row]
            track[s, q, 1] = dy_ref[row]

        def diffuse_some(size, start, k, carry):
            for q in range(size):
                x = start + size * k + q
                u = main[0, x]
                flow = row_spread(weight_ref, pot, dy_ref, sy_ref, x) - u * total[skip + x]
                main[0, x] = u + inside[skip + x] * flow
            return carry

        pairs = jnp.maximum(count // 2 - 1 - s, 0)
        lax.fori_loop(0, pairs // 2, functools.partial(diffuse_some, 4, s + 1), 0)
        rest = s + 1 + pairs // 2 * 4
        lax.fori_loop(0, lax.rem(pairs, 2), functools.partial(diffuse_some, 2, rest), 0)

        @pl.when(s < min(STEPS, count // 2))
        def _():
            finished(main, main_out, out_sems, s, False)

        def react_some(k, carry):
            x = s + 1 + 2 * k
            react_rows(main, inside.at[pl.ds(skip, count)], pot, (x, x + 1))
            return carry

        lax.fori_loop(0, jnp.where(s < STEPS - 1, count // 2 - 1 - s, 0), react_some, 0)
        return carry

    lax.fori_loop(0, STEPS, step, 0)

    def drained(s, carry):
        finished(main, main_out, out_sems, s, True)
        return carry

    lax.fori_loop(0, min(STEPS, count // 2), drained, 0)


def ring_kernel(last, *refs):
    inner_hbm, main_hbm, outer_hbm, relay_hbm = refs[:4]
    inside, total, strip_track, track, weight_ref = refs[4:9]
    if last:
        out_hbm, main, pot, dy_ref, sy_ref, sems = refs[9:]
    else:
        main_out, track_out, main, pot, dy_ref, sy_ref, sems, out_sems = refs[9:]
    far, _, _ = inner_hbm.shape[1:]
    count = main_hbm.shape[1]
    span = far + count + far
    cells = inside.shape[0] // 3
    skip = (inside.shape[0] - span) // 2
    before = (count - cells) // 2
    odd = lax.rem(lax.axis_index("gx"), 2)
    across = lax.rem(lax.axis_index("gx") + 1, PLANE)
    relayed = jnp.logical_or(across == 0, across == 1)
    inner_place, outer_place = far + count - odd * (far + count), odd * (far + count)
    copies = [
        pltpu.make_async_copy(source, main.at[:, pl.ds(row, source.shape[1])], sems.at[i])
        for i, (row, source) in enumerate(
            (
                (inner_place, inner_hbm),
                (far, main_hbm),
                (outer_place, relay_hbm),
                (outer_place, outer_hbm),
            )
        )
    ]
    copies[0].start()
    copies[1].start()

    @pl.when(relayed)
    def _():
        copies[2].start()
        copies[2].wait()

    @pl.when(jnp.logical_not(relayed))
    def _():
        copies[3].start()
        copies[3].wait()

    copies[0].wait()
    copies[1].wait()
    for q in range(far):
        for x in (q, span - 1 - q):
            pot[x] = inside[skip + x] * main[0, x]

    def step(s, carry):
        for row in (s + far, span - 1 - far - s):
            pot[row] = inside[skip + row] * main[0, row]
        for first in (s, span - 1 - far - s):
            for q in range(far + 1):
                x = first + q
                shift_row(
                    pot, dy_ref, sy_ref, x, skip + x, lambda side, block: strip_track[s, side, :, block]
                )

        def known():
            for q, row in enumerate((s + far + 1, span - 2 - far - s)):
                pot[row] = track[s, q, 0]
                dy_ref[row] = track[s, q, 1]

        if before < cells // 2:
            pl.when(s < cells // 2 + before)(known)
        else:
            known()
        if not last:
            for q, row in enumerate((s + 1, span - 2 - s)):
                track_out[s, q, 0] = pot[row]
                track_out[s, q, 1] = dy_ref[row]

        def diffuse(x):
            u = main[0, x]
            flow = row_spread(weight_ref, pot, dy_ref, sy_ref, x) - u * total[skip + x]
            main[0, x] = u + inside[skip + x] * flow

        for side, first in enumerate((s + 1, span - 1 - far - s)):
            for q in range(far):
                x = first + q
                if before < cells // 2 and q == (far - 1, 0)[side]:
                    pl.when((x < span // 2, x >= span // 2)[side])(functools.partial(diffuse, x))
                else:
                    diffuse(x)
        if not last:
            finished(main, main_out, out_sems, s, False)

        def react_pair(k, carry):
            near_row, far_row = s + 1 + k, span - 2 - s - k
            react_rows(main, inside.at[pl.ds(skip, span)], pot, (near_row, far_row))
            return carry

        lax.fori_loop(0, jnp.where(s < STEPS - 1, far, 0), react_pair, 0)
        return carry

    lax.fori_loop(0, STEPS, step, 0)
    if last:
        copies = [pltpu.make_async_copy(main.at[:, pl.ds(cells, cells)], out_hbm, sems.at[0])]
    else:
        rest = span - 2 * STEPS
        copies = [
            pltpu.make_async_copy(
                main.at[:, pl.ds(STEPS, rest)], main_out.at[:, pl.ds(STEPS, rest)], sems.at[0]
            )
        ] * (rest > 0)
    for copy in copies:
        copy.start()
    for copy in copies:
        copy.wait()
    if not last:

        def drained(s, carry):
            finished(main, main_out, out_sems, s, True)
            return carry

        lax.fori_loop(0, STEPS, drained, 0)


def shards(state, tissue_mask, layer_index, fibre):
    comps, cells, depth, width = state.shape
    across, along = lax.axis_size("gx"), lax.axis_size("gy")
    span = 3 * cells
    f32 = jnp.float32

    def swaps(size, first):
        pairs = [(i, i + 1) for i in range(first, size - 1, 2)]
        return pairs + [(j, i) for i, j in pairs]

    def both(inner, outer, axis, size):
        outer = lax.ppermute(outer, axis, swaps(size, 1))
        return lax.ppermute(inner, axis, swaps(size, 0)), outer

    def shape(*sizes):
        return jax.ShapeDtypeStruct(sizes, f32)

    vmem = pl.BlockSpec(memory_space=pltpu.VMEM)
    hbm = pl.BlockSpec(memory_space=pl.ANY)
    params = pltpu.CompilerParams(vmem_limit_bytes=12 << 20)

    def cost(rows):
        work = int(rows * depth * width * 350)
        return pl.CostEstimate(flops=work, bytes_accessed=8 << 20, transcendentals=0)

    *faces, edge = pl.pallas_call(
        functools.partial(first_kernel, CHUNKS),
        out_shape=[shape(comps, rows, depth, width) for rows in CHUNKS for _ in range(2)]
        + [shape(comps + 2, depth, LANES)],
        in_specs=[vmem, vmem],
        out_specs=[hbm] * (2 * len(CHUNKS)) + [vmem],
        scratch_shapes=[
            pltpu.VMEM((comps, cells, depth, width), f32),
            pltpu.VMEM((cells, depth, width), f32),
            pltpu.SemaphoreType.DMA((2 * len(CHUNKS),)),
        ],
        compiler_params=params,
        name="first",
    )(state, tissue_mask.transpose(0, 2, 1))
    inner_faces, outer_faces = faces[0::2], faces[1::2]
    edge_inner, edge_outer = both(edge, edge, "gy", along)
    odd_along = lax.rem(lax.axis_index("gy"), 2) == 1
    edge_before = jnp.where(odd_along, edge_inner, edge_outer)
    edge_after = jnp.where(odd_along, edge_outer, edge_inner)
    outer = lax.broadcasted_iota(jnp.int32, edge.shape, 2) % GROUP < EDGE
    strips = jnp.concatenate(
        [
            jnp.where(outer, edge_before, edge)[:-1],
            jnp.where(outer, edge, edge_after)[:-1],
            edge[-1:],
        ]
    )
    strip_inner, strip_outer = both(strips, strips, "gx", across)
    halos = [both(inner_faces[0], outer_faces[0], "gx", across)]
    bounds = [i for i in range(PLANE - 1, across - 1, PLANE)]
    close = [pair for pair in swaps(across, 1) if pair[0] // PLANE == pair[1] // PLANE]
    around = [(i, i - PLANE + 1) for i in bounds] + [(i + 1, i + PLANE) for i in bounds]
    onward = [(i - PLANE + 1, i + 1) for i in bounds] + [(i + PLANE, i) for i in bounds]
    far_outer = lax.ppermute(outer_faces[1], "gx", close + around)
    far_inner = lax.ppermute(inner_faces[1], "gx", swaps(across, 0))
    far_relay = lax.ppermute(far_outer, "gx", onward)
    halos.append((far_inner, far_outer, far_relay))

    weights = level_weights(layer_tensor(layer_index, fibre), 3 * LANES)
    inside, total, strip_track = pl.pallas_call(
        strip_kernel,
        out_shape=[
            shape(span, depth, width),
            shape(span, depth, width),
            shape(STEPS, 2, depth, 3 * LANES),
        ],
        in_specs=[hbm] * 3 + [vmem],
        out_specs=[vmem] * 3,
        scratch_shapes=[
            pltpu.VMEM((span, depth, width), f32),
            pltpu.VMEM((span, depth, width), f32),
            pltpu.VMEM((2, comps + 1, depth, 3 * LANES), f32),
            pltpu.VMEM((3, depth, LANES), f32),
            pltpu.VMEM((2, depth, 3 * LANES), f32),
            pltpu.SemaphoreType.DMA((9,)),
        ],
        compiler_params=params,
        cost_estimate=cost(30),
        name="strips",
    )(strip_inner, strips, strip_outer, weights)
    shared = (inside, total, strip_track)

    def buffers(count):
        return [pltpu.VMEM((comps, count, depth, width), f32)] + [
            pltpu.VMEM((count, depth, width), f32) for _ in range(3)
        ]

    track_shape = shape(STEPS, 2, 2, depth, width)
    near = CHUNKS[0]
    count = cells + 2 * near
    main, track = pl.pallas_call(
        functools.partial(near_kernel, len(CHUNKS), near),
        out_shape=[shape(comps, count, depth, width), track_shape],
        in_specs=[hbm] * (2 + len(CHUNKS)) + [vmem] * 4,
        out_specs=[hbm, vmem],
        scratch_shapes=buffers(count)
        + [pltpu.SemaphoreType.DMA((2 + len(CHUNKS),)), pltpu.SemaphoreType.DMA((2 * STEPS,))],
        compiler_params=params,
        cost_estimate=cost(70),
        name="near",
    )(*halos[0], *inner_faces, *shared, weights)
    for i, rows in enumerate(CHUNKS[1:], 1):
        last = i == len(CHUNKS) - 1
        count += 2 * rows
        outs = [shape(*state.shape)] if last else [shape(comps, count, depth, width), track_shape]
        result = pl.pallas_call(
            functools.partial(ring_kernel, last),
            out_shape=outs,
            in_specs=[hbm] * 4 + [vmem] * 5,
            out_specs=[hbm, vmem][: len(outs)],
            scratch_shapes=buffers(count)
            + [pltpu.SemaphoreType.DMA((4,))]
            + ([] if last else [pltpu.SemaphoreType.DMA((2 * STEPS,))]),
            compiler_params=params,
            cost_estimate=cost(18 * rows),
        )(halos[i][0], main, *halos[i][1:], *shared, track, weights)
        main, track = result if not last else (result[0], None)
    return main


def solution(mesh):
    placed = (P(None, "gx", None, "gy"), P("gx", None, "gy"), P(), P())

    return jax.shard_map(
        shards, mesh=mesh, in_specs=placed, out_specs=P(None, "gx", None, "gy"), check_vma=False
    )
```

time: 95.1 us -> 97.2 us (1.022)
  the two profiles are of different devices: /device:TPU:130 before, /device:TPU:100 now
where the time goes in v4:
time: 97.2 us; the launch traced here: 96.8 us
  Pallas kernels  41.4 us (43%)
  waiting for transfers between devices  27.8 us (29%)
  starting transfers between devices  22.2 us (23%)
  local copies, waits for them, and re-layouts  3.91 us (4%)
  other arithmetic  1.28 us (1%)
    ppermute x1, waiting for transfers between devices, shards(): far_outer = lax.ppermute(outer_faces[1], 'gx', close + around)  17.6 us
    pallas_call x1, Pallas kernels, shards(): pl.pallas_call(functools.partial(near_kernel, len(CHUNKS), near), out_sha...  16.7 us
    pallas_call x1, Pallas kernels, shards(): pl.pallas_call(functools.partial(ring_kernel, last), out_shape=outs, in_s...  14.4 us
    ppermute x3, starting transfers between devices, both(): outer = lax.ppermute(outer, axis, swaps(size, 1))  10.5 us
    ppermute x3, waiting for transfers between devices, both(): outer = lax.ppermute(outer, axis, swaps(size, 1))  8.86 us
    pallas_call x1, Pallas kernels, shards(): pl.pallas_call(strip_kernel, out_shape=[shape(span, depth, width), shape(...  7.55 us
    ppermute x1, starting transfers between devices, shards(): far_outer = lax.ppermute(outer_faces[1], 'gx', close + around)  5.69 us
    ppermute x1, starting transfers between devices, shards(): far_relay = lax.ppermute(far_outer, 'gx', onward)  5.54 us
  transfers between devices with their start and end apart: 9, of which 3 were waited for; matrix products, arithmetic and copies ran while one was open for 1% of the time, Pallas kernels for 25%

profile of v4, /device:TPU:100, one launch (start us, length us, event | category | flops | bytes accessed | tf_op | source)
XLA Modules:
  0.0 96.8 jit_solution(9612582476541195427)
XLA Ops:
  0.0 0.0 copy-start.4
  0.0 0.0 copy-start.5
  0.0 0.0 copy-start
  0.0 1.4 %copy-done = f32[12,8,16,256]{3,2,1,0:T(8,128)S(1)} copy-done((f32[12,8,16,256]{3,2,1,0:T(8,128)S(1)}, f32[12,8,16,256]{3,2,1,0:T(8,128)}, u32[]{:S(2)}) %copy-start) | copy-done | bytes 1572888
  1.4 0.0 copy-start.3
  1.4 0.7 copy-done.3
  2.1 2.8 %first.1 = (f32[12,4,16,256]{3,2,1,0:T(8,128)}, f32[12,4,16,256]{3,2,1,0:T(8,128)}, f32[12,4,16,256]{3,2,1,0:T(8,128)S(1)}, f32[12,4,16,256]{3,2,1,0:T(8,128)S(1)}, f32[14,16,128]{2,1,0:T(8,128)S(1)}) custom-call(f32[12,8,16,256]{3,2,1,0:T(8,128)S(1)} %copy-done, s32[8,2,16]{2,1,0:T(2,128)S(1)} %bitcast.1), custom_call_target="tpu_custom_call" | custom-call | tf_op jit(solution)/shard_map/first/pallas_call | solution.py:691
  4.9 0.2 collective-permute-start.3
  5.1 4.4 %collective-permute-start.4 = (f32[14,16,128]{2,1,0:T(8,128)S(1)}, f32[14,16,128]{2,1,0:T(8,128)}, u32[]{:S(2)}, u32[]{:S(2)}) collective-permute-start(f32[14,16,128]{2,1,0:T(8,128)S(1)} %get-tuple-element.18), channel_id=1, source_target_pairs={{1,2},{3,4},{5,6},{2,1},{4,3},{6,5},{9,10},{11,12},{13,14},{10,9},... | collective-permute-start | bytes 344072 | tf_op jit(solution)/shard_map/ppermute | solution.py:677
  9.5 0.1 collective-permute-start.1
  9.6 4.1 %collective-permute-start.2 = (f32[12,4,16,256]{3,2,1,0:T(8,128)}, f32[12,4,16,256]{3,2,1,0:T(8,128)}, u32[]{:S(2)}, u32[]{:S(2)}) collective-permute-start(f32[12,4,16,256]{3,2,1,0:T(8,128)} %get-tuple-element.17), channel_id=1, source_target_pairs={{8,16},{24,32},{40,48},{56,64},{72,80},{88,96},{104,112},{120,128}... | collective-permute-start | bytes 2359304 | tf_op jit(solution)/shard_map/ppermute | solution.py:677
  13.8 5.7 %collective-permute-start.7 = (f32[12,4,16,256]{3,2,1,0:T(8,128)S(1)}, f32[12,4,16,256]{3,2,1,0:T(8,128)S(1)}, u32[]{:S(2)}, u32[]{:S(2)}) collective-permute-start(f32[12,4,16,256]{3,2,1,0:T(8,128)S(1)} %get-tuple-element.23), channel_id=1, source_target_pairs={{8,16},{24,32},{40,48},{72,80},{88,96},{104,112},{136,144},{152,16... | collective-permute-start | bytes 2359304 | tf_op jit(solution)/shard_map/ppermute | solution.py:724
  19.5 0.0 copy-done.4
  19.5 0.1 multiply_multiply_fusion.1
  19.6 0.0 copy-done.5
  19.6 0.1 select_reduce_fusion
  19.7 0.0 collective-permute-done.3
  19.8 0.1 collective-permute-start
  19.9 17.6 %collective-permute-done.7.refs_2_ = f32[12,4,16,256]{3,2,1,0:T(8,128)S(1)} collective-permute-done((f32[12,4,16,256]{3,2,1,0:T(8,128)S(1)}, f32[12,4,16,256]{3,2,1,0:T(8,128)S(1)}, u32[]{:S(2)}, u32[]{:S(2)}) %collective-permute-start.7) | collective-permute-done | bytes 786464 | tf_op jit(solution)/shard_map/ppermute | solution.py:724
  37.4 5.5 %collective-permute-start.8 = (f32[12,4,16,256]{3,2,1,0:T(8,128)S(1)}, f32[12,4,16,256]{3,2,1,0:T(8,128)S(1)}, u32[]{:S(2)}, u32[]{:S(2)}) collective-permute-start(f32[12,4,16,256]{3,2,1,0:T(8,128)S(1)} %collective-permute-done.7.refs_2_), channel_id=1, source_target_pairs={{0,64},{64,128},{128,192},{120,56},{184,120},{248,184},{1,65},{65,... | collective-permute-start | bytes 2359304 | tf_op jit(solution)/shard_map/ppermute | solution.py:726
  43.0 0.0 collective-permute-done.4
  43.0 0.9 select_select_fusion.1
  44.0 0.1 collective-permute-start.5
  44.1 0.1 add_multiply_fusion
  44.1 1.4 %collective-permute-done.5.strip_inner_hbm = f32[27,16,128]{2,1,0:T(8,128)S(1)} collective-permute-done((f32[27,16,128]{2,1,0:T(8,128)S(1)}, f32[27,16,128]{2,1,0:T(8,128)S(1)}, u32[]{:S(2)}, u32[]{:S(2)}) %collective-permute-start.5) | collective-permute-done | bytes 221216 | tf_op jit(solution)/shard_map/ppermute | solution.py:678
  45.5 0.0 copy-start.1
  45.5 0.7 copy-done.1
  46.2 1.9 %collective-permute-start.6 = (f32[27,16,128]{2,1,0:T(8,128)S(1)}, f32[27,16,128]{2,1,0:T(8,128)}, u32[]{:S(2)}, u32[]{:S(2)}) collective-permute-start(f32[27,16,128]{2,1,0:T(8,128)S(1)} %pad_maximum_fusion.strip_hbm), channel_id=1, source_target_pairs={{8,16},{24,32},{40,48},{56,64},{72,80},{88,96},{104,112},{120,128}... | collective-permute-start | bytes 663560 | tf_op jit(solution)/shard_map/ppermute | solution.py:677
  48.1 0.1 fusion.5
  48.3 8.9 %collective-permute-done.6.strip_outer_hbm = f32[27,16,128]{2,1,0:T(8,128)} collective-permute-done((f32[27,16,128]{2,1,0:T(8,128)S(1)}, f32[27,16,128]{2,1,0:T(8,128)}, u32[]{:S(2)}, u32[]{:S(2)}) %collective-permute-start.6) | collective-permute-done | bytes 221216 | tf_op jit(solution)/shard_map/ppermute | solution.py:677
  57.1 0.1 broadcast_in_dim.33.weight_ref.refs_7_.refs_8_
  57.2 0.0 copy-start.2
  57.2 0.9 copy-done.2
  58.1 7.5 %strips.1 = (f32[24,16,256]{2,1,0:T(8,128)S(1)}, f32[24,16,256]{2,1,0:T(8,128)S(1)}, f32[8,2,16,384]{3,2,1,0:T(8,128)S(1)}) custom-call(f32[27,16,128]{2,1,0:T(8,128)S(1)} %copy-done.2, f32[27,16,128]{2,1,0:T(8,128)S(1)} %pad_maximum_fusion.strip_hbm, f32[27,16,128]{2,1,0:T(8,128)} %collective-permute-done.6.strip_outer_hbm, ...), custom_call_target="tpu_custom_call" | custom-call | flops 43008000 | bytes 8388608 | tf_op jit(solution)/shard_map/strips/pallas_call | solution.py:730
  65.7 0.0 collective-permute-done.1.refs_0_
  65.7 0.0 collective-permute-done.2.refs_1_
  65.7 16.7 %near.1 = (f32[12,16,16,256]{3,2,1,0:T(8,128)S(1)}, f32[8,2,2,16,256]{4,3,2,1,0:T(8,128)S(1)}) custom-call(f32[12,4,16,256]{3,2,1,0:T(8,128)} %collective-permute-done.1.refs_0_, f32[12,4,16,256]{3,2,1,0:T(8,128)} %collective-permute-done.2.refs_1_, f32[12,4,16,256]{3,2,1,0:T(8,128)} %get-tuple-element.16.refs_2_, ...), custom_call_target="tpu_custom_call" | custom-call | flops 100352000 | bytes 8388608 | tf_op jit(solution)/shard_map/near/pallas_call | solution.py:761
  82.4 0.0 collective-permute-done.refs_0_
  82.4 0.0 collective-permute-done.8.refs_3_
  82.4 14.4 %shard_map.46 = f32[12,8,16,256]{3,2,1,0:T(8,128)} custom-call(f32[12,4,16,256]{3,2,1,0:T(8,128)S(1)} %collective-permute-done.refs_0_, f32[12,16,16,256]{3,2,1,0:T(8,128)S(1)} %get-tuple-element.22.refs_1_, f32[12,4,16,256]{3,2,1,0:T(8,128)S(1)} %collective-permute-done.7.refs_2_, f32[12,4,16,256]{3,2,1,0:T(8,128)S(1)} %collective-permute-done.8.refs_3_, ...), custom_call_target="tpu_custom_call" | custom-call | flops 103219200 | bytes 8388608 | tf_op jit(solution)/shard_map/pallas_call | solution.py:776
  (10 shorter events, 0.1 us)
Async XLA Ops:
  0.0 19.5 %copy-start.4 = (f32[2,8]{1,0:T(2,128)S(1)}, f32[2,8]{1,0:T(2,128)}, u32[]{:S(2)}) copy-start(f32[2,8]{1,0:T(2,128)} %param.7) | copy-start | bytes 196
  0.0 19.6 %copy-start.5 = (s32[16]{0:T(128)S(1)}, s32[16]{0:T(128)}, u32[]{:S(2)}) copy-start(s32[16]{0:T(128)} %param.6) | copy-start | bytes 196
  0.0 1.4 %copy-start = (f32[12,8,16,256]{3,2,1,0:T(8,128)S(1)}, f32[12,8,16,256]{3,2,1,0:T(8,128)}, u32[]{:S(2)}) copy-start(f32[12,8,16,256]{3,2,1,0:T(8,128)} %state_ref.1) | copy-start | bytes 4718596
  1.4 0.7 copy-start.3
  4.9 14.9 %collective-permute-start.3 = (f32[14,16,128]{2,1,0:T(8,128)S(1)}, f32[14,16,128]{2,1,0:T(8,128)S(1)}, u32[]{:S(2)}, u32[]{:S(2)}) collective-permute-start(f32[14,16,128]{2,1,0:T(8,128)S(1)} %get-tuple-element.18), channel_id=1, source_target_pairs={{0,1},{2,3},{4,5},{6,7},{1,0},{3,2},{5,4},{7,6},{8,9},{10,11},{12,... | collective-permute-start | bytes 344072 | tf_op jit(solution)/shard_map/ppermute | solution.py:678
  5.1 37.9 %collective-permute-start.4 = (f32[14,16,128]{2,1,0:T(8,128)S(1)}, f32[14,16,128]{2,1,0:T(8,128)}, u32[]{:S(2)}, u32[]{:S(2)}) collective-permute-start(f32[14,16,128]{2,1,0:T(8,128)S(1)} %get-tuple-element.18), channel_id=1, source_target_pairs={{1,2},{3,4},{5,6},{2,1},{4,3},{6,5},{9,10},{11,12},{13,14},{10,9},... | collective-permute-start | bytes 344072 | tf_op jit(solution)/shard_map/ppermute | solution.py:677
  9.5 56.1 %collective-permute-start.1 = (f32[12,4,16,256]{3,2,1,0:T(8,128)}, f32[12,4,16,256]{3,2,1,0:T(8,128)}, u32[]{:S(2)}, u32[]{:S(2)}) collective-permute-start(f32[12,4,16,256]{3,2,1,0:T(8,128)} %get-tuple-element.16.refs_2_), channel_id=1, source_target_pairs={{0,8},{16,24},{32,40},{48,56},{64,72},{80,88},{96,104},{112,120},{... | collective-permute-start | bytes 2359304 | tf_op jit(solution)/shard_map/ppermute | solution.py:678
  9.6 56.1 %collective-permute-start.2 = (f32[12,4,16,256]{3,2,1,0:T(8,128)}, f32[12,4,16,256]{3,2,1,0:T(8,128)}, u32[]{:S(2)}, u32[]{:S(2)}) collective-permute-start(f32[12,4,16,256]{3,2,1,0:T(8,128)} %get-tuple-element.17), channel_id=1, source_target_pairs={{8,16},{24,32},{40,48},{56,64},{72,80},{88,96},{104,112},{120,128}... | collective-permute-start | bytes 2359304 | tf_op jit(solution)/shard_map/ppermute | solution.py:677
  13.8 23.7 %collective-permute-start.7 = (f32[12,4,16,256]{3,2,1,0:T(8,128)S(1)}, f32[12,4,16,256]{3,2,1,0:T(8,128)S(1)}, u32[]{:S(2)}, u32[]{:S(2)}) collective-permute-start(f32[12,4,16,256]{3,2,1,0:T(8,128)S(1)} %get-tuple-element.23), channel_id=1, source_target_pairs={{8,16},{24,32},{40,48},{72,80},{88,96},{104,112},{136,144},{152,16... | collective-permute-start | bytes 2359304 | tf_op jit(solution)/shard_map/ppermute | solution.py:724
  19.8 62.6 %collective-permute-start = (f32[12,4,16,256]{3,2,1,0:T(8,128)S(1)}, f32[12,4,16,256]{3,2,1,0:T(8,128)S(1)}, u32[]{:S(2)}, u32[]{:S(2)}) collective-permute-start(f32[12,4,16,256]{3,2,1,0:T(8,128)S(1)} %get-tuple-element.15.refs_3_), channel_id=1, source_target_pairs={{0,8},{16,24},{32,40},{48,56},{64,72},{80,88},{96,104},{112,120},{... | collective-permute-start | bytes 2359304 | tf_op jit(solution)/shard_map/ppermute | solution.py:725
  37.4 45.0 %collective-permute-start.8 = (f32[12,4,16,256]{3,2,1,0:T(8,128)S(1)}, f32[12,4,16,256]{3,2,1,0:T(8,128)S(1)}, u32[]{:S(2)}, u32[]{:S(2)}) collective-permute-start(f32[12,4,16,256]{3,2,1,0:T(8,128)S(1)} %collective-permute-done.7.refs_2_), channel_id=1, source_target_pairs={{0,64},{64,128},{128,192},{120,56},{184,120},{248,184},{1,65},{65,... | collective-permute-start | bytes 2359304 | tf_op jit(solution)/shard_map/ppermute | solution.py:726
  44.0 1.6 %collective-permute-start.5 = (f32[27,16,128]{2,1,0:T(8,128)S(1)}, f32[27,16,128]{2,1,0:T(8,128)S(1)}, u32[]{:S(2)}, u32[]{:S(2)}) collective-permute-start(f32[27,16,128]{2,1,0:T(8,128)S(1)} %pad_maximum_fusion.strip_hbm), channel_id=1, source_target_pairs={{0,8},{16,24},{32,40},{48,56},{64,72},{80,88},{96,104},{112,120},{... | collective-permute-start | bytes 663560 | tf_op jit(solution)/shard_map/ppermute | solution.py:678
  45.5 0.7 copy-start.1
  46.2 10.9 %collective-permute-start.6 = (f32[27,16,128]{2,1,0:T(8,128)S(1)}, f32[27,16,128]{2,1,0:T(8,128)}, u32[]{:S(2)}, u32[]{:S(2)}) collective-permute-start(f32[27,16,128]{2,1,0:T(8,128)S(1)} %pad_maximum_fusion.strip_hbm), channel_id=1, source_target_pairs={{8,16},{24,32},{40,48},{56,64},{72,80},{88,96},{104,112},{120,128}... | collective-permute-start | bytes 663560 | tf_op jit(solution)/shard_map/ppermute | solution.py:677
  57.2 0.9 copy-start.2

commit v5 on v4

--- a/solution.py
+++ b/solution.py
@@ -295,21 +295,19 @@
         copy.wait()
 
 
-def react_tile(at, live):
+def react_tile(at, live, kept=COMPS):
     new = react([at(c)[...] for c in range(COMPS)])
-    for c in range(COMPS):
+    for c in range(kept):
         pltpu.store(at(c), new[c], mask=live > 0.5)
     return live * new[0]
 
 
-def react_rows(main, inside, pot, rows):
+def react_rows(main, inside, pot, rows, kept=COMPS):
     for x in rows:
         for level in range(main.shape[2] // 8):
             for i in range(main.shape[3] // LANES):
                 place = (x, pl.ds(level * 8, 8), pl.ds(i * LANES, LANES))
-                held = react_tile(lambda c: main.at[(c,) + place], inside[place])
-                if pot is not None:
-                    pot[place] = held
+                pot[place] = react_tile(lambda c: main.at[(c,) + place], inside[place], kept)
 
 
 def shift_row(pot, dy_ref, sy_ref, x, ext, strip_row):
@@ -433,7 +431,7 @@
         strip_total[side] = strip_spread(weight_ref, strip[side, COMPS])
         strip_track[0, side] = strip[side, COMPS] * strip[side, 0]
 
-    def step(s, carry):
+    def step(kept, s, carry):
         for side in sides:
             u = strip[side, 0]
             flow = strip_spread(weight_ref, strip_track[s, side]) - u * strip_total[side]
@@ -444,12 +442,13 @@
                 for i in range(3):
                     place = (pl.ds(level * 8, 8), pl.ds(i * LANES, LANES))
                     held = react_tile(
-                        lambda c: strip.at[(side, c) + place], strip[(side, COMPS) + place]
+                        lambda c: strip.at[(side, c) + place], strip[(side, COMPS) + place], kept
                     )
                     strip_track[(s + 1, side) + place] = held
         return carry
 
-    lax.fori_loop(0, STEPS - 1, step, 0)
+    lax.fori_loop(0, STEPS - 2, functools.partial(step, COMPS), 0)
+    step(1, STEPS - 2, 0)
 
 
 def finished(main, main_out, sems, s, wait):
@@ -498,16 +497,19 @@
 
     lax.fori_loop(0, count // 2, start_row, 0)
 
+    def shift(s, x):
+        shift_row(
+            pot, dy_ref, sy_ref, x, skip + x, lambda side, block: strip_track[s, side, :, block]
+        )
+
+    def shift_some(k, carry):
+        for q in range(group):
+            shift(0, group * k + q)
+        return carry
+
+    lax.fori_loop(0, count // group, shift_some, 0)
+
     def step(s, carry):
-        def shift_some(k, carry):
-            for q in range(group):
-                x = group * k + q
-                shift_row(
-                    pot, dy_ref, sy_ref, x, skip + x, lambda side, block: strip_track[s, side, :, block]
-                )
-            return carry
-
-        lax.fori_loop(s // group, (count - 1 - s) // group + 1, shift_some, 0)
         for q, row in enumerate((s + 1, count - 2 - s)):
             track[s, q, 0] = pot[row]
             track[s, q, 1] = dy_ref[row]
@@ -531,10 +533,17 @@
 
         def react_some(k, carry):
             x = s + 1 + 2 * k
+            for q in range(2):
+                shift(s + 1, jnp.maximum(x - 2 + q, 0))
             react_rows(main, inside.at[pl.ds(skip, count)], pot, (x, x + 1))
             return carry
 
-        lax.fori_loop(0, jnp.where(s < STEPS - 1, count // 2 - 1 - s, 0), react_some, 0)
+        @pl.when(s < min(STEPS - 1, count // 2 - 1))
+        def _():
+            lax.fori_loop(0, count // 2 - 1 - s, react_some, 0)
+            for q in range(2):
+                shift(s + 1, count - 3 - s + q)
+
         return carry
 
     lax.fori_loop(0, STEPS, step, 0)
@@ -593,15 +602,21 @@
         for x in (q, span - 1 - q):
             pot[x] = inside[skip + x] * main[0, x]
 
+    def shift(s, x):
+        shift_row(
+            pot, dy_ref, sy_ref, x, skip + x, lambda side, block: strip_track[s, side, :, block]
+        )
+
+    for q in range(far - 1):
+        for x in (q, span - 1 - q):
+            shift(0, x)
+
     def step(s, carry):
         for row in (s + far, span - 1 - far - s):
             pot[row] = inside[skip + row] * main[0, row]
-        for first in (s, span - 1 - far - s):
-            for q in range(far + 1):
-                x = first + q
-                shift_row(
-                    pot, dy_ref, sy_ref, x, skip + x, lambda side, block: strip_track[s, side, :, block]
-                )
+        for q in (far - 1, far):
+            for x in (s + q, span - 1 - s - q):
+                shift(s, x)
 
         def known():
             for q, row in enumerate((s + far + 1, span - 2 - far - s)):
@@ -632,12 +647,20 @@
         if not last:
             finished(main, main_out, out_sems, s, False)
 
+        held = inside.at[pl.ds(skip, span)]
+
         def react_pair(k, carry):
             near_row, far_row = s + 1 + k, span - 2 - s - k
-            react_rows(main, inside.at[pl.ds(skip, span)], pot, (near_row, far_row))
+            shift(s + 1, near_row - 1)
+            shift(s + 1, far_row + 1)
+            react_rows(main, held, pot, (near_row, far_row))
             return carry
 
-        lax.fori_loop(0, jnp.where(s < STEPS - 1, far, 0), react_pair, 0)
+        @pl.when(s < STEPS - 1)
+        def _():
+            react_rows(main, held, pot, (s + 1, span - 2 - s), 1 if last else COMPS)
+            lax.fori_loop(1, far, react_pair, 0)
+
         return carry
 
     lax.fori_loop(0, STEPS, step, 0)

time: 97.2 us -> 92.7 us (0.954)
  Pallas kernels: 41.4 us -> 36.9 us
    pallas_call x1, Pallas kernels: 14.4 us -> 12.3 us  [shards(): pl.pallas_call(functools.partial(ring_kernel, last), out_shape=outs, in_s...]
    pallas_call x1, Pallas kernels: 16.7 us -> 14.7 us  [shards(): pl.pallas_call(functools.partial(near_kernel, len(CHUNKS), near), out_sha...]
  transfers between devices with their start and end apart: 9 -> 9, of which waited for: 3 -> 3; matrix products, arithmetic and copies ran while one was open for 1% -> 2% of each run, Pallas kernels for 25% -> 24%
where the time goes in v5:
time: 92.7 us; the launch traced here: 92.4 us
  Pallas kernels  36.9 us (40%)
  waiting for transfers between devices  27.8 us (30%)
  starting transfers between devices  22.2 us (24%)
  local copies, waits for them, and re-layouts  3.91 us (4%)
  other arithmetic  1.28 us (1%)
    ppermute x1, waiting for transfers between devices, shards(): far_outer = lax.ppermute(outer_faces[1], 'gx', close + around)  17.6 us
    pallas_call x1, Pallas kernels, shards(): pl.pallas_call(functools.partial(near_kernel, len(CHUNKS), near), out_sha...  14.7 us
    pallas_call x1, Pallas kernels, shards(): pl.pallas_call(functools.partial(ring_kernel, last), out_shape=outs, in_s...  12.3 us
    ppermute x3, starting transfers between devices, both(): outer = lax.ppermute(outer, axis, swaps(size, 1))  10.5 us
    ppermute x3, waiting for transfers between devices, both(): outer = lax.ppermute(outer, axis, swaps(size, 1))  8.86 us
    pallas_call x1, Pallas kernels, shards(): pl.pallas_call(strip_kernel, out_shape=[shape(span, depth, width), shape(...  7.15 us
    ppermute x1, starting transfers between devices, shards(): far_outer = lax.ppermute(outer_faces[1], 'gx', close + around)  5.69 us
    ppermute x1, starting transfers between devices, shards(): far_relay = lax.ppermute(far_outer, 'gx', onward)  5.54 us
  transfers between devices with their start and end apart: 9, of which 3 were waited for; matrix products, arithmetic and copies ran while one was open for 2% of the time, Pallas kernels for 24%

profile of v5, /device:TPU:100, one launch (start us, length us, event | category | flops | bytes accessed | tf_op | source)
XLA Modules:
  0.0 92.4 jit_solution(3635092417350197857)
XLA Ops:
  0.0 0.0 copy-start.4
  0.0 0.0 copy-start.5
  0.0 0.0 copy-start
  0.0 1.4 %copy-done = f32[12,8,16,256]{3,2,1,0:T(8,128)S(1)} copy-done((f32[12,8,16,256]{3,2,1,0:T(8,128)S(1)}, f32[12,8,16,256]{3,2,1,0:T(8,128)}, u32[]{:S(2)}) %copy-start) | copy-done | bytes 1572888
  1.4 0.0 copy-start.3
  1.4 0.7 copy-done.3
  2.1 2.8 %first.1 = (f32[12,4,16,256]{3,2,1,0:T(8,128)}, f32[12,4,16,256]{3,2,1,0:T(8,128)}, f32[12,4,16,256]{3,2,1,0:T(8,128)S(1)}, f32[12,4,16,256]{3,2,1,0:T(8,128)S(1)}, f32[14,16,128]{2,1,0:T(8,128)S(1)}) custom-call(f32[12,8,16,256]{3,2,1,0:T(8,128)S(1)} %copy-done, s32[8,2,16]{2,1,0:T(2,128)S(1)} %bitcast.1), custom_call_target="tpu_custom_call" | custom-call | tf_op jit(solution)/shard_map/first/pallas_call | solution.py:714
  4.9 0.2 collective-permute-start.3
  5.1 4.4 %collective-permute-start.4 = (f32[14,16,128]{2,1,0:T(8,128)S(1)}, f32[14,16,128]{2,1,0:T(8,128)}, u32[]{:S(2)}, u32[]{:S(2)}) collective-permute-start(f32[14,16,128]{2,1,0:T(8,128)S(1)} %get-tuple-element.18), channel_id=1, source_target_pairs={{1,2},{3,4},{5,6},{2,1},{4,3},{6,5},{9,10},{11,12},{13,14},{10,9},... | collective-permute-start | bytes 344072 | tf_op jit(solution)/shard_map/ppermute | solution.py:700
  9.5 0.1 collective-permute-start.1
  9.6 4.1 %collective-permute-start.2 = (f32[12,4,16,256]{3,2,1,0:T(8,128)}, f32[12,4,16,256]{3,2,1,0:T(8,128)}, u32[]{:S(2)}, u32[]{:S(2)}) collective-permute-start(f32[12,4,16,256]{3,2,1,0:T(8,128)} %get-tuple-element.17), channel_id=1, source_target_pairs={{8,16},{24,32},{40,48},{56,64},{72,80},{88,96},{104,112},{120,128}... | collective-permute-start | bytes 2359304 | tf_op jit(solution)/shard_map/ppermute | solution.py:700
  13.8 5.7 %collective-permute-start.7 = (f32[12,4,16,256]{3,2,1,0:T(8,128)S(1)}, f32[12,4,16,256]{3,2,1,0:T(8,128)S(1)}, u32[]{:S(2)}, u32[]{:S(2)}) collective-permute-start(f32[12,4,16,256]{3,2,1,0:T(8,128)S(1)} %get-tuple-element.23), channel_id=1, source_target_pairs={{8,16},{24,32},{40,48},{72,80},{88,96},{104,112},{136,144},{152,16... | collective-permute-start | bytes 2359304 | tf_op jit(solution)/shard_map/ppermute | solution.py:747
  19.5 0.0 copy-done.4
  19.5 0.1 multiply_multiply_fusion.1
  19.6 0.0 copy-done.5
  19.6 0.1 select_reduce_fusion
  19.7 0.0 collective-permute-done.3
  19.8 0.1 collective-permute-start
  19.9 17.6 %collective-permute-done.7.refs_2_ = f32[12,4,16,256]{3,2,1,0:T(8,128)S(1)} collective-permute-done((f32[12,4,16,256]{3,2,1,0:T(8,128)S(1)}, f32[12,4,16,256]{3,2,1,0:T(8,128)S(1)}, u32[]{:S(2)}, u32[]{:S(2)}) %collective-permute-start.7) | collective-permute-done | bytes 786464 | tf_op jit(solution)/shard_map/ppermute | solution.py:747
  37.4 5.5 %collective-permute-start.8 = (f32[12,4,16,256]{3,2,1,0:T(8,128)S(1)}, f32[12,4,16,256]{3,2,1,0:T(8,128)S(1)}, u32[]{:S(2)}, u32[]{:S(2)}) collective-permute-start(f32[12,4,16,256]{3,2,1,0:T(8,128)S(1)} %collective-permute-done.7.refs_2_), channel_id=1, source_target_pairs={{0,64},{64,128},{128,192},{120,56},{184,120},{248,184},{1,65},{65,... | collective-permute-start | bytes 2359304 | tf_op jit(solution)/shard_map/ppermute | solution.py:749
  43.0 0.0 collective-permute-done.4
  43.0 0.9 %select_select_fusion.1 = (f32[13,16,128]{2,1,0:T(8,128)S(1)}, f32[13,16,128]{2,1,0:T(8,128)S(1)}) fusion(f32[14,16,128]{2,1,0:T(8,128)S(1)} %get-tuple-element.18, f32[14,16,128]{2,1,0:T(8,128)} %collective-permute-done.4, f32[14,16,128]{2,1,0:T(8,128)S(1)} %collective-permute-done.3, pred[14,16,128]{2,1,0:T(8,128)(4,1)S(1)} %select_compare_fusion, pred[]{:T(512)S(6)} %eq.22), kind=kLoop, calls=%fused_computation.3 | loop fusion | flops 106496 | bytes 559105 | tf_op jit(solution)/shard_map/jit(_where)/select_n | solution.py:736
  44.0 0.1 collective-permute-start.5
  44.1 0.1 add_multiply_fusion
  44.1 1.4 %collective-permute-done.5.strip_inner_hbm = f32[27,16,128]{2,1,0:T(8,128)S(1)} collective-permute-done((f32[27,16,128]{2,1,0:T(8,128)S(1)}, f32[27,16,128]{2,1,0:T(8,128)S(1)}, u32[]{:S(2)}, u32[]{:S(2)}) %collective-permute-start.5) | collective-permute-done | bytes 221216 | tf_op jit(solution)/shard_map/ppermute | solution.py:701
  45.5 0.0 copy-start.1
  45.5 0.7 copy-done.1
  46.2 1.9 %collective-permute-start.6 = (f32[27,16,128]{2,1,0:T(8,128)S(1)}, f32[27,16,128]{2,1,0:T(8,128)}, u32[]{:S(2)}, u32[]{:S(2)}) collective-permute-start(f32[27,16,128]{2,1,0:T(8,128)S(1)} %pad_maximum_fusion.strip_hbm), channel_id=1, source_target_pairs={{8,16},{24,32},{40,48},{56,64},{72,80},{88,96},{104,112},{120,128}... | collective-permute-start | bytes 663560 | tf_op jit(solution)/shard_map/ppermute | solution.py:700
  48.1 0.1 fusion.5
  48.3 8.9 %collective-permute-done.6.strip_outer_hbm = f32[27,16,128]{2,1,0:T(8,128)} collective-permute-done((f32[27,16,128]{2,1,0:T(8,128)S(1)}, f32[27,16,128]{2,1,0:T(8,128)}, u32[]{:S(2)}, u32[]{:S(2)}) %collective-permute-start.6) | collective-permute-done | bytes 221216 | tf_op jit(solution)/shard_map/ppermute | solution.py:700
  57.1 0.1 broadcast_in_dim.33.weight_ref.refs_7_.refs_8_
  57.2 0.0 copy-start.2
  57.2 0.9 %copy-done.2 = f32[27,16,128]{2,1,0:T(8,128)S(1)} copy-done((f32[27,16,128]{2,1,0:T(8,128)S(1)}, f32[27,16,128]{2,1,0:T(8,128)}, u32[]{:S(2)}) %copy-start.2) | copy-done | bytes 221208
  58.1 7.1 %strips.1 = (f32[24,16,256]{2,1,0:T(8,128)S(1)}, f32[24,16,256]{2,1,0:T(8,128)S(1)}, f32[8,2,16,384]{3,2,1,0:T(8,128)S(1)}) custom-call(f32[27,16,128]{2,1,0:T(8,128)S(1)} %copy-done.2, f32[27,16,128]{2,1,0:T(8,128)S(1)} %pad_maximum_fusion.strip_hbm, f32[27,16,128]{2,1,0:T(8,128)} %collective-permute-done.6.strip_outer_hbm, ...), custom_call_target="tpu_custom_call" | custom-call | flops 43008000 | bytes 8388608 | tf_op jit(solution)/shard_map/strips/pallas_call | solution.py:753
  65.3 0.0 collective-permute-done.1.refs_0_
  65.3 0.0 collective-permute-done.2.refs_1_
  65.3 14.7 %near.1 = (f32[12,16,16,256]{3,2,1,0:T(8,128)S(1)}, f32[8,2,2,16,256]{4,3,2,1,0:T(8,128)S(1)}) custom-call(f32[12,4,16,256]{3,2,1,0:T(8,128)} %collective-permute-done.1.refs_0_, f32[12,4,16,256]{3,2,1,0:T(8,128)} %collective-permute-done.2.refs_1_, f32[12,4,16,256]{3,2,1,0:T(8,128)} %get-tuple-element.16.refs_2_, ...), custom_call_target="tpu_custom_call" | custom-call | flops 100352000 | bytes 8388608 | tf_op jit(solution)/shard_map/near/pallas_call | solution.py:784
  80.1 0.0 collective-permute-done.refs_0_
  80.1 0.0 collective-permute-done.8.refs_3_
  80.1 12.3 %shard_map.46 = f32[12,8,16,256]{3,2,1,0:T(8,128)} custom-call(f32[12,4,16,256]{3,2,1,0:T(8,128)S(1)} %collective-permute-done.refs_0_, f32[12,16,16,256]{3,2,1,0:T(8,128)S(1)} %get-tuple-element.22.refs_1_, f32[12,4,16,256]{3,2,1,0:T(8,128)S(1)} %collective-permute-done.7.refs_2_, f32[12,4,16,256]{3,2,1,0:T(8,128)S(1)} %collective-permute-done.8.refs_3_, ...), custom_call_target="tpu_custom_call" | custom-call | flops 103219200 | bytes 8388608 | tf_op jit(solution)/shard_map/pallas_call | solution.py:799
  (10 shorter events, 0.1 us)
Async XLA Ops:
  0.0 19.5 %copy-start.4 = (f32[2,8]{1,0:T(2,128)S(1)}, f32[2,8]{1,0:T(2,128)}, u32[]{:S(2)}) copy-start(f32[2,8]{1,0:T(2,128)} %param.7) | copy-start | bytes 196
  0.0 19.6 %copy-start.5 = (s32[16]{0:T(128)S(1)}, s32[16]{0:T(128)}, u32[]{:S(2)}) copy-start(s32[16]{0:T(128)} %param.6) | copy-start | bytes 196
  0.0 1.4 %copy-start = (f32[12,8,16,256]{3,2,1,0:T(8,128)S(1)}, f32[12,8,16,256]{3,2,1,0:T(8,128)}, u32[]{:S(2)}) copy-start(f32[12,8,16,256]{3,2,1,0:T(8,128)} %state_ref.1) | copy-start | bytes 4718596
  1.4 0.7 copy-start.3
  4.9 14.9 %collective-permute-start.3 = (f32[14,16,128]{2,1,0:T(8,128)S(1)}, f32[14,16,128]{2,1,0:T(8,128)S(1)}, u32[]{:S(2)}, u32[]{:S(2)}) collective-permute-start(f32[14,16,128]{2,1,0:T(8,128)S(1)} %get-tuple-element.18), channel_id=1, source_target_pairs={{0,1},{2,3},{4,5},{6,7},{1,0},{3,2},{5,4},{7,6},{8,9},{10,11},{12,... | collective-permute-start | bytes 344072 | tf_op jit(solution)/shard_map/ppermute | solution.py:701
  5.1 37.9 %collective-permute-start.4 = (f32[14,16,128]{2,1,0:T(8,128)S(1)}, f32[14,16,128]{2,1,0:T(8,128)}, u32[]{:S(2)}, u32[]{:S(2)}) collective-permute-start(f32[14,16,128]{2,1,0:T(8,128)S(1)} %get-tuple-element.18), channel_id=1, source_target_pairs={{1,2},{3,4},{5,6},{2,1},{4,3},{6,5},{9,10},{11,12},{13,14},{10,9},... | collective-permute-start | bytes 344072 | tf_op jit(solution)/shard_map/ppermute | solution.py:700
  9.5 55.7 %collective-permute-start.1 = (f32[12,4,16,256]{3,2,1,0:T(8,128)}, f32[12,4,16,256]{3,2,1,0:T(8,128)}, u32[]{:S(2)}, u32[]{:S(2)}) collective-permute-start(f32[12,4,16,256]{3,2,1,0:T(8,128)} %get-tuple-element.16.refs_2_), channel_id=1, source_target_pairs={{0,8},{16,24},{32,40},{48,56},{64,72},{80,88},{96,104},{112,120},{... | collective-permute-start | bytes 2359304 | tf_op jit(solution)/shard_map/ppermute | solution.py:701
  9.6 55.7 %collective-permute-start.2 = (f32[12,4,16,256]{3,2,1,0:T(8,128)}, f32[12,4,16,256]{3,2,1,0:T(8,128)}, u32[]{:S(2)}, u32[]{:S(2)}) collective-permute-start(f32[12,4,16,256]{3,2,1,0:T(8,128)} %get-tuple-element.17), channel_id=1, source_target_pairs={{8,16},{24,32},{40,48},{56,64},{72,80},{88,96},{104,112},{120,128}... | collective-permute-start | bytes 2359304 | tf_op jit(solution)/shard_map/ppermute | solution.py:700
  13.8 23.7 %collective-permute-start.7 = (f32[12,4,16,256]{3,2,1,0:T(8,128)S(1)}, f32[12,4,16,256]{3,2,1,0:T(8,128)S(1)}, u32[]{:S(2)}, u32[]{:S(2)}) collective-permute-start(f32[12,4,16,256]{3,2,1,0:T(8,128)S(1)} %get-tuple-element.23), channel_id=1, source_target_pairs={{8,16},{24,32},{40,48},{72,80},{88,96},{104,112},{136,144},{152,16... | collective-permute-start | bytes 2359304 | tf_op jit(solution)/shard_map/ppermute | solution.py:747
  19.8 60.3 %collective-permute-start = (f32[12,4,16,256]{3,2,1,0:T(8,128)S(1)}, f32[12,4,16,256]{3,2,1,0:T(8,128)S(1)}, u32[]{:S(2)}, u32[]{:S(2)}) collective-permute-start(f32[12,4,16,256]{3,2,1,0:T(8,128)S(1)} %get-tuple-element.15.refs_3_), channel_id=1, source_target_pairs={{0,8},{16,24},{32,40},{48,56},{64,72},{80,88},{96,104},{112,120},{... | collective-permute-start | bytes 2359304 | tf_op jit(solution)/shard_map/ppermute | solution.py:748
  37.4 42.6 %collective-permute-start.8 = (f32[12,4,16,256]{3,2,1,0:T(8,128)S(1)}, f32[12,4,16,256]{3,2,1,0:T(8,128)S(1)}, u32[]{:S(2)}, u32[]{:S(2)}) collective-permute-start(f32[12,4,16,256]{3,2,1,0:T(8,128)S(1)} %collective-permute-done.7.refs_2_), channel_id=1, source_target_pairs={{0,64},{64,128},{128,192},{120,56},{184,120},{248,184},{1,65},{65,... | collective-permute-start | bytes 2359304 | tf_op jit(solution)/shard_map/ppermute | solution.py:749
  44.0 1.6 %collective-permute-start.5 = (f32[27,16,128]{2,1,0:T(8,128)S(1)}, f32[27,16,128]{2,1,0:T(8,128)S(1)}, u32[]{:S(2)}, u32[]{:S(2)}) collective-permute-start(f32[27,16,128]{2,1,0:T(8,128)S(1)} %pad_maximum_fusion.strip_hbm), channel_id=1, source_target_pairs={{0,8},{16,24},{32,40},{48,56},{64,72},{80,88},{96,104},{112,120},{... | collective-permute-start | bytes 663560 | tf_op jit(solution)/shard_map/ppermute | solution.py:701
  45.5 0.7 copy-start.1
  46.2 10.9 %collective-permute-start.6 = (f32[27,16,128]{2,1,0:T(8,128)S(1)}, f32[27,16,128]{2,1,0:T(8,128)}, u32[]{:S(2)}, u32[]{:S(2)}) collective-permute-start(f32[27,16,128]{2,1,0:T(8,128)S(1)} %pad_maximum_fusion.strip_hbm), channel_id=1, source_target_pairs={{8,16},{24,32},{40,48},{56,64},{72,80},{88,96},{104,112},{120,128}... | collective-permute-start | bytes 663560 | tf_op jit(solution)/shard_map/ppermute | solution.py:700
  57.2 0.9 %copy-start.2 = (f32[27,16,128]{2,1,0:T(8,128)S(1)}, f32[27,16,128]{2,1,0:T(8,128)}, u32[]{:S(2)}) copy-start(f32[27,16,128]{2,1,0:T(8,128)} %copy-done.1) | copy-start | bytes 663556

commit v6 on v5

--- a/solution.py
+++ b/solution.py
@@ -463,6 +463,14 @@
             copy.start()
 
 
+def in_two(source, main, row, sems, i):
+    place = pl.ds(row, source.shape[1])
+    return [
+        pltpu.make_async_copy(source.at[part], main.at[part, place], sems.at[2 * i + q])
+        for q, part in enumerate((pl.ds(0, 1), pl.ds(1, COMPS - 1)))
+    ]
+
+
 def near_kernel(pieces, near, *refs):
     sources, refs = refs[: pieces + 2], refs[pieces + 2 :]
     inside, total, strip_track, weight_ref, main_out, track = refs[:6]
@@ -479,14 +487,12 @@
         above, below = cells - start - rows, start
         places.append((near + above + odd * (below - above), source))
         start += rows
-    copies = [
-        pltpu.make_async_copy(source, main.at[:, pl.ds(row, source.shape[1])], sems.at[i])
-        for i, (row, source) in enumerate(places)
-    ]
+    copies = [in_two(source, main, row, sems, i) for i, (row, source) in enumerate(places)]
+    for part in range(2):
+        for copy in copies:
+            copy[part].start()
     for copy in copies:
-        copy.start()
-    for copy in copies:
-        copy.wait()
+        copy[0].wait()
 
     group = 4 if count % 4 == 0 else 2
 
@@ -526,6 +532,11 @@
         lax.fori_loop(0, pairs // 2, functools.partial(diffuse_some, 4, s + 1), 0)
         rest = s + 1 + pairs // 2 * 4
         lax.fori_loop(0, lax.rem(pairs, 2), functools.partial(diffuse_some, 2, rest), 0)
+
+        @pl.when(s == 0)
+        def _():
+            for copy in copies:
+                copy[1].wait()
 
         @pl.when(s < min(STEPS, count // 2))
         def _():
@@ -787,7 +798,7 @@
         in_specs=[hbm] * (2 + len(CHUNKS)) + [vmem] * 4,
         out_specs=[hbm, vmem],
         scratch_shapes=buffers(count)
-        + [pltpu.SemaphoreType.DMA((2 + len(CHUNKS),)), pltpu.SemaphoreType.DMA((2 * STEPS,))],
+        + [pltpu.SemaphoreType.DMA((2 * (2 + len(CHUNKS)),)), pltpu.SemaphoreType.DMA((2 * STEPS,))],
         compiler_params=params,
         cost_estimate=cost(70),
         name="near",

time: 92.7 us -> 92.1 us (level)
  transfers between devices with their start and end apart: 9 -> 9, of which waited for: 3 -> 3; matrix products, arithmetic and copies ran while one was open for 2% -> 2% of each run, Pallas kernels for 24% -> 23%
where the time goes in v6:
time: 92.1 us; the launch traced here: 91.7 us
  Pallas kernels  36.3 us (39%)
  waiting for transfers between devices  27.8 us (30%)
  starting transfers between devices  22.2 us (24%)
  local copies, waits for them, and re-layouts  3.91 us (4%)
  other arithmetic  1.28 us (1%)
    ppermute x1, waiting for transfers between devices, shards(): far_outer = lax.ppermute(outer_faces[1], 'gx', close + around)  17.6 us
    pallas_call x1, Pallas kernels, shards(): pl.pallas_call(functools.partial(near_kernel, len(CHUNKS), near), out_sha...  14.1 us
    pallas_call x1, Pallas kernels, shards(): pl.pallas_call(functools.partial(ring_kernel, last), out_shape=outs, in_s...  12.3 us
    ppermute x3, starting transfers between devices, both(): outer = lax.ppermute(outer, axis, swaps(size, 1))  10.5 us
    ppermute x3, waiting for transfers between devices, both(): outer = lax.ppermute(outer, axis, swaps(size, 1))  8.86 us
    pallas_call x1, Pallas kernels, shards(): pl.pallas_call(strip_kernel, out_shape=[shape(span, depth, width), shape(...  7.15 us
    ppermute x1, starting transfers between devices, shards(): far_outer = lax.ppermute(outer_faces[1], 'gx', close + around)  5.69 us
    ppermute x1, starting transfers between devices, shards(): far_relay = lax.ppermute(far_outer, 'gx', onward)  5.54 us
  transfers between devices with their start and end apart: 9, of which 3 were waited for; matrix products, arithmetic and copies ran while one was open for 2% of the time, Pallas kernels for 23%

profile of v6, /device:TPU:100, one launch (start us, length us, event | category | flops | bytes accessed | tf_op | source)
XLA Modules:
  0.0 91.7 jit_solution(5939942427412575901)
XLA Ops:
  0.0 0.0 copy-start.4
  0.0 0.0 copy-start.5
  0.0 0.0 copy-start
  0.0 1.4 %copy-done = f32[12,8,16,256]{3,2,1,0:T(8,128)S(1)} copy-done((f32[12,8,16,256]{3,2,1,0:T(8,128)S(1)}, f32[12,8,16,256]{3,2,1,0:T(8,128)}, u32[]{:S(2)}) %copy-start) | copy-done | bytes 1572888
  1.4 0.0 copy-start.3
  1.4 0.7 copy-done.3
  2.1 2.8 %first.1 = (f32[12,4,16,256]{3,2,1,0:T(8,128)}, f32[12,4,16,256]{3,2,1,0:T(8,128)}, f32[12,4,16,256]{3,2,1,0:T(8,128)S(1)}, f32[12,4,16,256]{3,2,1,0:T(8,128)S(1)}, f32[14,16,128]{2,1,0:T(8,128)S(1)}) custom-call(f32[12,8,16,256]{3,2,1,0:T(8,128)S(1)} %copy-done, s32[8,2,16]{2,1,0:T(2,128)S(1)} %bitcast.1), custom_call_target="tpu_custom_call" | custom-call | tf_op jit(solution)/shard_map/first/pallas_call | solution.py:725
  4.9 0.2 collective-permute-start.3
  5.1 4.4 %collective-permute-start.4 = (f32[14,16,128]{2,1,0:T(8,128)S(1)}, f32[14,16,128]{2,1,0:T(8,128)}, u32[]{:S(2)}, u32[]{:S(2)}) collective-permute-start(f32[14,16,128]{2,1,0:T(8,128)S(1)} %get-tuple-element.18), channel_id=1, source_target_pairs={{1,2},{3,4},{5,6},{2,1},{4,3},{6,5},{9,10},{11,12},{13,14},{10,9},... | collective-permute-start | bytes 344072 | tf_op jit(solution)/shard_map/ppermute | solution.py:711
  9.5 0.1 collective-permute-start.1
  9.6 4.1 %collective-permute-start.2 = (f32[12,4,16,256]{3,2,1,0:T(8,128)}, f32[12,4,16,256]{3,2,1,0:T(8,128)}, u32[]{:S(2)}, u32[]{:S(2)}) collective-permute-start(f32[12,4,16,256]{3,2,1,0:T(8,128)} %get-tuple-element.17), channel_id=1, source_target_pairs={{8,16},{24,32},{40,48},{56,64},{72,80},{88,96},{104,112},{120,128}... | collective-permute-start | bytes 2359304 | tf_op jit(solution)/shard_map/ppermute | solution.py:711
  13.8 5.7 %collective-permute-start.7 = (f32[12,4,16,256]{3,2,1,0:T(8,128)S(1)}, f32[12,4,16,256]{3,2,1,0:T(8,128)S(1)}, u32[]{:S(2)}, u32[]{:S(2)}) collective-permute-start(f32[12,4,16,256]{3,2,1,0:T(8,128)S(1)} %get-tuple-element.23), channel_id=1, source_target_pairs={{8,16},{24,32},{40,48},{72,80},{88,96},{104,112},{136,144},{152,16... | collective-permute-start | bytes 2359304 | tf_op jit(solution)/shard_map/ppermute | solution.py:758
  19.5 0.0 copy-done.4
  19.5 0.1 multiply_multiply_fusion.1
  19.6 0.0 copy-done.5
  19.6 0.1 select_reduce_fusion
  19.7 0.0 collective-permute-done.3
  19.8 0.1 collective-permute-start
  19.9 17.6 %collective-permute-done.7.refs_2_ = f32[12,4,16,256]{3,2,1,0:T(8,128)S(1)} collective-permute-done((f32[12,4,16,256]{3,2,1,0:T(8,128)S(1)}, f32[12,4,16,256]{3,2,1,0:T(8,128)S(1)}, u32[]{:S(2)}, u32[]{:S(2)}) %collective-permute-start.7) | collective-permute-done | bytes 786464 | tf_op jit(solution)/shard_map/ppermute | solution.py:758
  37.4 5.5 %collective-permute-start.8 = (f32[12,4,16,256]{3,2,1,0:T(8,128)S(1)}, f32[12,4,16,256]{3,2,1,0:T(8,128)S(1)}, u32[]{:S(2)}, u32[]{:S(2)}) collective-permute-start(f32[12,4,16,256]{3,2,1,0:T(8,128)S(1)} %collective-permute-done.7.refs_2_), channel_id=1, source_target_pairs={{0,64},{64,128},{128,192},{120,56},{184,120},{248,184},{1,65},{65,... | collective-permute-start | bytes 2359304 | tf_op jit(solution)/shard_map/ppermute | solution.py:760
  43.0 0.0 collective-permute-done.4
  43.0 0.9 %select_select_fusion.1 = (f32[13,16,128]{2,1,0:T(8,128)S(1)}, f32[13,16,128]{2,1,0:T(8,128)S(1)}) fusion(f32[14,16,128]{2,1,0:T(8,128)S(1)} %get-tuple-element.18, f32[14,16,128]{2,1,0:T(8,128)} %collective-permute-done.4, f32[14,16,128]{2,1,0:T(8,128)S(1)} %collective-permute-done.3, pred[14,16,128]{2,1,0:T(8,128)(4,1)S(1)} %select_compare_fusion, pred[]{:T(512)S(6)} %eq.22), kind=kLoop, calls=%fused_computation.3 | loop fusion | flops 106496 | bytes 559105 | tf_op jit(solution)/shard_map/jit(_where)/select_n | solution.py:747
  44.0 0.1 collective-permute-start.5
  44.1 0.1 add_multiply_fusion
  44.1 1.4 %collective-permute-done.5.strip_inner_hbm = f32[27,16,128]{2,1,0:T(8,128)S(1)} collective-permute-done((f32[27,16,128]{2,1,0:T(8,128)S(1)}, f32[27,16,128]{2,1,0:T(8,128)S(1)}, u32[]{:S(2)}, u32[]{:S(2)}) %collective-permute-start.5) | collective-permute-done | bytes 221216 | tf_op jit(solution)/shard_map/ppermute | solution.py:712
  45.5 0.0 copy-start.1
  45.5 0.7 copy-done.1
  46.2 1.9 %collective-permute-start.6 = (f32[27,16,128]{2,1,0:T(8,128)S(1)}, f32[27,16,128]{2,1,0:T(8,128)}, u32[]{:S(2)}, u32[]{:S(2)}) collective-permute-start(f32[27,16,128]{2,1,0:T(8,128)S(1)} %pad_maximum_fusion.strip_hbm), channel_id=1, source_target_pairs={{8,16},{24,32},{40,48},{56,64},{72,80},{88,96},{104,112},{120,128}... | collective-permute-start | bytes 663560 | tf_op jit(solution)/shard_map/ppermute | solution.py:711
  48.1 0.1 fusion.5
  48.3 8.9 %collective-permute-done.6.strip_outer_hbm = f32[27,16,128]{2,1,0:T(8,128)} collective-permute-done((f32[27,16,128]{2,1,0:T(8,128)S(1)}, f32[27,16,128]{2,1,0:T(8,128)}, u32[]{:S(2)}, u32[]{:S(2)}) %collective-permute-start.6) | collective-permute-done | bytes 221216 | tf_op jit(solution)/shard_map/ppermute | solution.py:711
  57.1 0.1 broadcast_in_dim.33.weight_ref.refs_7_.refs_8_
  57.2 0.0 copy-start.2
  57.2 0.9 %copy-done.2 = f32[27,16,128]{2,1,0:T(8,128)S(1)} copy-done((f32[27,16,128]{2,1,0:T(8,128)S(1)}, f32[27,16,128]{2,1,0:T(8,128)}, u32[]{:S(2)}) %copy-start.2) | copy-done | bytes 221208
  58.1 7.1 %strips.1 = (f32[24,16,256]{2,1,0:T(8,128)S(1)}, f32[24,16,256]{2,1,0:T(8,128)S(1)}, f32[8,2,16,384]{3,2,1,0:T(8,128)S(1)}) custom-call(f32[27,16,128]{2,1,0:T(8,128)S(1)} %copy-done.2, f32[27,16,128]{2,1,0:T(8,128)S(1)} %pad_maximum_fusion.strip_hbm, f32[27,16,128]{2,1,0:T(8,128)} %collective-permute-done.6.strip_outer_hbm, ...), custom_call_target="tpu_custom_call" | custom-call | flops 43008000 | bytes 8388608 | tf_op jit(solution)/shard_map/strips/pallas_call | solution.py:764
  65.3 0.0 collective-permute-done.1.refs_0_
  65.3 0.0 collective-permute-done.2.refs_1_
  65.3 14.1 %near.1 = (f32[12,16,16,256]{3,2,1,0:T(8,128)S(1)}, f32[8,2,2,16,256]{4,3,2,1,0:T(8,128)S(1)}) custom-call(f32[12,4,16,256]{3,2,1,0:T(8,128)} %collective-permute-done.1.refs_0_, f32[12,4,16,256]{3,2,1,0:T(8,128)} %collective-permute-done.2.refs_1_, f32[12,4,16,256]{3,2,1,0:T(8,128)} %get-tuple-element.16.refs_2_, ...), custom_call_target="tpu_custom_call" | custom-call | flops 100352000 | bytes 8388608 | tf_op jit(solution)/shard_map/near/pallas_call | solution.py:795
  79.4 0.0 collective-permute-done.refs_0_
  79.4 0.0 collective-permute-done.8.refs_3_
  79.4 12.3 %shard_map.46 = f32[12,8,16,256]{3,2,1,0:T(8,128)} custom-call(f32[12,4,16,256]{3,2,1,0:T(8,128)S(1)} %collective-permute-done.refs_0_, f32[12,16,16,256]{3,2,1,0:T(8,128)S(1)} %get-tuple-element.22.refs_1_, f32[12,4,16,256]{3,2,1,0:T(8,128)S(1)} %collective-permute-done.7.refs_2_, f32[12,4,16,256]{3,2,1,0:T(8,128)S(1)} %collective-permute-done.8.refs_3_, ...), custom_call_target="tpu_custom_call" | custom-call | flops 103219200 | bytes 8388608 | tf_op jit(solution)/shard_map/pallas_call | solution.py:810
  (10 shorter events, 0.1 us)
Async XLA Ops:
  0.0 19.5 %copy-start.4 = (f32[2,8]{1,0:T(2,128)S(1)}, f32[2,8]{1,0:T(2,128)}, u32[]{:S(2)}) copy-start(f32[2,8]{1,0:T(2,128)} %param.7) | copy-start | bytes 196
  0.0 19.6 %copy-start.5 = (s32[16]{0:T(128)S(1)}, s32[16]{0:T(128)}, u32[]{:S(2)}) copy-start(s32[16]{0:T(128)} %param.6) | copy-start | bytes 196
  0.0 1.4 %copy-start = (f32[12,8,16,256]{3,2,1,0:T(8,128)S(1)}, f32[12,8,16,256]{3,2,1,0:T(8,128)}, u32[]{:S(2)}) copy-start(f32[12,8,16,256]{3,2,1,0:T(8,128)} %state_ref.1) | copy-start | bytes 4718596
  1.4 0.7 copy-start.3
  4.9 14.9 %collective-permute-start.3 = (f32[14,16,128]{2,1,0:T(8,128)S(1)}, f32[14,16,128]{2,1,0:T(8,128)S(1)}, u32[]{:S(2)}, u32[]{:S(2)}) collective-permute-start(f32[14,16,128]{2,1,0:T(8,128)S(1)} %get-tuple-element.18), channel_id=1, source_target_pairs={{0,1},{2,3},{4,5},{6,7},{1,0},{3,2},{5,4},{7,6},{8,9},{10,11},{12,... | collective-permute-start | bytes 344072 | tf_op jit(solution)/shard_map/ppermute | solution.py:712
  5.1 37.9 %collective-permute-start.4 = (f32[14,16,128]{2,1,0:T(8,128)S(1)}, f32[14,16,128]{2,1,0:T(8,128)}, u32[]{:S(2)}, u32[]{:S(2)}) collective-permute-start(f32[14,16,128]{2,1,0:T(8,128)S(1)} %get-tuple-element.18), channel_id=1, source_target_pairs={{1,2},{3,4},{5,6},{2,1},{4,3},{6,5},{9,10},{11,12},{13,14},{10,9},... | collective-permute-start | bytes 344072 | tf_op jit(solution)/shard_map/ppermute | solution.py:711
  9.5 55.7 %collective-permute-start.1 = (f32[12,4,16,256]{3,2,1,0:T(8,128)}, f32[12,4,16,256]{3,2,1,0:T(8,128)}, u32[]{:S(2)}, u32[]{:S(2)}) collective-permute-start(f32[12,4,16,256]{3,2,1,0:T(8,128)} %get-tuple-element.16.refs_2_), channel_id=1, source_target_pairs={{0,8},{16,24},{32,40},{48,56},{64,72},{80,88},{96,104},{112,120},{... | collective-permute-start | bytes 2359304 | tf_op jit(solution)/shard_map/ppermute | solution.py:712
  9.6 55.7 %collective-permute-start.2 = (f32[12,4,16,256]{3,2,1,0:T(8,128)}, f32[12,4,16,256]{3,2,1,0:T(8,128)}, u32[]{:S(2)}, u32[]{:S(2)}) collective-permute-start(f32[12,4,16,256]{3,2,1,0:T(8,128)} %get-tuple-element.17), channel_id=1, source_target_pairs={{8,16},{24,32},{40,48},{56,64},{72,80},{88,96},{104,112},{120,128}... | collective-permute-start | bytes 2359304 | tf_op jit(solution)/shard_map/ppermute | solution.py:711
  13.8 23.7 %collective-permute-start.7 = (f32[12,4,16,256]{3,2,1,0:T(8,128)S(1)}, f32[12,4,16,256]{3,2,1,0:T(8,128)S(1)}, u32[]{:S(2)}, u32[]{:S(2)}) collective-permute-start(f32[12,4,16,256]{3,2,1,0:T(8,128)S(1)} %get-tuple-element.23), channel_id=1, source_target_pairs={{8,16},{24,32},{40,48},{72,80},{88,96},{104,112},{136,144},{152,16... | collective-permute-start | bytes 2359304 | tf_op jit(solution)/shard_map/ppermute | solution.py:758
  19.8 59.7 %collective-permute-start = (f32[12,4,16,256]{3,2,1,0:T(8,128)S(1)}, f32[12,4,16,256]{3,2,1,0:T(8,128)S(1)}, u32[]{:S(2)}, u32[]{:S(2)}) collective-permute-start(f32[12,4,16,256]{3,2,1,0:T(8,128)S(1)} %get-tuple-element.15.refs_3_), channel_id=1, source_target_pairs={{0,8},{16,24},{32,40},{48,56},{64,72},{80,88},{96,104},{112,120},{... | collective-permute-start | bytes 2359304 | tf_op jit(solution)/shard_map/ppermute | solution.py:759
  37.4 42.0 %collective-permute-start.8 = (f32[12,4,16,256]{3,2,1,0:T(8,128)S(1)}, f32[12,4,16,256]{3,2,1,0:T(8,128)S(1)}, u32[]{:S(2)}, u32[]{:S(2)}) collective-permute-start(f32[12,4,16,256]{3,2,1,0:T(8,128)S(1)} %collective-permute-done.7.refs_2_), channel_id=1, source_target_pairs={{0,64},{64,128},{128,192},{120,56},{184,120},{248,184},{1,65},{65,... | collective-permute-start | bytes 2359304 | tf_op jit(solution)/shard_map/ppermute | solution.py:760
  44.0 1.6 %collective-permute-start.5 = (f32[27,16,128]{2,1,0:T(8,128)S(1)}, f32[27,16,128]{2,1,0:T(8,128)S(1)}, u32[]{:S(2)}, u32[]{:S(2)}) collective-permute-start(f32[27,16,128]{2,1,0:T(8,128)S(1)} %pad_maximum_fusion.strip_hbm), channel_id=1, source_target_pairs={{0,8},{16,24},{32,40},{48,56},{64,72},{80,88},{96,104},{112,120},{... | collective-permute-start | bytes 663560 | tf_op jit(solution)/shard_map/ppermute | solution.py:712
  45.5 0.7 copy-start.1
  46.2 10.9 %collective-permute-start.6 = (f32[27,16,128]{2,1,0:T(8,128)S(1)}, f32[27,16,128]{2,1,0:T(8,128)}, u32[]{:S(2)}, u32[]{:S(2)}) collective-permute-start(f32[27,16,128]{2,1,0:T(8,128)S(1)} %pad_maximum_fusion.strip_hbm), channel_id=1, source_target_pairs={{8,16},{24,32},{40,48},{56,64},{72,80},{88,96},{104,112},{120,128}... | collective-permute-start | bytes 663560 | tf_op jit(solution)/shard_map/ppermute | solution.py:711
  57.2 0.9 %copy-start.2 = (f32[27,16,128]{2,1,0:T(8,128)S(1)}, f32[27,16,128]{2,1,0:T(8,128)}, u32[]{:S(2)}) copy-start(f32[27,16,128]{2,1,0:T(8,128)} %copy-done.1) | copy-start | bytes 663556
